TPU v7x, 32 devices: a whole 2x2x4 slice. The times are simulated.
32 devices in a mesh: gx: 2 (over x), gy: 4 (over y, core), gz: 4 (over z).
Axes of the slice: x: 2, y: 2, z: 4, core: 2. Of those that a mesh axis runs over, the one named last changes fastest.
Arguments:
- point_xyz: float32 [1536, 3, 128], P(('gx', 'gy', 'gz')), may hold values from 0 to 64, as said below
- point_weight: float32 [1536, 128], P(('gx', 'gy', 'gz')), may hold values from 0.25 to 2
- block_cell: int32 [1536], P(('gx', 'gy', 'gz')), may hold values from 0 to 2047, as said below
- block_count: int32 [1536], P(('gx', 'gy', 'gz')), may hold values from 1 to 128, as said below
- gauss_mean: float32 [2, 16, 64, 3, 32], P('gx', 'gy', 'gz'), may hold values from 0 to 64, as said below
- gauss_opacity: float32 [2, 16, 64, 32], P('gx', 'gy', 'gz'), may hold values from 0.05 to 1
- gauss_count: int32 [2, 16, 64], P('gx', 'gy', 'gz'), may hold values from 8 to 32, as said below
Outputs:
- point_out: float32 [1536, 4, 128], P(('gx', 'gy', 'gz'))
- gauss_grad: float32 [2, 16, 64, 4, 32], P('gx', 'gy', 'gz')
Inputs may be any that keep to these rules, and one draw needn't show every extreme that they name: `block_cell`: no two blocks name the same cell. Of the blocks that one device holds, at most 2 lie in the cells of any one brick (a brick is the 1 x 4 x 16 cells of one device of the grid). `block_count`: the valid points of a block are its first ones. `gauss_count`: the used slots of a cell are its first ones. `point_xyz`: every point lies in the cell of its block: each coordinate minus the cell's index lies in [0, 1]. `gauss_mean`: every centre, used or not, lies in its own cell: each coordinate minus the cell's index lies in [0, 1].
All inputs are finite; a program needn't handle non-finite values.
Results may differ from a plain program's by a relative error of at most 0.0003.
Values sent between devices are 32-bit elements; how exact they have to be, the bound alone decides.
No kernel may reach another device: no remote copies, remote signals or barrier semaphores. Data moves between devices by JAX's collectives and lax.ppermute only.
A program may use at most 64 MiB of HBM per device.

v0:
```python
import math

import jax
import jax.numpy as jnp
from jax import lax
from jax.sharding import PartitionSpec as P

MOST = 2


kernel_width = 0.05
cutoff_sq = 0.5
floor_term = math.exp(-10.0)


def with_halo(cells, sides, width):
    for axis, dim in sides:
        count = lax.axis_size(axis)
        ends = count - 1
        head = lax.slice_in_dim(cells, 0, width, axis=dim)
        tail = lax.slice_in_dim(cells, cells.shape[dim] - width, cells.shape[dim], axis=dim)
        cells = jnp.concatenate(
            [
                lax.ppermute(tail, axis, [(i, (i + 1) % count) for i in range(ends)]),
                cells,
                lax.ppermute(head, axis, [((i + 1) % count, i) for i in range(ends)]),
            ],
            axis=dim,
        )
    return cells


def window(values, step_x, step_y, step_z, extent):
    anchor = jnp.zeros((), jnp.int32)
    corner = (step_x, step_y, step_z) + (anchor,) * (values.ndim - 3)
    return lax.dynamic_slice(values, corner, tuple(extent) + values.shape[3:])


def put_window(values, update, step_x, step_y, step_z):
    anchor = jnp.zeros((), jnp.int32)
    corner = (step_x, step_y, step_z) + (anchor,) * (values.ndim - 3)
    return lax.dynamic_update_slice(values, update, corner)


def pair_block(own_items, own_inv, far_items, far_inv, second):
    delta_x = own_items[..., 0, :, None] - far_items[..., 0, None, :]
    delta_y = own_items[..., 1, :, None] - far_items[..., 1, None, :]
    delta_z = own_items[..., 2, :, None] - far_items[..., 2, None, :]
    distance = delta_x * delta_x + delta_y * delta_y + delta_z * delta_z
    falloff = jnp.exp(-distance / cutoff_sq)
    kernel = jnp.exp((falloff - 1.0) * (cutoff_sq / kernel_width))
    own_wt = own_items[..., 3, :, None]
    far_wt = far_items[..., 3, None, :]
    if not second:
        own_sum = jnp.sum(kernel * far_wt, axis=-1)
        far_sum = jnp.sum(kernel * own_wt, axis=-2)
        return (own_sum, far_sum)
    coupling = (
        2.0 * own_wt * far_wt * kernel * falloff * (own_inv[..., :, None] + far_inv[..., None, :])
    )
    own_grad = jnp.stack(
        [
            jnp.sum(coupling * delta_x, axis=-1),
            jnp.sum(coupling * delta_y, axis=-1),
            jnp.sum(coupling * delta_z, axis=-1),
        ],
        axis=-2,
    )
    far_out = None
    far_grad = -jnp.stack(
        [
            jnp.sum(coupling * delta_x, axis=-2),
            jnp.sum(coupling * delta_y, axis=-2),
            jnp.sum(coupling * delta_z, axis=-2),
        ],
        axis=-2,
    )
    far_density = jnp.sum(kernel * own_wt * own_inv[..., :, None], axis=-2)
    far_out = jnp.concatenate([far_grad, far_density[..., None, :]], axis=-2)
    return (own_grad, far_out)


def sweep_pairs(own_items, own_inv, far_grid, far_inv, second):
    extent = own_items.shape[:3]
    own_len = own_items.shape[-1]
    far_len = far_grid.shape[-1]
    if second:
        own_acc = jnp.zeros(extent + (3, own_len), jnp.float32)
        far_acc = jnp.zeros(far_grid.shape[:3] + (4, far_len), jnp.float32)
    else:
        own_acc = jnp.zeros(extent + (own_len,), jnp.float32)
        far_acc = jnp.zeros(far_grid.shape[:3] + (far_len,), jnp.float32)

    def one_offset(offset, state_pair):
        own_total, far_total = state_pair
        step_x = (offset // 9).astype(jnp.int32)
        step_y = (offset // 3 % 3).astype(jnp.int32)
        step_z = (offset % 3).astype(jnp.int32)
        far_items = window(far_grid, step_x, step_y, step_z, extent)
        far_part_inv = window(far_inv, step_x, step_y, step_z, extent) if second else None
        own_part, far_part = pair_block(own_items, own_inv, far_items, far_part_inv, second)
        own_total = own_total + own_part
        region = window(far_total, step_x, step_y, step_z, extent) + far_part
        far_total = put_window(far_total, region, step_x, step_y, step_z)
        return (own_total, far_total)

    return lax.fori_loop(0, 27, one_offset, (own_acc, far_acc))


def fold_rim(values):
    for dim_index in range(3):
        inner_len = values.shape[dim_index] - 4
        middle = lax.slice_in_dim(values, 2, inner_len + 2, axis=dim_index)
        lower_rim = lax.slice_in_dim(values, 0, 1, axis=dim_index)
        upper_rim = lax.slice_in_dim(values, inner_len + 3, inner_len + 4, axis=dim_index)
        widths_low = [(0, 0)] * values.ndim
        widths_low[dim_index] = (0, inner_len - 1)
        widths_high = [(0, 0)] * values.ndim
        widths_high[dim_index] = (inner_len - 1, 0)
        values = middle + jnp.pad(lower_rim, widths_low) + jnp.pad(upper_rim, widths_high)
    return values


def on_device(
    point_xyz, point_weight, block_cell, block_count, gauss_mean, gauss_opacity, gauss_count
):
    points_len = point_xyz.shape[2]
    span_x, span_y, span_z, unused_dim, gauss_slots = gauss_mean.shape
    size_x = lax.axis_size("gx")
    size_y = lax.axis_size("gy")
    size_z = lax.axis_size("gz")
    bricks = size_x * size_y * size_z
    cell_total = span_x * span_y * span_z
    depth_y = span_y * size_y
    depth_z = span_z * size_z
    along_x = block_cell // (depth_y * depth_z)
    along_y = block_cell // depth_z % depth_y
    along_z = block_cell % depth_z
    target = (along_x // span_x * size_y + along_y // span_y) * size_z + along_z // span_z
    local_cell = (along_x % span_x * span_y + along_y % span_y) * span_z + along_z % span_z
    chosen = (target[:, None] == jnp.arange(bricks, dtype=jnp.int32)[None, :]).astype(jnp.int32)
    before = jnp.sum((jnp.cumsum(chosen, axis=0) - chosen) * chosen, axis=1)
    send_slot = target * MOST + before
    is_valid = jnp.arange(points_len, dtype=jnp.int32)[None, :] < block_count[:, None]
    weights = jnp.where(is_valid, point_weight, 0.0)
    payload = jnp.concatenate([point_xyz, weights[:, None, :]], axis=1)
    outgoing = jnp.zeros((bricks * MOST, 4, points_len), jnp.float32).at[send_slot].set(payload)
    labels = jnp.full((bricks * MOST,), -1, jnp.int32).at[send_slot].set(local_cell)
    incoming, arrived = (
        lax.all_to_all(outgoing, ("gx", "gy", "gz"), split_axis=0, concat_axis=0, tiled=True),
        lax.all_to_all(labels, ("gx", "gy", "gz"), split_axis=0, concat_axis=0, tiled=True),
    )
    placed = jnp.where(arrived >= 0, arrived, cell_total)
    points = (
        jnp.zeros((cell_total, 4, points_len), jnp.float32).at[placed].set(incoming, mode="drop")
    )
    points = points.reshape(span_x, span_y, span_z, 4, points_len)
    present = jnp.arange(gauss_slots, dtype=jnp.int32) < gauss_count[..., None]
    gaussians = jnp.concatenate(
        [gauss_mean, jnp.where(present, gauss_opacity, 0.0)[..., None, :]], axis=3
    )
    far_gauss = with_halo(gaussians, (("gx", 0), ("gy", 1), ("gz", 2)), 1)
    density_p, density_far = sweep_pairs(points, None, far_gauss, None, False)
    density_g = fold_rim(with_halo(density_far, (("gx", 0), ("gy", 1), ("gz", 2)), 1))
    total_p = floor_term + density_p
    total_g = floor_term + density_g
    inverse_p = 1.0 / total_p
    inverse_g = 1.0 / total_g
    far_inverse = with_halo(inverse_g, (("gx", 0), ("gy", 1), ("gz", 2)), 1)
    gradient_p, gradient_far = sweep_pairs(points, inverse_p, far_gauss, far_inverse, True)
    gradient_g = fold_rim(with_halo(gradient_far, (("gx", 0), ("gy", 1), ("gz", 2)), 1))
    loss_p = jnp.where(points[..., 3, :] > 0.0, -kernel_width * jnp.log(total_p), 0.0)
    cell_result = jnp.concatenate([loss_p[..., None, :], gradient_p], axis=3).reshape(
        cell_total, 4, points_len
    )
    reply_rows = jnp.where(
        (arrived >= 0)[:, None, None], cell_result[jnp.clip(arrived, 0, cell_total - 1)], 0.0
    )
    answer = lax.all_to_all(reply_rows, ("gx", "gy", "gz"), split_axis=0, concat_axis=0, tiled=True)
    point_out = answer[send_slot]
    grad_opacity = jnp.where(
        present, -kernel_width * jnp.log(total_g) - kernel_width * gradient_g[..., 3, :], 0.0
    )
    gauss_grad = jnp.concatenate([gradient_g[..., :3, :], grad_opacity[..., None, :]], axis=3)
    return (point_out, gauss_grad)


def solution(mesh):
    return jax.shard_map(
        on_device,
        mesh=mesh,
        in_specs=(
            P(("gx", "gy", "gz"), None, None),
            P(("gx", "gy", "gz"), None),
            P(("gx", "gy", "gz")),
            P(("gx", "gy", "gz")),
            P("gx", "gy", "gz", None, None),
            P("gx", "gy", "gz", None),
            P("gx", "gy", "gz"),
        ),
        out_specs=(P(("gx", "gy", "gz"), None, None), P("gx", "gy", "gz", None, None)),
        check_vma=False,
    )
```

profile of v0, /device:TPU:0, one launch (start us, length us, event | category | flops | bytes accessed | tf_op | source)
XLA Modules:
  0.0 299.9 jit_solution(4181908584539742054)
XLA Ops:
  3.7 4.9 %collective-permute-start = (f32[1,4,16,4,32]{4,2,1,3,0:T(8,128)S(1)}, f32[1,4,16,4,32]{4,2,1,3,0:T(8,128)S(1)}, u32[]{:S(2)}, u32[]{:S(2)}) collective-permute-start(f32[1,4,16,4,32]{4,2,1,3,0:T(8,128)S(1)} %pad_maximum_fusion.6), channel_id=1, source_target_pairs={{0,16},{1,17},{2,18},{3,19},{4,20},{5,21},{6,22},{7,23},{8,24},{9,... | collective-permute-start | bytes 98312 | tf_op jit(solution)/shard_map/ppermute | solution.py:24
  11.8 6.1 %all-to-all-start = ((s32[32,2,1]{1,2,0:T(1,128)}), s32[32,2,1]{1,2,0:T(1,128)S(1)}, u32[]{:S(2)}, u32[]{:S(2)}) async-start(s32[32,2,1]{1,2,0:T(1,128)} %bitcast), calls=%async_computation | async-start | bytes 32768 | tf_op jit(solution)/shard_map/all_to_all | solution.py:151
  24.5 5.3 %scatter_fusion = f32[64,4,128]{2,1,0:T(4,128)} fusion(f32[64,4,128]{2,1,0:T(4,128)} %broadcast.1082.clone, s32[48]{0:T(128)S(1)} %compare_select_fusion.3, f32[48,4,128]{2,1,0:T(4,128)S(1)} %copy.44), kind=kCustom, calls=%fused_computation.3 | custom fusion | bytes 295104 | tf_op jit(solution)/shard_map/scatter | solution.py:147
  29.9 7.9 %all-to-all-start.1 = ((f32[64,4,128]{2,1,0:T(4,128)}), f32[64,4,128]{2,1,0:T(4,128)S(1)}, u32[]{:S(2)}, u32[]{:S(2)}) async-start(f32[64,4,128]{2,1,0:T(4,128)} %scatter_fusion), calls=%async_computation.1 | async-start | bytes 262144 | tf_op jit(solution)/shard_map/all_to_all | solution.py:150
  39.2 3.7 %collective-permute-start.4 = (f32[3,6,1,4,32]{4,2,1,3,0:T(1,128)S(1)}, f32[3,6,1,4,32]{4,2,1,3,0:T(1,128)S(1)}, u32[]{:S(2)}, u32[]{:S(2)}) collective-permute-start(f32[3,6,1,4,32]{4,2,1,3,0:T(1,128)S(1)} %get-tuple-element.506), channel_id=1, source_target_pairs={{0,1},{1,2},{2,3},{4,5},{5,6},{6,7},{8,9},{9,10},{10,11},{12,13},{... | collective-permute-start | bytes 27656 | tf_op jit(solution)/shard_map/ppermute | solution.py:24
  44.5 4.2 %collective-permute-done.5 = f32[3,6,1,4,32]{4,2,1,3,0:T(1,128)S(1)} collective-permute-done((f32[3,6,1,4,32]{4,2,1,3,0:T(1,128)S(1)}, f32[3,6,1,4,32]{4,2,1,3,0:T(1,128)S(1)}, u32[]{:S(2)}, u32[]{:S(2)}) %collective-permute-start.5) | collective-permute-done | bytes 9248 | tf_op jit(solution)/shard_map/ppermute | solution.py:26
  51.5 60.9 %while.38 = (s32[]{:T(128)}, f32[1,4,16,128]{3,2,1,0:T(8,128)S(1)}, f32[3,6,18,32]{3,2,1,0:T(8,128)S(1)}, f32[1,4,16,4,128]{4,2,1,3,0:T(8,128)S(1)}, f32[3,6,18,...) while((s32[]{:T(128)}, f32[1,4,16,128]{3,2,1,0:T(8,128)S(1)}, ...), condition=%wide.region_8.9_spmd.clone, body=%wide.region_5.8_spmd.clone.sunk | while | flops 4202535 | bytes 672315 | solution.py:107
  112.5 3.4 %collective-permute-start.6 = (f32[1,6,18,32]{3,2,1,0:T(8,128)S(1)}, f32[1,6,18,32]{3,2,1,0:T(8,128)S(1)}, u32[]{:S(2)}, u32[]{:S(2)}) collective-permute-start(f32[1,6,18,32]{3,2,1,0:T(8,128)S(1)} %get-tuple-element.515), channel_id=1, source_target_pairs={{0,16},{1,17},{2,18},{3,19},{4,20},{5,21},{6,22},{7,23},{8,24},{9,... | collective-permute-start | bytes 41480 | tf_op jit(solution)/shard_map/ppermute | solution.py:24
  117.9 4.3 %collective-permute-done.7 = f32[1,6,18,32]{3,2,1,0:T(8,128)S(1)} collective-permute-done((f32[1,6,18,32]{3,2,1,0:T(8,128)S(1)}, f32[1,6,18,32]{3,2,1,0:T(8,128)S(1)}, u32[]{:S(2)}, u32[]{:S(2)}) %collective-permute-start.7) | collective-permute-done | bytes 13856 | tf_op jit(solution)/shard_map/ppermute | solution.py:26
  124.8 3.5 %collective-permute-done.9 = f32[5,1,18,32]{3,2,1,0:T(8,128)S(1)} collective-permute-done((f32[5,1,18,32]{3,2,1,0:T(8,128)S(1)}, f32[5,1,18,32]{3,2,1,0:T(8,128)S(1)}, u32[]{:S(2)}, u32[]{:S(2)}) %collective-permute-start.9) | collective-permute-done | bytes 11552 | tf_op jit(solution)/shard_map/ppermute | solution.py:26
  128.4 3.4 %collective-permute-start.10 = (f32[5,8,1,32]{3,2,1,0:T(1,128)S(1)}, f32[5,8,1,32]{3,2,1,0:T(1,128)S(1)}, u32[]{:S(2)}, u32[]{:S(2)}) collective-permute-start(f32[5,8,1,32]{3,2,1,0:T(1,128)S(1)} %get-tuple-element.508), channel_id=1, source_target_pairs={{0,1},{1,2},{2,3},{4,5},{5,6},{6,7},{8,9},{9,10},{10,11},{12,13},{... | collective-permute-start | bytes 15368 | tf_op jit(solution)/shard_map/ppermute | solution.py:24
  133.2 4.2 %collective-permute-done.11 = f32[5,8,1,32]{3,2,1,0:T(1,128)S(1)} collective-permute-done((f32[5,8,1,32]{3,2,1,0:T(1,128)S(1)}, f32[5,8,1,32]{3,2,1,0:T(1,128)S(1)}, u32[]{:S(2)}, u32[]{:S(2)}) %collective-permute-start.11) | collective-permute-done | bytes 5152 | tf_op jit(solution)/shard_map/ppermute | solution.py:26
  139.0 4.5 %collective-permute-start.12 = (f32[1,4,16,32]{3,2,1,0:T(8,128)S(1)}, f32[1,4,16,32]{3,2,1,0:T(8,128)S(1)}, u32[]{:S(2)}, u32[]{:S(2)}) collective-permute-start(f32[1,4,16,32]{3,2,1,0:T(8,128)S(1)} %broadcast_divide_fusion), channel_id=1, source_target_pairs={{0,16},{1,17},{2,18},{3,19},{4,20},{5,21},{6,22},{7,23},{8,24},{9,... | collective-permute-start | bytes 24584 | tf_op jit(solution)/shard_map/ppermute | solution.py:24
  148.8 3.8 %collective-permute-done.15 = f32[3,1,16,32]{3,2,1,0:T(8,128)S(1)} collective-permute-done((f32[3,1,16,32]{3,2,1,0:T(8,128)S(1)}, f32[3,1,16,32]{3,2,1,0:T(8,128)S(1)}, u32[]{:S(2)}, u32[]{:S(2)}) %collective-permute-start.15) | collective-permute-done | bytes 6176 | tf_op jit(solution)/shard_map/ppermute | solution.py:26
  152.6 3.4 %collective-permute-start.16 = (f32[3,6,1,32]{3,2,1,0:T(1,128)S(1)}, f32[3,6,1,32]{3,2,1,0:T(1,128)S(1)}, u32[]{:S(2)}, u32[]{:S(2)}) collective-permute-start(f32[3,6,1,32]{3,2,1,0:T(1,128)S(1)} %get-tuple-element.516), channel_id=1, source_target_pairs={{0,1},{1,2},{2,3},{4,5},{5,6},{6,7},{8,9},{9,10},{10,11},{12,13},{... | collective-permute-start | bytes 6920 | tf_op jit(solution)/shard_map/ppermute | solution.py:24
  157.4 4.2 %collective-permute-done.17 = f32[3,6,1,32]{3,2,1,0:T(1,128)S(1)} collective-permute-done((f32[3,6,1,32]{3,2,1,0:T(1,128)S(1)}, f32[3,6,1,32]{3,2,1,0:T(1,128)S(1)}, u32[]{:S(2)}, u32[]{:S(2)}) %collective-permute-start.17) | collective-permute-done | bytes 2336 | tf_op jit(solution)/shard_map/ppermute | solution.py:26
  161.7 96.5 %while.39 = (s32[]{:T(128)}, f32[1,4,16,3,128]{4,2,1,3,0:T(8,128)S(1)}, f32[3,6,18,4,32]{4,2,1,3,0:T(8,128)S(1)}, f32[1,4,16,4,128]{4,2,1,3,0:T(8,128)S(1)}, f32...) while((s32[]{:T(128)}, ...), condition=%wide.region_17.18_spmd.clone, body=%wide.region_9.17_spmd.clone.sunk | while | flops 7710759 | bytes 1286743 | solution.py:107
  161.9 3.0 %fusion.43 = (f32[4,16,32]{2,1,0:T(8,128)S(1)}, f32[4,16,128]{2,1,0:T(8,128)S(1)}, f32[4,16,32]{2,1,0:T(8,128)S(1)}, f32[4,16,32]{2,1,0:T(8,128)S(1)}, f32[4,16,...) fusion(f32[4,16,32]{2,1,0:T(8,128)S(1)} %get-tuple-element.633, ...), kind=kLoop, calls=%fused_computation.32.clone.1 | loop fusion | flops 7569408 | bytes 368640 | tf_op jit(solution)/shard_map/while/body/eval_jaxpr/reduce_sum | solution.py:72
  165.4 3.0 %fusion.43 = (f32[4,16,32]{2,1,0:T(8,128)S(1)}, f32[4,16,128]{2,1,0:T(8,128)S(1)}, f32[4,16,32]{2,1,0:T(8,128)S(1)}, f32[4,16,32]{2,1,0:T(8,128)S(1)}, f32[4,16,...) fusion(f32[4,16,32]{2,1,0:T(8,128)S(1)} %get-tuple-element.633, ...), kind=kLoop, calls=%fused_computation.32.clone.1 | loop fusion | flops 7569408 | bytes 368640 | tf_op jit(solution)/shard_map/while/body/eval_jaxpr/reduce_sum | solution.py:72
  258.2 4.2 %collective-permute-start.18 = (f32[1,6,18,4,32]{4,2,1,3,0:T(8,128)S(1)}, f32[1,6,18,4,32]{4,2,1,3,0:T(8,128)S(1)}, u32[]{:S(2)}, u32[]{:S(2)}) collective-permute-start(f32[1,6,18,4,32]{4,2,1,3,0:T(8,128)S(1)} %get-tuple-element.505), channel_id=1, source_target_pairs={{0,16},{1,17},{2,18},{3,19},{4,20},{5,21},{6,22},{7,23},{8,24},{9,... | collective-permute-start | bytes 165896 | tf_op jit(solution)/shard_map/ppermute | solution.py:24
  264.0 5.7 %collective-permute-done.18 = f32[1,6,18,4,32]{4,2,1,3,0:T(8,128)S(1)} collective-permute-done((f32[1,6,18,4,32]{4,2,1,3,0:T(8,128)S(1)}, f32[1,6,18,4,32]{4,2,1,3,0:T(8,128)S(1)}, u32[]{:S(2)}, u32[]{:S(2)}) %collective-permute-start.18) | collective-permute-done | bytes 55328 | tf_op jit(solution)/shard_map/ppermute | solution.py:24
  269.8 4.6 %collective-permute-done.19 = f32[1,6,18,4,32]{4,2,1,3,0:T(8,128)S(1)} collective-permute-done((f32[1,6,18,4,32]{4,2,1,3,0:T(8,128)S(1)}, f32[1,6,18,4,32]{4,2,1,3,0:T(8,128)S(1)}, u32[]{:S(2)}, u32[]{:S(2)}) %collective-permute-start.19) | collective-permute-done | bytes 55328 | tf_op jit(solution)/shard_map/ppermute | solution.py:26
  284.0 6.3 %all-to-all-start.2 = ((f32[64,4,128]{2,1,0:T(4,128)}), f32[64,4,128]{2,1,0:T(4,128)S(1)}, u32[]{:S(2)}, u32[]{:S(2)}) async-start(f32[64,4,128]{2,1,0:T(4,128)} %broadcast_select_fusion), calls=%async_computation.2 | async-start | bytes 262144 | tf_op jit(solution)/shard_map/all_to_all | solution.py:179
  291.8 6.8 %all-to-all-done.2 = f32[64,4,128]{2,1,0:T(4,128)S(1)} async-done(((f32[64,4,128]{2,1,0:T(4,128)}), f32[64,4,128]{2,1,0:T(4,128)S(1)}, u32[]{:S(2)}, u32[]{:S(2)}) %all-to-all-start.2) | async-done | bytes 131104 | tf_op jit(solution)/shard_map/all_to_all | solution.py:179
  (513 shorter events, 189.9 us)
Async XLA Ops:
  2.4 16.2 %collective-permute-start.1 = (f32[1,4,16,4,32]{4,2,1,3,0:T(8,128)S(1)}, f32[1,4,16,4,32]{4,2,1,3,0:T(8,128)S(1)}, u32[]{:S(2)}, u32[]{:S(2)}) collective-permute-start(f32[1,4,16,4,32]{4,2,1,3,0:T(8,128)S(1)} %pad_maximum_fusion.6), channel_id=1, source_target_pairs={{16,0},{17,1},{18,2},{19,3},{20,4},{21,5},{22,6},{23,7},{24,8},{25... | collective-permute-start | bytes 98312 | tf_op jit(solution)/shard_map/ppermute | solution.py:26
  3.7 14.9 %collective-permute-start = (f32[1,4,16,4,32]{4,2,1,3,0:T(8,128)S(1)}, f32[1,4,16,4,32]{4,2,1,3,0:T(8,128)S(1)}, u32[]{:S(2)}, u32[]{:S(2)}) collective-permute-start(f32[1,4,16,4,32]{4,2,1,3,0:T(8,128)S(1)} %pad_maximum_fusion.6), channel_id=1, source_target_pairs={{0,16},{1,17},{2,18},{3,19},{4,20},{5,21},{6,22},{7,23},{8,24},{9,... | collective-permute-start | bytes 98312 | tf_op jit(solution)/shard_map/ppermute | solution.py:24
  11.8 18.1 %all-to-all-start = ((s32[32,2,1]{1,2,0:T(1,128)}), s32[32,2,1]{1,2,0:T(1,128)S(1)}, u32[]{:S(2)}, u32[]{:S(2)}) async-start(s32[32,2,1]{1,2,0:T(1,128)} %bitcast), calls=%async_computation | async-start | bytes 32768 | tf_op jit(solution)/shard_map/all_to_all | solution.py:151
  19.5 19.7 %collective-permute-start.2 = (f32[3,1,16,4,32]{4,2,1,3,0:T(8,128)S(1)}, f32[3,1,16,4,32]{4,2,1,3,0:T(8,128)S(1)}, u32[]{:S(2)}, u32[]{:S(2)}) collective-permute-start(f32[3,1,16,4,32]{4,2,1,3,0:T(8,128)S(1)} %get-tuple-element.510), channel_id=1, source_target_pairs={{0,4},{4,8},{8,12},{1,5},{5,9},{9,13},{2,6},{6,10},{10,14},{3,7},{... | collective-permute-start | bytes 73736 | tf_op jit(solution)/shard_map/ppermute | solution.py:24
  21.6 17.5 %collective-permute-start.3 = (f32[3,1,16,4,32]{4,2,1,3,0:T(8,128)S(1)}, f32[3,1,16,4,32]{4,2,1,3,0:T(8,128)S(1)}, u32[]{:S(2)}, u32[]{:S(2)}) collective-permute-start(f32[3,1,16,4,32]{4,2,1,3,0:T(8,128)S(1)} %get-tuple-element.511), channel_id=1, source_target_pairs={{4,0},{8,4},{12,8},{5,1},{9,5},{13,9},{6,2},{10,6},{14,10},{7,3},{... | collective-permute-start | bytes 73736 | tf_op jit(solution)/shard_map/ppermute | solution.py:26
  29.9 19.1 %all-to-all-start.1 = ((f32[64,4,128]{2,1,0:T(4,128)}), f32[64,4,128]{2,1,0:T(4,128)S(1)}, u32[]{:S(2)}, u32[]{:S(2)}) async-start(f32[64,4,128]{2,1,0:T(4,128)} %scatter_fusion), calls=%async_computation.1 | async-start | bytes 262144 | tf_op jit(solution)/shard_map/all_to_all | solution.py:150
  39.2 5.3 %collective-permute-start.4 = (f32[3,6,1,4,32]{4,2,1,3,0:T(1,128)S(1)}, f32[3,6,1,4,32]{4,2,1,3,0:T(1,128)S(1)}, u32[]{:S(2)}, u32[]{:S(2)}) collective-permute-start(f32[3,6,1,4,32]{4,2,1,3,0:T(1,128)S(1)} %get-tuple-element.506), channel_id=1, source_target_pairs={{0,1},{1,2},{2,3},{4,5},{5,6},{6,7},{8,9},{9,10},{10,11},{12,13},{... | collective-permute-start | bytes 27656 | tf_op jit(solution)/shard_map/ppermute | solution.py:24
  42.9 5.9 %collective-permute-start.5 = (f32[3,6,1,4,32]{4,2,1,3,0:T(1,128)S(1)}, f32[3,6,1,4,32]{4,2,1,3,0:T(1,128)S(1)}, u32[]{:S(2)}, u32[]{:S(2)}) collective-permute-start(f32[3,6,1,4,32]{4,2,1,3,0:T(1,128)S(1)} %get-tuple-element.507), channel_id=1, source_target_pairs={{1,0},{2,1},{3,2},{5,4},{6,5},{7,6},{9,8},{10,9},{11,10},{13,12},{... | collective-permute-start | bytes 27656 | tf_op jit(solution)/shard_map/ppermute | solution.py:26
  112.5 5.3 %collective-permute-start.6 = (f32[1,6,18,32]{3,2,1,0:T(8,128)S(1)}, f32[1,6,18,32]{3,2,1,0:T(8,128)S(1)}, u32[]{:S(2)}, u32[]{:S(2)}) collective-permute-start(f32[1,6,18,32]{3,2,1,0:T(8,128)S(1)} %get-tuple-element.515), channel_id=1, source_target_pairs={{0,16},{1,17},{2,18},{3,19},{4,20},{5,21},{6,22},{7,23},{8,24},{9,... | collective-permute-start | bytes 41480 | tf_op jit(solution)/shard_map/ppermute | solution.py:24
  115.9 6.2 %collective-permute-start.7 = (f32[1,6,18,32]{3,2,1,0:T(8,128)S(1)}, f32[1,6,18,32]{3,2,1,0:T(8,128)S(1)}, u32[]{:S(2)}, u32[]{:S(2)}) collective-permute-start(f32[1,6,18,32]{3,2,1,0:T(8,128)S(1)} %get-tuple-element.514), channel_id=1, source_target_pairs={{16,0},{17,1},{18,2},{19,3},{20,4},{21,5},{22,6},{23,7},{24,8},{25... | collective-permute-start | bytes 41480 | tf_op jit(solution)/shard_map/ppermute | solution.py:26
  123.5 4.8 %collective-permute-start.9 = (f32[5,1,18,32]{3,2,1,0:T(8,128)S(1)}, f32[5,1,18,32]{3,2,1,0:T(8,128)S(1)}, u32[]{:S(2)}, u32[]{:S(2)}) collective-permute-start(f32[5,1,18,32]{3,2,1,0:T(8,128)S(1)} %get-tuple-element.513), channel_id=1, source_target_pairs={{4,0},{8,4},{12,8},{5,1},{9,5},{13,9},{6,2},{10,6},{14,10},{7,3},{... | collective-permute-start | bytes 34568 | tf_op jit(solution)/shard_map/ppermute | solution.py:26
  128.4 4.9 %collective-permute-start.10 = (f32[5,8,1,32]{3,2,1,0:T(1,128)S(1)}, f32[5,8,1,32]{3,2,1,0:T(1,128)S(1)}, u32[]{:S(2)}, u32[]{:S(2)}) collective-permute-start(f32[5,8,1,32]{3,2,1,0:T(1,128)S(1)} %get-tuple-element.508), channel_id=1, source_target_pairs={{0,1},{1,2},{2,3},{4,5},{5,6},{6,7},{8,9},{9,10},{10,11},{12,13},{... | collective-permute-start | bytes 15368 | tf_op jit(solution)/shard_map/ppermute | solution.py:24
  131.8 5.7 %collective-permute-start.11 = (f32[5,8,1,32]{3,2,1,0:T(1,128)S(1)}, f32[5,8,1,32]{3,2,1,0:T(1,128)S(1)}, u32[]{:S(2)}, u32[]{:S(2)}) collective-permute-start(f32[5,8,1,32]{3,2,1,0:T(1,128)S(1)} %get-tuple-element.509), channel_id=1, source_target_pairs={{1,0},{2,1},{3,2},{5,4},{6,5},{7,6},{9,8},{10,9},{11,10},{13,12},{... | collective-permute-start | bytes 15368 | tf_op jit(solution)/shard_map/ppermute | solution.py:26
  137.7 5.9 %collective-permute-start.13 = (f32[1,4,16,32]{3,2,1,0:T(8,128)S(1)}, f32[1,4,16,32]{3,2,1,0:T(8,128)S(1)}, u32[]{:S(2)}, u32[]{:S(2)}) collective-permute-start(f32[1,4,16,32]{3,2,1,0:T(8,128)S(1)} %broadcast_divide_fusion), channel_id=1, source_target_pairs={{16,0},{17,1},{18,2},{19,3},{20,4},{21,5},{22,6},{23,7},{24,8},{25... | collective-permute-start | bytes 24584 | tf_op jit(solution)/shard_map/ppermute | solution.py:26
  139.0 6.1 %collective-permute-start.12 = (f32[1,4,16,32]{3,2,1,0:T(8,128)S(1)}, f32[1,4,16,32]{3,2,1,0:T(8,128)S(1)}, u32[]{:S(2)}, u32[]{:S(2)}) collective-permute-start(f32[1,4,16,32]{3,2,1,0:T(8,128)S(1)} %broadcast_divide_fusion), channel_id=1, source_target_pairs={{0,16},{1,17},{2,18},{3,19},{4,20},{5,21},{6,22},{7,23},{8,24},{9,... | collective-permute-start | bytes 24584 | tf_op jit(solution)/shard_map/ppermute | solution.py:24
  147.4 5.1 %collective-permute-start.15 = (f32[3,1,16,32]{3,2,1,0:T(8,128)S(1)}, f32[3,1,16,32]{3,2,1,0:T(8,128)S(1)}, u32[]{:S(2)}, u32[]{:S(2)}) collective-permute-start(f32[3,1,16,32]{3,2,1,0:T(8,128)S(1)} %get-tuple-element.519), channel_id=1, source_target_pairs={{4,0},{8,4},{12,8},{5,1},{9,5},{13,9},{6,2},{10,6},{14,10},{7,3},{... | collective-permute-start | bytes 18440 | tf_op jit(solution)/shard_map/ppermute | solution.py:26
  152.6 4.8 %collective-permute-start.16 = (f32[3,6,1,32]{3,2,1,0:T(1,128)S(1)}, f32[3,6,1,32]{3,2,1,0:T(1,128)S(1)}, u32[]{:S(2)}, u32[]{:S(2)}) collective-permute-start(f32[3,6,1,32]{3,2,1,0:T(1,128)S(1)} %get-tuple-element.516), channel_id=1, source_target_pairs={{0,1},{1,2},{2,3},{4,5},{5,6},{6,7},{8,9},{9,10},{10,11},{12,13},{... | collective-permute-start | bytes 6920 | tf_op jit(solution)/shard_map/ppermute | solution.py:24
  156.0 5.6 %collective-permute-start.17 = (f32[3,6,1,32]{3,2,1,0:T(1,128)S(1)}, f32[3,6,1,32]{3,2,1,0:T(1,128)S(1)}, u32[]{:S(2)}, u32[]{:S(2)}) collective-permute-start(f32[3,6,1,32]{3,2,1,0:T(1,128)S(1)} %get-tuple-element.517), channel_id=1, source_target_pairs={{1,0},{2,1},{3,2},{5,4},{6,5},{7,6},{9,8},{10,9},{11,10},{13,12},{... | collective-permute-start | bytes 6920 | tf_op jit(solution)/shard_map/ppermute | solution.py:26
  258.2 11.5 %collective-permute-start.18 = (f32[1,6,18,4,32]{4,2,1,3,0:T(8,128)S(1)}, f32[1,6,18,4,32]{4,2,1,3,0:T(8,128)S(1)}, u32[]{:S(2)}, u32[]{:S(2)}) collective-permute-start(f32[1,6,18,4,32]{4,2,1,3,0:T(8,128)S(1)} %get-tuple-element.505), channel_id=1, source_target_pairs={{0,16},{1,17},{2,18},{3,19},{4,20},{5,21},{6,22},{7,23},{8,24},{9,... | collective-permute-start | bytes 165896 | tf_op jit(solution)/shard_map/ppermute | solution.py:24
  262.7 11.7 %collective-permute-start.19 = (f32[1,6,18,4,32]{4,2,1,3,0:T(8,128)S(1)}, f32[1,6,18,4,32]{4,2,1,3,0:T(8,128)S(1)}, u32[]{:S(2)}, u32[]{:S(2)}) collective-permute-start(f32[1,6,18,4,32]{4,2,1,3,0:T(8,128)S(1)} %get-tuple-element.504), channel_id=1, source_target_pairs={{16,0},{17,1},{18,2},{19,3},{20,4},{21,5},{22,6},{23,7},{24,8},{25... | collective-permute-start | bytes 165896 | tf_op jit(solution)/shard_map/ppermute | solution.py:26
  274.4 3.9 %collective-permute-start.20 = (f32[5,1,18,4,32]{4,2,1,3,0:T(8,128)S(1)}, f32[5,1,18,4,32]{4,2,1,3,0:T(8,128)S(1)}, u32[]{:S(2)}, u32[]{:S(2)}) collective-permute-start(f32[5,1,18,4,32]{4,2,1,3,0:T(8,128)S(1)} %get-tuple-element.502), channel_id=1, source_target_pairs={{0,4},{4,8},{8,12},{1,5},{5,9},{9,13},{2,6},{6,10},{10,14},{3,7},{... | collective-permute-start | bytes 138248 | tf_op jit(solution)/shard_map/ppermute | solution.py:24
  279.9 10.4 %collective-permute-start.22 = (f32[5,8,1,4,32]{4,2,1,3,0:T(1,128)S(1)}, f32[5,8,1,4,32]{4,2,1,3,0:T(1,128)S(1)}, u32[]{:S(2)}, u32[]{:S(2)}) collective-permute-start(f32[5,8,1,4,32]{4,2,1,3,0:T(1,128)S(1)} %get-tuple-element.500), channel_id=1, source_target_pairs={{0,1},{1,2},{2,3},{4,5},{5,6},{6,7},{8,9},{9,10},{10,11},{12,13},{... | collective-permute-start | bytes 61448 | tf_op jit(solution)/shard_map/ppermute | solution.py:24
  281.9 8.4 %collective-permute-start.23 = (f32[5,8,1,4,32]{4,2,1,3,0:T(1,128)S(1)}, f32[5,8,1,4,32]{4,2,1,3,0:T(1,128)S(1)}, u32[]{:S(2)}, u32[]{:S(2)}) collective-permute-start(f32[5,8,1,4,32]{4,2,1,3,0:T(1,128)S(1)} %get-tuple-element.501), channel_id=1, source_target_pairs={{1,0},{2,1},{3,2},{5,4},{6,5},{7,6},{9,8},{10,9},{11,10},{13,12},{... | collective-permute-start | bytes 61448 | tf_op jit(solution)/shard_map/ppermute | solution.py:26
  284.0 14.7 %all-to-all-start.2 = ((f32[64,4,128]{2,1,0:T(4,128)}), f32[64,4,128]{2,1,0:T(4,128)S(1)}, u32[]{:S(2)}, u32[]{:S(2)}) async-start(f32[64,4,128]{2,1,0:T(4,128)} %broadcast_select_fusion), calls=%async_computation.2 | async-start | bytes 262144 | tf_op jit(solution)/shard_map/all_to_all | solution.py:179
  (7 other events, 99.0 us)
where the time goes:
time: 301 us; the launch traced here: 300 us
  other arithmetic  145 us (48%)
  starting transfers between devices  73 us (24%)
  waiting for transfers between devices  45.3 us (15%)
  local copies, waits for them, and re-layouts  27.2 us (9%)
  loops' own time  8.24 us (3%)
    reduce_sum x27, other arithmetic, pair_block(): jnp.sum(coupling * delta_x, axis=-2)  82.2 us
    reduce_sum x27, other arithmetic, pair_block(): far_sum = jnp.sum(kernel * own_wt, axis=-2)  50.1 us
    ppermute x12, starting transfers between devices, with_halo(): lax.ppermute(tail, axis, [(i, (i + 1) % count) for i in range(ends)])  37.2 us
    ppermute x12, waiting for transfers between devices, with_halo(): lax.ppermute(head, axis, [((i + 1) % count, i) for i in range(ends)])  30.1 us
    ppermute x12, starting transfers between devices, with_halo(): lax.ppermute(head, axis, [((i + 1) % count, i) for i in range(ends)])  15.5 us
    dynamic_update_slice x54, local copies, waits for them, and re-layouts, put_window(): return lax.dynamic_update_slice(values, update, corner)  11 us
    ppermute x12, waiting for transfers between devices, with_halo(): lax.ppermute(tail, axis, [(i, (i + 1) % count) for i in range(ends)])  8.42 us
    another operation x2, loops' own time, sweep_pairs(): return lax.fori_loop(0, 27, one_offset, (own_acc, far_acc))  8.24 us
  transfers between devices with their start and end apart: 27, of which 14 were waited for; matrix products, arithmetic and copies ran while one was open for 5% of the time, Pallas kernels for 0%

commit v1 on v0

v1 whole, which is shorter than its diff:
```python
import functools
import math

import jax
import jax.numpy as jnp
from jax import lax
from jax.experimental import pallas as pl
from jax.experimental.pallas import tpu as pltpu
from jax.sharding import PartitionSpec as P

MOST = 2
AXES = ("gx", "gy", "gz")
LANES = 128
GROUP = 32

kernel_width = 0.05
cutoff_sq = 0.5
sharp = cutoff_sq / kernel_width
log2e = math.log2(math.e)
scale = math.sqrt(log2e / cutoff_sq)
gain = sharp * log2e
shift = math.log2(gain)
grad_unit = 2.0 / (gain * scale)

VMEM = pl.BlockSpec(memory_space=pltpu.VMEM)
SMEM = pl.BlockSpec(memory_space=pltpu.SMEM)


def div_rem(value, size):
    if size & (size - 1) == 0:
        return lax.shift_right_logical(value, size.bit_length() - 1), value & (size - 1)
    return lax.div(value, size), lax.rem(value, size)


def route_kernel(spans, sizes, cell_ref, count_ref, xyz_ref, wt_ref, out_ref, slot_ref, used_ref):
    blocks, _, pts = xyz_ref.shape
    bricks = sizes[0] * sizes[1] * sizes[2]
    lane = lax.broadcasted_iota(jnp.int32, (1, pts), 1)
    out_ref[:, :, : 4 * pts] = jnp.zeros((out_ref.shape[0], 1, 4 * pts), jnp.float32)
    out_ref[:, :, 4 * pts :] = jnp.full((out_ref.shape[0], 1, LANES), -1.0, jnp.float32)

    def clear(i, carry):
        used_ref[i] = 0
        return carry

    lax.fori_loop(0, bricks, clear, 0, unroll=8)

    def one(b, carry):
        rest, along_z = div_rem(cell_ref[b], spans[2] * sizes[2])
        along_x, along_y = div_rem(rest, spans[1] * sizes[1])
        brick_x, in_x = div_rem(along_x, spans[0])
        brick_y, in_y = div_rem(along_y, spans[1])
        brick_z, in_z = div_rem(along_z, spans[2])
        target = (brick_x * sizes[1] + brick_y) * sizes[2] + brick_z
        local = (in_x * spans[1] + in_y) * spans[2] + in_z
        before = used_ref[target]
        used_ref[target] = before + 1
        slot = target * MOST + before
        slot_ref[b] = slot
        count = count_ref[b]
        for f in range(3):
            out_ref[slot, :, f * pts : (f + 1) * pts] = xyz_ref[b, f : f + 1, :]
        out_ref[slot, :, 3 * pts : 4 * pts] = jnp.where(lane < count, wt_ref[pl.ds(b, 1), :], 0.0)
        head = lax.broadcasted_iota(jnp.int32, (1, LANES), 1)
        tag = jnp.where(head == 0, local, count)
        out_ref[slot, :, 4 * pts :] = tag.astype(jnp.float32)
        return carry

    lax.fori_loop(0, blocks, one, 0)


def lane_ids(shape):
    return lax.broadcasted_iota(jnp.int32, shape, len(shape) - 1)


def tile_of(ref, lead, i):
    j = i // 2
    first = ref[lead + (slice(None), pl.ds(j * LANES, LANES))]
    if i % 2 == 0:
        return first
    second = ref[lead + (slice(None), pl.ds((j + 1) * LANES, LANES))]
    return pltpu.roll(jnp.where(lane_ids(first.shape) < 64, second, first), 64, first.ndim - 1)


def untile(parts, chunk):
    total = None
    lane = lane_ids(parts[0].shape)
    for i, low in ((2 * chunk, None), (2 * chunk - 1, True), (2 * chunk + 1, False)):
        if not 0 <= i < len(parts):
            continue
        part = parts[i]
        if low is not None:
            part = pltpu.roll(part, 64, part.ndim - 1)
            part = jnp.where(lane < 64 if low else lane >= 64, part, 0.0)
        total = part if total is None else total + part
    return jnp.zeros_like(parts[0]) if total is None else total


def slot_view(label, spans, rows, planes, tiles):
    in_y, in_z = div_rem(label, spans[2])
    tile, odd = div_rem(in_z, 2)
    lane = lane_ids((1, LANES))
    start = odd * 32
    mask = jnp.where((lane >= start) & (lane < start + 96), 1.0, 0.0)
    index = [(p * rows + in_y + dy) * tiles + tile for p in range(planes) for dy in range(3)]
    return mask, index


def density_kernel(
    spans, planes, in_ref, gauss_ref, origin_ref,
    pt_ref, tile_ref, zg_ref, label_ref, count_ref,
    rows_ref, acc_ref, red_ref,
):
    slots = in_ref.shape[0]
    pts = LANES
    rows = spans[1] + 2
    tiles = spans[2] // 2
    per = LANES // 8
    batches = slots // per
    for s in range(slots):
        head = in_ref[s, :, 4 * pts : 5 * pts]
        whole = head.astype(jnp.int32)
        label_ref[s] = whole[0, 0]
        count_ref[s] = whole[0, 1]
        for f in range(4):
            rows_ref[s, f : f + 1, :] = in_ref[s, :, f * pts : (f + 1) * pts]
        rows_ref[s, 4:8, :] = jnp.ones((4, pts), jnp.float32)
    field = lane_ids((1, LANES)) & 7
    off = jnp.where(
        field == 0, origin_ref[0], jnp.where(field == 1, origin_ref[1], jnp.where(field == 2, origin_ref[2], 0.0))
    )
    mul = jnp.where(field < 3, scale, 1.0)
    for b in range(batches):
        block = rows_ref[b * per : (b + 1) * per].reshape(per * 8, pts)
        pt_ref[b] = (block.T - off) * mul
    part = lax.broadcasted_iota(jnp.int32, (4, 1), 0)
    goff = jnp.where(
        part == 0, origin_ref[0], jnp.where(part == 1, origin_ref[1], jnp.where(part == 2, origin_ref[2], 0.0))
    )
    gmul = jnp.where(part < 3, scale, 1.0)
    for r in range(planes * rows):
        for i in range(tiles):
            tile_ref[r * tiles + i, 0:4, :] = (tile_of(gauss_ref, (r,), i) - goff) * gmul
            tile_ref[r * tiles + i, 4:8, :] = jnp.zeros((4, LANES), jnp.float32)
    acc_ref[...] = jnp.zeros(acc_ref.shape, jnp.float32)

    def one_slot(slot, carry):
        label = label_ref[slot]

        @pl.when(label >= 0)
        def _():
            batch, place = div_rem(slot, per)
            place = place * 8
            mask, index = slot_view(label, spans, rows, planes, tiles)
            alphas = [tile_ref[j, 3:4, :] * mask for j in index]

            def one_group(g, inner):
                at = pl.ds(pl.multiple_of(g * GROUP, GROUP), GROUP)
                raw = pt_ref[batch, at, :]
                view = pltpu.roll(raw, LANES - place, 1)
                x, y, z, w = (view[:, f : f + 1] for f in range(4))
                total = None
                for n, j in enumerate(index):
                    dx = x - tile_ref[j, 0:1, :]
                    dy = y - tile_ref[j, 1:2, :]
                    dz = z - tile_ref[j, 2:3, :]
                    fall = jnp.exp2(shift - (dx * dx + dy * dy + dz * dz))
                    kern = jnp.exp2(fall)
                    term = kern * alphas[n]
                    total = term if total is None else total + term
                    wk = kern * w
                    acc_ref[j] += jnp.sum(wk.reshape(GROUP // 8, 8, LANES), axis=0) * mask
                zp = 1.0 + jnp.sum(total, axis=1, keepdims=True)
                pt_ref[batch, at, :] = jnp.where(lane_ids(raw.shape) == place + 4, zp, raw)
                return inner

            lax.fori_loop(0, (count_ref[slot] + GROUP - 1) // GROUP, one_group, 0)

        return carry

    lax.fori_loop(0, slots, one_slot, 0)
    red_ref[...] = jnp.zeros(red_ref.shape, jnp.float32)
    for r in range(planes * rows):
        for i in range(tiles):
            red_ref[i, r : r + 1, :] = jnp.sum(acc_ref[r * tiles + i], axis=0, keepdims=True)
    parts = [red_ref[i] for i in range(tiles)]
    for c in range(zg_ref.shape[1] // LANES):
        zg_ref[:, c * LANES : (c + 1) * LANES] = untile(parts, c)[: planes * rows]


def gradient_kernel(
    spans, planes, pt_ref, tin_ref, zg_ref, label_ref, count_ref,
    reply_ref, grad_ref,
    tile_ref, acc_ref, out_ref, red_ref,
):
    slots = reply_ref.shape[0]
    rows = spans[1] + 2
    tiles = spans[2] // 2
    per = LANES // 8
    batches = slots // per
    for r in range(planes * rows):
        for i in range(tiles):
            at = r * tiles + i
            tile_ref[at] = tin_ref[at]
    for i in range(tiles):
        inv = 1.0 / (1.0 + tile_of(zg_ref, (), i))
        for r in range(planes * rows):
            at = r * tiles + i
            tile_ref[at, 4:5, :] = tin_ref[at, 3:4, :] * inv[r : r + 1]
    acc_ref[...] = jnp.zeros(acc_ref.shape, jnp.float32)
    out_ref[...] = jnp.zeros(out_ref.shape, jnp.float32)

    def one_slot(slot, carry):
        label = label_ref[slot]

        @pl.when(label >= 0)
        def _():
            batch, place = div_rem(slot, per)
            place = place * 8
            mask, index = slot_view(label, spans, rows, planes, tiles)

            def one_group(g, inner):
                at = pl.ds(pl.multiple_of(g * GROUP, GROUP), GROUP)
                view = pltpu.roll(pt_ref[batch, at, :], LANES - place, 1)
                x, y, z, w, zp = (view[:, f : f + 1] for f in range(5))
                ip = 1.0 / zp
                px = py = pz = None
                for n, j in enumerate(index):
                    dx = x - tile_ref[j, 0:1, :]
                    dy = y - tile_ref[j, 1:2, :]
                    dz = z - tile_ref[j, 2:3, :]
                    fall = jnp.exp2(shift - (dx * dx + dy * dy + dz * dz))
                    wk = jnp.exp2(fall) * w
                    coef = (tile_ref[j, 3:4, :] * mask) * ip + tile_ref[j, 4:5, :] * mask
                    h = wk * fall * coef
                    dx = h * dx
                    dy = h * dy
                    dz = h * dz
                    px = dx if px is None else px + dx
                    py = dy if py is None else py + dy
                    pz = dz if pz is None else pz + dz
                    den = wk * ip
                    for f, v in enumerate((dx, dy, dz)):
                        acc_ref[j, f] += jnp.sum(v.reshape(GROUP // 8, 8, LANES), axis=0)
                    acc_ref[j, 3] += jnp.sum(den.reshape(GROUP // 8, 8, LANES), axis=0) * mask
                val = out_ref[batch, at, :]
                lane = lane_ids(val.shape)
                for f, v in enumerate((px, py, pz)):
                    val = jnp.where(lane == place + 1 + f, jnp.sum(v, axis=1, keepdims=True) * grad_unit, val)
                out_ref[batch, at, :] = val
                return inner

            lax.fori_loop(0, (count_ref[slot] + GROUP - 1) // GROUP, one_group, 0)

        return carry

    lax.fori_loop(0, slots, one_slot, 0)
    for b in range(batches):
        pt = pt_ref[b]
        lane = lane_ids(pt.shape)
        zp = pltpu.roll(pt, LANES - 4, 1)
        w = pltpu.roll(pt, LANES - 3, 1)
        head = (lane & 7) == 0
        ok = head & (w > 0.0)
        zp = jnp.where(ok, zp, 1.0)
        loss = kernel_width * sharp - kernel_width * jnp.log(zp)
        val = jnp.where(head, jnp.where(ok, loss, 0.0), out_ref[b])
        reply_ref[b * per : (b + 1) * per] = val.T.reshape(per, 8, LANES)[:, :4, :]
    for f in range(4):
        red_ref[...] = jnp.zeros(red_ref.shape, jnp.float32)
        for r in range(planes * rows):
            for i in range(tiles):
                red_ref[i, r : r + 1, :] = jnp.sum(acc_ref[r * tiles + i, f], axis=0, keepdims=True)
        parts = [red_ref[i] for i in range(tiles)]
        unit = -grad_unit if f < 3 else 1.0
        for c in range(grad_ref.shape[2] // LANES):
            grad_ref[f, :, c * LANES : (c + 1) * LANES] = untile(parts, c)[: planes * rows] * unit


def pick_kernel(slot_ref, reply_ref, out_ref):
    def one(b, carry):
        out_ref[b] = reply_ref[slot_ref[b]]
        return carry

    lax.fori_loop(0, out_ref.shape[0], one, 0, unroll=4)


def swap(value, axis, odd):
    count = lax.axis_size(axis)
    pairs = []
    for i in range(odd, count - 1, 2):
        pairs += [(i, i + 1), (i + 1, i)]
    if odd and count % 2 == 0 and count > 2:
        pairs += [(0, count - 1), (count - 1, 0)]
    return lax.ppermute(value, axis, pairs)


def trade(low, high, axis):
    count = lax.axis_size(axis)
    here = lax.axis_index(axis)
    even = here % 2 == 0
    first = swap(jnp.where(even, high, low), axis, 0)
    second = swap(jnp.where(even, low, high), axis, 1) if count > 2 else jnp.zeros_like(first)
    from_low = jnp.where(here > 0, jnp.where(even, second, first), 0.0)
    from_high = jnp.where(here < count - 1, jnp.where(even, first, second), 0.0)
    return from_low, from_high


def on_device(
    point_xyz, point_weight, block_cell, block_count, gauss_mean, gauss_opacity, gauss_count
):
    blocks, _, pts = point_xyz.shape
    span_x, span_y, span_z, _, slots = gauss_mean.shape
    spans = (span_x, span_y, span_z)
    sizes = tuple(lax.axis_size(a) for a in AXES)
    if span_x != 1 or slots != 32 or pts != LANES or span_y < 2 or span_z % 4:
        raise ValueError("unsupported brick")
    bricks = sizes[0] * sizes[1] * sizes[2]
    places = bricks * MOST
    room = -(-places // 16) * 16
    f32 = jnp.float32

    outgoing, send_slot = pl.pallas_call(
        functools.partial(route_kernel, spans, sizes),
        out_shape=(
            jax.ShapeDtypeStruct((places, 1, 5 * pts), f32),
            jax.ShapeDtypeStruct((blocks,), jnp.int32),
        ),
        in_specs=[SMEM, SMEM, VMEM, VMEM],
        out_specs=(VMEM, SMEM),
        scratch_shapes=[pltpu.SMEM((bricks,), jnp.int32)],
        name="route",
    )(block_cell, block_count, point_xyz, point_weight)
    incoming = lax.all_to_all(outgoing, AXES, split_axis=0, concat_axis=0, tiled=True)

    present = jnp.arange(slots, dtype=jnp.int32) < gauss_count[..., None]
    own = jnp.concatenate([gauss_mean, jnp.where(present, gauss_opacity, 0.0)[..., None, :]], axis=3)
    own = own[0].transpose(0, 2, 1, 3).reshape(span_y, 4, span_z * slots)
    if sizes[0] == 2:
        stack = jnp.stack([own, swap(own, "gx", 0)])
    else:
        stack = jnp.stack([own, *trade(own, own, "gx")])
    planes = stack.shape[0]
    rows = span_y + 2
    low, high = trade(stack[:, :1], stack[:, -1:], "gy")
    stack = jnp.concatenate([low, stack, high], axis=1).reshape(planes * rows, 4, span_z * slots)
    low, high = trade(stack[..., :slots], stack[..., -slots:], "gz")
    width = (span_z + 2) * slots
    wide = -(-width // LANES) * LANES
    stack = jnp.concatenate(
        [low, stack, high, jnp.zeros((planes * rows, 4, wide - width), f32)], axis=2
    )
    origin = jnp.stack([lax.axis_index(a) * s for a, s in zip(AXES, spans)]).astype(f32)

    tiles = span_z // 2
    count_tiles = planes * rows * tiles
    tall = -(-(planes * rows) // 8) * 8
    points, gtiles, zg_part, label, count = pl.pallas_call(
        functools.partial(density_kernel, spans, planes),
        out_shape=(
            jax.ShapeDtypeStruct((places // 16, LANES, LANES), f32),
            jax.ShapeDtypeStruct((count_tiles, 8, LANES), f32),
            jax.ShapeDtypeStruct((planes * rows, wide), f32),
            jax.ShapeDtypeStruct((places,), jnp.int32),
            jax.ShapeDtypeStruct((places,), jnp.int32),
        ),
        in_specs=[VMEM, VMEM, SMEM],
        out_specs=(VMEM, VMEM, VMEM, SMEM, SMEM),
        scratch_shapes=[
            pltpu.VMEM((places, 8, LANES), f32),
            pltpu.VMEM((count_tiles, 8, LANES), f32),
            pltpu.VMEM((tiles, tall, LANES), f32),
        ],
        name="density",
    )(incoming, stack, origin)

    part = zg_part.reshape(planes, rows, wide)
    if sizes[0] == 2:
        part = part + swap(part[::-1], "gx", 0)
    else:
        low, high = trade(part[1], part[2], "gx")
        whole = part[0] + low + high
        part = jnp.stack([whole, *trade(whole, whole, "gx")])
    low, high = trade(part[:, :2], part[:, -2:], "gy")
    part = jnp.concatenate([part[:, :2] + low, part[:, 2:-2], part[:, -2:] + high], axis=1)
    edge = 2 * slots
    low, high = trade(part[..., :edge], part[..., width - edge : width], "gz")
    part = jnp.concatenate(
        [
            part[..., :edge] + low,
            part[..., edge : width - edge],
            part[..., width - edge : width] + high,
            jnp.zeros((planes, rows, wide - width), f32),
        ],
        axis=2,
    )
    zg_sum = part.reshape(planes * rows, wide)

    reply, grad_part = pl.pallas_call(
        functools.partial(gradient_kernel, spans, planes),
        out_shape=(
            jax.ShapeDtypeStruct((places, 4, LANES), f32),
            jax.ShapeDtypeStruct((4, planes * rows, wide), f32),
        ),
        in_specs=[VMEM, VMEM, VMEM, SMEM, SMEM],
        out_specs=(VMEM, VMEM),
        scratch_shapes=[
            pltpu.VMEM((count_tiles, 8, LANES), f32),
            pltpu.VMEM((count_tiles, 4, 8, LANES), f32),
            pltpu.VMEM((places // 16, LANES, LANES), f32),
            pltpu.VMEM((tiles, tall, LANES), f32),
        ],
        name="gradient",
    )(points, gtiles, zg_sum, label, count)

    answer = lax.all_to_all(reply, AXES, split_axis=0, concat_axis=0, tiled=True)
    point_out = pl.pallas_call(
        pick_kernel,
        out_shape=jax.ShapeDtypeStruct((blocks, 4, pts), f32),
        in_specs=[SMEM, VMEM],
        out_specs=VMEM,
        name="pick",
    )(send_slot, answer)

    grad = grad_part.reshape(4, planes, rows, wide)
    if sizes[0] == 2:
        grad = grad[:, 0] + swap(grad[:, 1], "gx", 0)
    else:
        low, high = trade(grad[:, 1], grad[:, 2], "gx")
        grad = grad[:, 0] + low + high
    low, high = trade(grad[:, :1], grad[:, -1:], "gy")
    grad = jnp.concatenate(
        [grad[:, 1:2] + low, grad[:, 2:-2], grad[:, -2:-1] + high], axis=1
    )
    low, high = trade(grad[..., :slots], grad[..., width - slots : width], "gz")
    grad = jnp.concatenate(
        [
            grad[..., slots : 2 * slots] + low,
            grad[..., 2 * slots : width - 2 * slots],
            grad[..., width - 2 * slots : width - slots] + high,
        ],
        axis=2,
    )
    grad = grad.reshape(4, span_y, span_z, slots).transpose(1, 2, 0, 3)[None]
    total_g = 1.0 + part[0, 1:-1, slots : width - slots].reshape(1, span_y, span_z, slots)
    opacity = jnp.where(
        present,
        kernel_width * sharp - kernel_width * jnp.log(total_g) - kernel_width * grad[..., 3, :],
        0.0,
    )
    gauss_grad = jnp.concatenate([grad[..., :3, :], opacity[..., None, :]], axis=3)
    return point_out, gauss_grad


def solution(mesh):
    return jax.shard_map(
        on_device,
        mesh=mesh,
        in_specs=(
            P(AXES, None, None),
            P(AXES, None),
            P(AXES),
            P(AXES),
            P("gx", "gy", "gz", None, None),
            P("gx", "gy", "gz", None),
            P("gx", "gy", "gz"),
        ),
        out_specs=(P(AXES, None, None), P("gx", "gy", "gz", None, None)),
        check_vma=False,
    )
```

time: 301 us -> 169 us (0.56)
  other arithmetic: 145 us -> 3.98 us
  Pallas kernels: 0 us -> 91.3 us
  starting transfers between devices: 73 us -> 39.7 us
  local copies, waits for them, and re-layouts: 27.2 us -> 6.37 us
  waiting for transfers between devices: 45.3 us -> 27.1 us
  loops' own time: 8.24 us -> 0 us
    reduce_sum x55 -> x0, other arithmetic: 132 us -> none  [the longest x27 82.2 us: pair_block(): jnp.sum(coupling * delta_x, axis=-2)]
    pallas_call x0 -> x4, Pallas kernels: none -> 91.3 us  [the longest x1 46 us: on_device(): pl.pallas_call(functools.partial(gradient_kernel, spans, planes), out_sha...]
    ppermute x24 -> x15, starting transfers between devices: 52.7 us -> 28.4 us  [swap(): return lax.ppermute(value, axis, pairs)]
    ppermute x24 -> x15, waiting for transfers between devices: 38.5 us -> 20.5 us  [swap(): return lax.ppermute(value, axis, pairs)]
    dynamic_update_slice x54 -> x0, local copies, waits for them, and re-layouts: 11 us -> none  [put_window(): return lax.dynamic_update_slice(values, update, corner)]
    all_to_all x3 -> x2, starting transfers between devices: 20.3 us -> 11.3 us  [the longest x1 6.26 us: on_device(): lax.all_to_all(reply, AXES, split_axis=0, concat_axis=0, tiled=True)]
    scatter x3 -> x0, local copies, waits for them, and re-layouts: 8.55 us -> none  [the longest x1 5.32 us: on_device(): jnp.zeros((bricks * MOST, 4, points_len), jnp.float32).at[send_slot]]
    another operation x2 -> x0, loops' own time: 8.24 us -> none  [sweep_pairs(): return lax.fori_loop(0, 27, one_offset, (own_acc, far_acc))]
  transfers between devices with their start and end apart: 27 -> 17, of which waited for: 14 -> 10; matrix products, arithmetic and copies ran while one was open for 5% -> 2% of each run, Pallas kernels for 0% -> 1%
where the time goes in v1:
time: 169 us
  Pallas kernels  91.3 us (54%)
  starting transfers between devices  39.7 us (23%)
  waiting for transfers between devices  27.1 us (16%)
  local copies, waits for them, and re-layouts  6.37 us (4%)
  other arithmetic  3.98 us (2%)
    pallas_call x1, Pallas kernels, on_device(): pl.pallas_call(functools.partial(gradient_kernel, spans, planes), out_sha...  46 us
    pallas_call x1, Pallas kernels, on_device(): pl.pallas_call(functools.partial(density_kernel, spans, planes), out_shap...  41.4 us
    ppermute x15, starting transfers between devices, swap(): return lax.ppermute(value, axis, pairs)  28.4 us
    ppermute x15, waiting for transfers between devices, swap(): return lax.ppermute(value, axis, pairs)  20.5 us
    all_to_all x1, waiting for transfers between devices, on_device(): lax.all_to_all(reply, AXES, split_axis=0, concat_axis=0, tiled=True)  6.39 us
    all_to_all x1, starting transfers between devices, on_device(): lax.all_to_all(reply, AXES, split_axis=0, concat_axis=0, tiled=True)  6.26 us
    all_to_all x1, starting transfers between devices, on_device(): lax.all_to_all(outgoing, AXES, split_axis=0, concat_axis=0, tiled=True)  5.01 us
    unnamed x10, local copies, waits for them, and re-layouts  3.39 us
  transfers between devices with their start and end apart: 17, of which 10 were waited for; matrix products, arithmetic and copies ran while one was open for 2% of the time, Pallas kernels for 1%

profile of v1, /device:TPU:0, one launch (start us, length us, event | category | flops | bytes accessed | tf_op | source)
XLA Modules:
  0.0 169.4 jit_solution(3899819304785081828)
XLA Ops:
  0.6 0.8 select_bitcast_fusion
  1.5 0.9 maximum_bitcast_fusion
  2.5 3.0 %collective-permute-start = (f32[4,4,512]{2,1,0:T(4,128)S(1)}, f32[4,4,512]{2,1,0:T(4,128)S(1)}, u32[]{:S(2)}, u32[]{:S(2)}) collective-permute-start(f32[4,4,512]{2,1,0:T(4,128)S(1)} %reshape.76), channel_id=1, source_target_pairs={{0,16},{16,0},{1,17},{17,1},{2,18},{18,2},{3,19},{19,3},{4,20},{20... | collective-permute-start | bytes 98312 | tf_op jit(solution)/shard_map/ppermute | solution.py:295
  5.7 1.8 %collective-permute-done = f32[4,4,512]{2,1,0:T(4,128)S(1)} collective-permute-done((f32[4,4,512]{2,1,0:T(4,128)S(1)}, f32[4,4,512]{2,1,0:T(4,128)S(1)}, u32[]{:S(2)}, u32[]{:S(2)}) %collective-permute-start) | collective-permute-done | bytes 32800 | tf_op jit(solution)/shard_map/ppermute | solution.py:295
  7.5 2.1 %collective-permute-start.1 = (f32[2,1,4,512]{3,2,1,0:T(4,128)S(1)}, f32[2,1,4,512]{3,2,1,0:T(4,128)S(1)}, u32[]{:S(2)}, u32[]{:S(2)}) collective-permute-start(f32[2,1,4,512]{3,2,1,0:T(4,128)S(1)} %get-tuple-element.25), channel_id=1, source_target_pairs={{4,8},{8,4},{0,12},{12,0},{5,9},{9,5},{1,13},{13,1},{6,10},{10,6},... | collective-permute-start | bytes 49160 | tf_op jit(solution)/shard_map/ppermute | solution.py:295
  10.4 2.3 %route.1 = (f32[64,1,640]{2,1,0:T(1,128)}, s32[48]{0:T(128)}) custom-call(s32[48]{0:T(128)} %cell_ref.1, s32[48]{0:T(128)} %count_ref.1, f32[48,3,128]{2,1,0:T(4,128)} %copy.12.xyz_ref, f32[48,128]{1,0:T(8,128)} %wt_ref.1), custom_call_target="tpu_custom_call" | custom-call | tf_op jit(solution)/shard_map/route/pallas_call | solution.py:323
  12.7 5.0 %all-to-all-start = ((f32[64,1,640]{2,1,0:T(1,128)}), f32[64,1,640]{2,1,0:T(1,128)S(1)}, u32[]{:S(2)}, u32[]{:S(2)}) async-start(f32[64,1,640]{2,1,0:T(1,128)} %get-tuple-element.12), calls=%async_computation | async-start | bytes 327680 | tf_op jit(solution)/shard_map/all_to_all | solution.py:334
  17.9 3.7 %collective-permute-start.3 = (f32[12,4,32]{2,1,0:T(4,128)S(1)}, f32[12,4,32]{2,1,0:T(4,128)S(1)}, u32[]{:S(2)}, u32[]{:S(2)}) collective-permute-start(f32[12,4,32]{2,1,0:T(4,128)S(1)} %get-tuple-element.28), channel_id=1, source_target_pairs={{1,2},{2,1},{0,3},{3,0},{5,6},{6,5},{4,7},{7,4},{9,10},{10,9},{8,1... | collective-permute-start | bytes 18440 | tf_op jit(solution)/shard_map/ppermute | solution.py:295
  22.3 3.6 %collective-permute-done.3 = f32[12,4,32]{2,1,0:T(4,128)S(1)} collective-permute-done((f32[12,4,32]{2,1,0:T(4,128)S(1)}, f32[12,4,32]{2,1,0:T(4,128)S(1)}, u32[]{:S(2)}, u32[]{:S(2)}) %collective-permute-start.3) | collective-permute-done | bytes 6176 | tf_op jit(solution)/shard_map/ppermute | solution.py:295
  25.9 0.8 maximum_maximum_fusion.gauss_ref
  27.5 41.4 %density.1 = (f32[4,128,128]{2,1,0:T(8,128)}, f32[96,8,128]{2,1,0:T(8,128)}, f32[12,640]{1,0:T(8,128)}, s32[64]{0:T(128)}, s32[64]{0:T(128)}) custom-call(f32[64,1,640]{2,1,0:T(1,128)} %copy-done, f32[12,4,640]{2,1,0:T(4,128)} %maximum_maximum_fusion.gauss_ref, f32[3]{0:T(128)} %add_convert_fusion.origin_ref), custom_call_target="tpu_custom_call" | custom-call | tf_op jit(solution)/shard_map/density/pallas_call | solution.py:358
  69.7 4.0 %collective-permute-done.5 = f32[2,6,640]{2,1,0:T(8,128)S(1)} collective-permute-done((f32[2,6,640]{2,1,0:T(8,128)S(1)}, f32[2,6,640]{2,1,0:T(8,128)S(1)}, u32[]{:S(2)}, u32[]{:S(2)}) %collective-permute-start.5) | collective-permute-done | bytes 30752 | tf_op jit(solution)/shard_map/ppermute | solution.py:295
  73.8 8.7 %collective-permute-start.7 = (f32[2,2,640]{2,1,0:T(2,128)S(1)}, f32[2,2,640]{2,1,0:T(2,128)S(1)}, u32[]{:S(2)}, u32[]{:S(2)}) collective-permute-start(f32[2,2,640]{2,1,0:T(2,128)S(1)} %get-tuple-element.44), channel_id=1, source_target_pairs={{0,4},{4,0},{8,12},{12,8},{1,5},{5,1},{9,13},{13,9},{2,6},{6,2},{1... | collective-permute-start | bytes 30728 | tf_op jit(solution)/shard_map/ppermute | solution.py:295
  82.5 0.8 collective-permute-done.7
  83.6 3.5 %collective-permute-done.9 = f32[2,6,64]{2,1,0:T(8,128)S(1)} collective-permute-done((f32[2,6,64]{2,1,0:T(8,128)S(1)}, f32[2,6,64]{2,1,0:T(8,128)S(1)}, u32[]{:S(2)}, u32[]{:S(2)}) %collective-permute-start.9) | collective-permute-done | bytes 3104 | tf_op jit(solution)/shard_map/ppermute | solution.py:295
  87.1 1.9 %collective-permute-done.8 = f32[2,6,64]{2,1,0:T(8,128)S(1)} collective-permute-done((f32[2,6,64]{2,1,0:T(8,128)S(1)}, f32[2,6,64]{2,1,0:T(8,128)S(1)}, u32[]{:S(2)}, u32[]{:S(2)}) %collective-permute-start.8) | collective-permute-done | bytes 3104 | tf_op jit(solution)/shard_map/ppermute | solution.py:295
  89.7 46.0 %gradient.1 = (f32[64,4,128]{2,1,0:T(4,128)}, f32[4,12,640]{2,1,0:T(8,128)}) custom-call(f32[4,128,128]{2,1,0:T(8,128)} %get-tuple-element.13.pt_ref, f32[96,8,128]{2,1,0:T(8,128)} %get-tuple-element.14.tin_ref, f32[12,640]{1,0:T(8,128)} %reshape.79.zg_ref, s32[64]{0:T(128)} %get-tuple-element.16.label_ref, s32[64]{0:T(128)} %get-tuple-element.17.count_ref), custom_call_target="tpu_custom_call" | custom-call | tf_op jit(solution)/shard_map/gradient/pallas_call | solution.py:399
  135.7 1.0 copy.14
  136.7 4.2 %collective-permute-done.10 = f32[4,6,640]{2,0,1:T(4,128)S(1)} collective-permute-done((f32[4,6,640]{2,0,1:T(4,128)S(1)}, f32[4,6,640]{2,0,1:T(4,128)S(1)}, u32[]{:S(2)}, u32[]{:S(2)}) %collective-permute-start.10) | collective-permute-done | bytes 61472 | tf_op jit(solution)/shard_map/ppermute | solution.py:295
  141.0 10.3 %collective-permute-start.12 = (f32[4,1,640]{2,0,1:T(4,128)S(1)}, f32[4,1,640]{2,0,1:T(4,128)S(1)}, u32[]{:S(2)}, u32[]{:S(2)}) collective-permute-start(f32[4,1,640]{2,0,1:T(4,128)S(1)} %get-tuple-element.33), channel_id=1, source_target_pairs={{0,4},{4,0},{8,12},{12,8},{1,5},{5,1},{9,13},{13,9},{2,6},{6,2},{1... | collective-permute-start | bytes 30728 | tf_op jit(solution)/shard_map/ppermute | solution.py:295
  151.3 0.8 collective-permute-done.12
  152.5 6.3 %all-to-all-start.1 = ((f32[64,4,128]{2,1,0:T(4,128)}), f32[64,4,128]{2,1,0:T(4,128)S(1)}, u32[]{:S(2)}, u32[]{:S(2)}) async-start(f32[64,4,128]{2,1,0:T(4,128)} %get-tuple-element.18), calls=%async_computation.1 | async-start | bytes 262144 | tf_op jit(solution)/shard_map/all_to_all | solution.py:416
  160.7 6.4 %all-to-all-done.1.reply_ref = f32[64,4,128]{2,1,0:T(4,128)S(1)} async-done(((f32[64,4,128]{2,1,0:T(4,128)}), f32[64,4,128]{2,1,0:T(4,128)S(1)}, u32[]{:S(2)}, u32[]{:S(2)}) %all-to-all-start.1) | async-done | bytes 131104 | tf_op jit(solution)/shard_map/all_to_all | solution.py:416
  167.7 1.6 pick.1
  (68 shorter events, 7.6 us)
Async XLA Ops:
  2.5 4.9 %collective-permute-start = (f32[4,4,512]{2,1,0:T(4,128)S(1)}, f32[4,4,512]{2,1,0:T(4,128)S(1)}, u32[]{:S(2)}, u32[]{:S(2)}) collective-permute-start(f32[4,4,512]{2,1,0:T(4,128)S(1)} %reshape.76), channel_id=1, source_target_pairs={{0,16},{16,0},{1,17},{17,1},{2,18},{18,2},{3,19},{19,3},{4,20},{20... | collective-permute-start | bytes 98312 | tf_op jit(solution)/shard_map/ppermute | solution.py:295
  7.4 2.3 %copy-start.2 = (f32[48,3,128]{2,0,1:T(8,128)S(1)}, f32[48,3,128]{2,0,1:T(8,128)}, u32[]{:S(2)}) copy-start(f32[48,3,128]{2,0,1:T(8,128)} %param.7) | copy-start | bytes 221188
  7.5 10.3 %collective-permute-start.2 = (f32[2,1,4,512]{3,2,1,0:T(4,128)S(1)}, f32[2,1,4,512]{3,2,1,0:T(4,128)S(1)}, u32[]{:S(2)}, u32[]{:S(2)}) collective-permute-start(f32[2,1,4,512]{3,2,1,0:T(4,128)S(1)} %broadcast_select_fusion.2), channel_id=1, source_target_pairs={{0,4},{4,0},{8,12},{12,8},{1,5},{5,1},{9,13},{13,9},{2,6},{6,2},{1... | collective-permute-start | bytes 49160 | tf_op jit(solution)/shard_map/ppermute | solution.py:295
  7.5 10.2 %collective-permute-start.1 = (f32[2,1,4,512]{3,2,1,0:T(4,128)S(1)}, f32[2,1,4,512]{3,2,1,0:T(4,128)S(1)}, u32[]{:S(2)}, u32[]{:S(2)}) collective-permute-start(f32[2,1,4,512]{3,2,1,0:T(4,128)S(1)} %get-tuple-element.25), channel_id=1, source_target_pairs={{4,8},{8,4},{0,12},{12,0},{5,9},{9,5},{1,13},{13,1},{6,10},{10,6},... | collective-permute-start | bytes 49160 | tf_op jit(solution)/shard_map/ppermute | solution.py:295
  12.7 14.1 %all-to-all-start = ((f32[64,1,640]{2,1,0:T(1,128)}), f32[64,1,640]{2,1,0:T(1,128)S(1)}, u32[]{:S(2)}, u32[]{:S(2)}) async-start(f32[64,1,640]{2,1,0:T(1,128)} %get-tuple-element.12), calls=%async_computation | async-start | bytes 327680 | tf_op jit(solution)/shard_map/all_to_all | solution.py:334
  17.9 7.9 %collective-permute-start.3 = (f32[12,4,32]{2,1,0:T(4,128)S(1)}, f32[12,4,32]{2,1,0:T(4,128)S(1)}, u32[]{:S(2)}, u32[]{:S(2)}) collective-permute-start(f32[12,4,32]{2,1,0:T(4,128)S(1)} %get-tuple-element.28), channel_id=1, source_target_pairs={{1,2},{2,1},{0,3},{3,0},{5,6},{6,5},{4,7},{7,4},{9,10},{10,9},{8,1... | collective-permute-start | bytes 18440 | tf_op jit(solution)/shard_map/ppermute | solution.py:295
  21.6 4.3 %collective-permute-start.4 = (f32[12,4,32]{2,1,0:T(4,128)S(1)}, f32[12,4,32]{2,1,0:T(4,128)S(1)}, u32[]{:S(2)}, u32[]{:S(2)}) collective-permute-start(f32[12,4,32]{2,1,0:T(4,128)S(1)} %get-tuple-element.29), channel_id=1, source_target_pairs={{0,1},{1,0},{2,3},{3,2},{4,5},{5,4},{6,7},{7,6},{8,9},{9,8},{10,11... | collective-permute-start | bytes 18440 | tf_op jit(solution)/shard_map/ppermute | solution.py:295
  26.8 0.7 copy-start
  69.6 4.1 %collective-permute-start.5 = (f32[2,6,640]{2,1,0:T(8,128)S(1)}, f32[2,6,640]{2,1,0:T(8,128)S(1)}, u32[]{:S(2)}, u32[]{:S(2)}) collective-permute-start(f32[2,6,640]{2,1,0:T(8,128)S(1)} %rev.3), channel_id=1, source_target_pairs={{0,16},{16,0},{1,17},{17,1},{2,18},{18,2},{3,19},{19,3},{4,20},{20... | collective-permute-start | bytes 92168 | tf_op jit(solution)/shard_map/ppermute | solution.py:295
  73.7 8.8 %collective-permute-start.6 = (f32[2,2,640]{2,1,0:T(2,128)S(1)}, f32[2,2,640]{2,1,0:T(2,128)S(1)}, u32[]{:S(2)}, u32[]{:S(2)}) collective-permute-start(f32[2,2,640]{2,1,0:T(2,128)S(1)} %get-tuple-element.43), channel_id=1, source_target_pairs={{4,8},{8,4},{0,12},{12,0},{5,9},{9,5},{1,13},{13,1},{6,10},{10,6},... | collective-permute-start | bytes 30728 | tf_op jit(solution)/shard_map/ppermute | solution.py:295
  73.8 9.5 %collective-permute-start.7 = (f32[2,2,640]{2,1,0:T(2,128)S(1)}, f32[2,2,640]{2,1,0:T(2,128)S(1)}, u32[]{:S(2)}, u32[]{:S(2)}) collective-permute-start(f32[2,2,640]{2,1,0:T(2,128)S(1)} %get-tuple-element.44), channel_id=1, source_target_pairs={{0,4},{4,0},{8,12},{12,8},{1,5},{5,1},{9,13},{13,9},{2,6},{6,2},{1... | collective-permute-start | bytes 30728 | tf_op jit(solution)/shard_map/ppermute | solution.py:295
  83.4 3.7 %collective-permute-start.9 = (f32[2,6,64]{2,1,0:T(8,128)S(1)}, f32[2,6,64]{2,1,0:T(8,128)S(1)}, u32[]{:S(2)}, u32[]{:S(2)}) collective-permute-start(f32[2,6,64]{2,1,0:T(8,128)S(1)} %broadcast_select_fusion.4), channel_id=1, source_target_pairs={{0,1},{1,0},{2,3},{3,2},{4,5},{5,4},{6,7},{7,6},{8,9},{9,8},{10,11... | collective-permute-start | bytes 9224 | tf_op jit(solution)/shard_map/ppermute | solution.py:295
  83.4 5.5 %collective-permute-start.8 = (f32[2,6,64]{2,1,0:T(8,128)S(1)}, f32[2,6,64]{2,1,0:T(8,128)S(1)}, u32[]{:S(2)}, u32[]{:S(2)}) collective-permute-start(f32[2,6,64]{2,1,0:T(8,128)S(1)} %get-tuple-element.22), channel_id=1, source_target_pairs={{1,2},{2,1},{0,3},{3,0},{5,6},{6,5},{4,7},{7,4},{9,10},{10,9},{8,1... | collective-permute-start | bytes 9224 | tf_op jit(solution)/shard_map/ppermute | solution.py:295
  136.6 4.3 %collective-permute-start.10 = (f32[4,6,640]{2,0,1:T(4,128)S(1)}, f32[4,6,640]{2,0,1:T(4,128)S(1)}, u32[]{:S(2)}, u32[]{:S(2)}) collective-permute-start(f32[4,6,640]{2,0,1:T(4,128)S(1)} %slice_bitcast_fusion), channel_id=1, source_target_pairs={{0,16},{16,0},{1,17},{17,1},{2,18},{18,2},{3,19},{19,3},{4,20},{20... | collective-permute-start | bytes 184328 | tf_op jit(solution)/shard_map/ppermute | solution.py:295
  141.0 10.4 %collective-permute-start.11 = (f32[4,1,640]{2,0,1:T(4,128)S(1)}, f32[4,1,640]{2,0,1:T(4,128)S(1)}, u32[]{:S(2)}, u32[]{:S(2)}) collective-permute-start(f32[4,1,640]{2,0,1:T(4,128)S(1)} %get-tuple-element.32), channel_id=1, source_target_pairs={{4,8},{8,4},{0,12},{12,0},{5,9},{9,5},{1,13},{13,1},{6,10},{10,6},... | collective-permute-start | bytes 30728 | tf_op jit(solution)/shard_map/ppermute | solution.py:295
  141.0 11.1 %collective-permute-start.12 = (f32[4,1,640]{2,0,1:T(4,128)S(1)}, f32[4,1,640]{2,0,1:T(4,128)S(1)}, u32[]{:S(2)}, u32[]{:S(2)}) collective-permute-start(f32[4,1,640]{2,0,1:T(4,128)S(1)} %get-tuple-element.33), channel_id=1, source_target_pairs={{0,4},{4,0},{8,12},{12,8},{1,5},{5,1},{9,13},{13,9},{2,6},{6,2},{1... | collective-permute-start | bytes 30728 | tf_op jit(solution)/shard_map/ppermute | solution.py:295
  152.3 6.6 %collective-permute-start.13 = (f32[4,4,32]{2,0,1:T(4,128)S(1)}, f32[4,4,32]{2,0,1:T(4,128)S(1)}, u32[]{:S(2)}, u32[]{:S(2)}) collective-permute-start(f32[4,4,32]{2,0,1:T(4,128)S(1)} %get-tuple-element.40), channel_id=1, source_target_pairs={{1,2},{2,1},{0,3},{3,0},{5,6},{6,5},{4,7},{7,4},{9,10},{10,9},{8,1... | collective-permute-start | bytes 6152 | tf_op jit(solution)/shard_map/ppermute | solution.py:295
  152.3 6.6 %collective-permute-start.14 = (f32[4,4,32]{2,0,1:T(4,128)S(1)}, f32[4,4,32]{2,0,1:T(4,128)S(1)}, u32[]{:S(2)}, u32[]{:S(2)}) collective-permute-start(f32[4,4,32]{2,0,1:T(4,128)S(1)} %get-tuple-element.41), channel_id=1, source_target_pairs={{0,1},{1,0},{2,3},{3,2},{4,5},{5,4},{6,7},{7,6},{8,9},{9,8},{10,11... | collective-permute-start | bytes 6152 | tf_op jit(solution)/shard_map/ppermute | solution.py:295
  152.5 14.6 %all-to-all-start.1 = ((f32[64,4,128]{2,1,0:T(4,128)}), f32[64,4,128]{2,1,0:T(4,128)S(1)}, u32[]{:S(2)}, u32[]{:S(2)}) async-start(f32[64,4,128]{2,1,0:T(4,128)} %get-tuple-element.18), calls=%async_computation.1 | async-start | bytes 262144 | tf_op jit(solution)/shard_map/all_to_all | solution.py:416
  159.2 0.7 copy-start.3
  167.1 0.6 copy-start.1

commit v2 on v1

v2 whole, which is shorter than its diff:
```python
import functools
import math

import jax
import jax.numpy as jnp
from jax import lax
from jax.experimental import pallas as pl
from jax.experimental.pallas import tpu as pltpu
from jax.sharding import PartitionSpec as P

MOST = 2
AXES = ("gx", "gy", "gz")
LANES = 128
SLOTS = 32

kernel_width = 0.05
cutoff_sq = 0.5
sharp = cutoff_sq / kernel_width
log2e = math.log2(math.e)
scale = math.sqrt(log2e / cutoff_sq)
gain = sharp * log2e
shift = math.log2(gain)
grad_unit = 2.0 / (gain * scale)

VMEM = pl.BlockSpec(memory_space=pltpu.VMEM)
SMEM = pl.BlockSpec(memory_space=pltpu.SMEM)


def div_rem(value, size):
    if size & (size - 1) == 0:
        return lax.shift_right_logical(value, size.bit_length() - 1), value & (size - 1)
    return lax.div(value, size), lax.rem(value, size)


def route_kernel(spans, sizes, cell_ref, count_ref, xyz_ref, wt_ref, out_ref, slot_ref, used_ref):
    blocks, _, pts = xyz_ref.shape
    bricks = sizes[0] * sizes[1] * sizes[2]
    lane = lax.broadcasted_iota(jnp.int32, (1, pts), 1)
    out_ref[:, :, : 4 * pts] = jnp.zeros((out_ref.shape[0], 1, 4 * pts), jnp.float32)
    out_ref[:, :, 4 * pts :] = jnp.full((out_ref.shape[0], 1, LANES), -1.0, jnp.float32)

    def clear(i, carry):
        used_ref[i] = 0
        return carry

    lax.fori_loop(0, bricks, clear, 0, unroll=8)

    def one(b, carry):
        rest, along_z = div_rem(cell_ref[b], spans[2] * sizes[2])
        along_x, along_y = div_rem(rest, spans[1] * sizes[1])
        brick_x, in_x = div_rem(along_x, spans[0])
        brick_y, in_y = div_rem(along_y, spans[1])
        brick_z, in_z = div_rem(along_z, spans[2])
        target = (brick_x * sizes[1] + brick_y) * sizes[2] + brick_z
        local = (in_x * spans[1] + in_y) * spans[2] + in_z
        before = used_ref[target]
        used_ref[target] = before + 1
        slot = target * MOST + before
        slot_ref[b] = slot
        count = count_ref[b]
        for f in range(3):
            out_ref[slot, :, f * pts : (f + 1) * pts] = xyz_ref[b, f : f + 1, :]
        out_ref[slot, :, 3 * pts : 4 * pts] = jnp.where(lane < count, wt_ref[pl.ds(b, 1), :], 0.0)
        head = lax.broadcasted_iota(jnp.int32, (1, LANES), 1)
        tag = jnp.where(head == 0, local, count)
        out_ref[slot, :, 4 * pts :] = tag.astype(jnp.float32)
        return carry

    lax.fori_loop(0, blocks, one, 0)


def lane_ids(shape):
    return lax.broadcasted_iota(jnp.int32, shape, len(shape) - 1)


def sub_ids(shape):
    return lax.broadcasted_iota(jnp.int32, shape, len(shape) - 2)


def bases_of(label, spans, rows, planes):
    in_y, in_z = div_rem(label, spans[2])
    cells = spans[2] + 2
    return [
        pl.multiple_of(((p * rows + in_y + dy) * cells + in_z) * SLOTS, SLOTS)
        for p in range(planes)
        for dy in range(3)
    ]


def spread(block, tables, base, height):
    columns = block.T
    for f, table in enumerate(tables):
        for t in range(height // 8):
            at = pl.ds(pl.multiple_of(base + 8 * t, 8), 8)
            table[at, :] = jnp.broadcast_to(columns[8 * t : 8 * t + 8, f : f + 1], (8, LANES))


def gather_sum(acc_ref, base, height):
    lane = lane_ids((8, LANES))
    sub = sub_ids((8, LANES))
    total = None
    for t in range(height // 8):
        at = pl.ds(pl.multiple_of(base + 8 * t, 8), 8)
        part = jnp.sum(acc_ref[at, :], axis=1, keepdims=True)
        part = jnp.where(lane == sub + 8 * t, part, 0.0)
        total = part if total is None else total + part
    return jnp.sum(total, axis=0, keepdims=True)


def fold8(value):
    return jnp.sum(value.reshape(value.shape[0] // 8, 8, value.shape[1]), axis=0)


def density_kernel(
    spans, planes, in_ref, gauss_ref, origin_ref,
    point_ref, zg_ref, label_ref, list_ref, used_ref,
    mx_ref, my_ref, mz_ref, ma_ref, acc_ref, line_ref,
):
    slots = in_ref.shape[0]
    pts = LANES
    rows = spans[1] + 2
    width = (spans[2] + 2) * SLOTS

    part = sub_ids((8, LANES))
    off = jnp.where(
        part == 0, origin_ref[0], jnp.where(part == 1, origin_ref[1], jnp.where(part == 2, origin_ref[2], 0.0))
    )
    mul = jnp.where(part < 3, scale, 1.0)
    for s in range(slots):
        label_ref[s] = in_ref[s, :, 4 * pts :].astype(jnp.int32)[0, 0]
        for f in range(4):
            point_ref[s, f : f + 1, :] = in_ref[s, :, f * pts : (f + 1) * pts]
        point_ref[s, 4:8, :] = jnp.ones((4, pts), jnp.float32)

    def order(s, n):
        list_ref[n] = s
        return n + (label_ref[s] >= 0).astype(jnp.int32)

    used = lax.fori_loop(0, slots, order, 0)
    used_ref[0] = used
    for s in range(slots):
        point_ref[s] = (point_ref[s] - off) * mul

    def table_row(r, carry):
        for c in range(-(-width // LANES)):
            height = min(LANES, width - c * LANES)
            block = jnp.concatenate(
                [gauss_ref[r, :, c * LANES : (c + 1) * LANES], jnp.zeros((4, LANES), jnp.float32)], axis=0
            )
            spread((block - off) * mul, (mx_ref, my_ref, mz_ref, ma_ref), r * width + c * LANES, height)
        return carry

    lax.fori_loop(0, planes * rows, table_row, 0)
    acc_ref[...] = jnp.zeros(acc_ref.shape, jnp.float32)

    def one(i, carry):
        slot = list_ref[i]
        x, y, z, w = (point_ref[slot, f : f + 1, :] for f in range(4))
        total = jnp.zeros((8, LANES), jnp.float32)
        for base in bases_of(label_ref[slot], spans, rows, planes):
            for c in range(3):
                at = pl.ds(pl.multiple_of(base + c * SLOTS, SLOTS), SLOTS)
                dx = x - mx_ref[at, :]
                dy = y - my_ref[at, :]
                dz = z - mz_ref[at, :]
                kern = jnp.exp2(jnp.exp2(shift - (dx * dx + dy * dy + dz * dz)))
                total = total + fold8(kern * ma_ref[at, :])
                acc_ref[at, :] += kern * w
        point_ref[slot, 4:5, :] = 1.0 + jnp.sum(total, axis=0, keepdims=True)
        return carry

    lax.fori_loop(0, used, one, 0)

    def sum_row(r, carry):
        for c in range(-(-width // LANES)):
            height = min(LANES, width - c * LANES)
            line_ref[0, r, :, c * LANES : (c + 1) * LANES] = gather_sum(
                acc_ref, r * width + c * LANES, height
            )
        return carry

    lax.fori_loop(0, planes * rows, sum_row, 0)
    for r in range(planes * rows):
        zg_ref[r : r + 1, :] = line_ref[0, r]


def gradient_kernel(
    spans, planes, point_ref, gauss_ref, zg_ref, origin_ref, label_ref, list_ref, used_ref,
    reply_ref, grad_ref,
    mx_ref, my_ref, mz_ref, ma_ref, mb_ref, ax_ref, ay_ref, az_ref, ad_ref, line_ref,
):
    rows = spans[1] + 2
    width = (spans[2] + 2) * SLOTS
    part = sub_ids((8, LANES))
    off = jnp.where(
        part == 0, origin_ref[0], jnp.where(part == 1, origin_ref[1], jnp.where(part == 2, origin_ref[2], 0.0))
    )
    mul = jnp.where(part < 3, scale, 1.0)

    for r in range(planes * rows):
        line_ref[0, r] = zg_ref[r : r + 1, :]

    def table_row(r, carry):
        for c in range(-(-width // LANES)):
            height = min(LANES, width - c * LANES)
            lanes = slice(c * LANES, (c + 1) * LANES)
            gauss = gauss_ref[r, :, lanes]
            last = gauss[3:4] / (1.0 + line_ref[0, r, :, lanes])
            block = jnp.concatenate([gauss, jnp.broadcast_to(last, (4, LANES))], axis=0)
            spread(
                (block - off) * mul,
                (mx_ref, my_ref, mz_ref, ma_ref, mb_ref),
                r * width + c * LANES,
                height,
            )
        return carry

    lax.fori_loop(0, planes * rows, table_row, 0)
    for ref in (ax_ref, ay_ref, az_ref, ad_ref):
        ref[...] = jnp.zeros(ref.shape, jnp.float32)

    def one(i, carry):
        slot = list_ref[i]
        x, y, z, w, zp = (point_ref[slot, f : f + 1, :] for f in range(5))
        ip = 1.0 / zp
        px = py = pz = jnp.zeros((8, LANES), jnp.float32)
        for base in bases_of(label_ref[slot], spans, rows, planes):
            for c in range(3):
                at = pl.ds(pl.multiple_of(base + c * SLOTS, SLOTS), SLOTS)
                dx = x - mx_ref[at, :]
                dy = y - my_ref[at, :]
                dz = z - mz_ref[at, :]
                fall = jnp.exp2(shift - (dx * dx + dy * dy + dz * dz))
                wk = jnp.exp2(fall) * w
                h = wk * fall * (ma_ref[at, :] * ip + mb_ref[at, :])
                dx = h * dx
                dy = h * dy
                dz = h * dz
                px = px + fold8(dx)
                py = py + fold8(dy)
                pz = pz + fold8(dz)
                ax_ref[at, :] += dx
                ay_ref[at, :] += dy
                az_ref[at, :] += dz
                ad_ref[at, :] += wk * ip
        loss = jnp.where(w > 0.0, kernel_width * sharp - kernel_width * jnp.log(zp), 0.0)
        reply_ref[slot, 0:1, :] = loss
        for f, v in enumerate((px, py, pz)):
            reply_ref[slot, f + 1 : f + 2, :] = jnp.sum(v, axis=0, keepdims=True) * grad_unit
        return carry

    lax.fori_loop(0, used_ref[0], one, 0)

    def sum_row(r, carry):
        for f, ref in enumerate((ax_ref, ay_ref, az_ref, ad_ref)):
            unit = -grad_unit if f < 3 else 1.0
            for c in range(-(-width // LANES)):
                height = min(LANES, width - c * LANES)
                line_ref[f, r, :, c * LANES : (c + 1) * LANES] = (
                    gather_sum(ref, r * width + c * LANES, height) * unit
                )
        return carry

    lax.fori_loop(0, planes * rows, sum_row, 0)
    for f in range(4):
        for r in range(planes * rows):
            grad_ref[f, r : r + 1, :] = line_ref[f, r]


def pick_kernel(slot_ref, reply_ref, out_ref):
    def one(b, carry):
        out_ref[b] = reply_ref[slot_ref[b]]
        return carry

    lax.fori_loop(0, out_ref.shape[0], one, 0, unroll=4)


def swap(value, axis, odd):
    count = lax.axis_size(axis)
    pairs = []
    for i in range(odd, count - 1, 2):
        pairs += [(i, i + 1), (i + 1, i)]
    if odd and count % 2 == 0 and count > 2:
        pairs += [(0, count - 1), (count - 1, 0)]
    return lax.ppermute(value, axis, pairs)


def trade(low, high, axis):
    count = lax.axis_size(axis)
    here = lax.axis_index(axis)
    even = here % 2 == 0
    first = swap(jnp.where(even, high, low), axis, 0)
    second = swap(jnp.where(even, low, high), axis, 1) if count > 2 else jnp.zeros_like(first)
    from_low = jnp.where(here > 0, jnp.where(even, second, first), 0.0)
    from_high = jnp.where(here < count - 1, jnp.where(even, first, second), 0.0)
    return from_low, from_high


def on_device(
    point_xyz, point_weight, block_cell, block_count, gauss_mean, gauss_opacity, gauss_count
):
    blocks, _, pts = point_xyz.shape
    span_x, span_y, span_z, _, slots = gauss_mean.shape
    spans = (span_x, span_y, span_z)
    sizes = tuple(lax.axis_size(a) for a in AXES)
    if span_x != 1 or slots != SLOTS or pts != LANES or span_y < 2 or span_z % 4:
        raise ValueError("unsupported brick")
    bricks = sizes[0] * sizes[1] * sizes[2]
    places = bricks * MOST
    f32 = jnp.float32

    outgoing, send_slot = pl.pallas_call(
        functools.partial(route_kernel, spans, sizes),
        out_shape=(
            jax.ShapeDtypeStruct((places, 1, 5 * pts), f32),
            jax.ShapeDtypeStruct((blocks,), jnp.int32),
        ),
        in_specs=[SMEM, SMEM, VMEM, VMEM],
        out_specs=(VMEM, SMEM),
        scratch_shapes=[pltpu.SMEM((bricks,), jnp.int32)],
        name="route",
    )(block_cell, block_count, point_xyz, point_weight)
    incoming = lax.all_to_all(outgoing, AXES, split_axis=0, concat_axis=0, tiled=True)

    present = jnp.arange(slots, dtype=jnp.int32) < gauss_count[..., None]
    own = jnp.concatenate([gauss_mean, jnp.where(present, gauss_opacity, 0.0)[..., None, :]], axis=3)
    own = own[0].transpose(0, 2, 1, 3).reshape(span_y, 4, span_z * slots)
    if sizes[0] == 2:
        stack = jnp.stack([own, swap(own, "gx", 0)])
    else:
        stack = jnp.stack([own, *trade(own, own, "gx")])
    planes = stack.shape[0]
    rows = span_y + 2
    low, high = trade(stack[:, :1], stack[:, -1:], "gy")
    stack = jnp.concatenate([low, stack, high], axis=1).reshape(planes * rows, 4, span_z * slots)
    low, high = trade(stack[..., :slots], stack[..., -slots:], "gz")
    width = (span_z + 2) * slots
    wide = -(-width // LANES) * LANES
    stack = jnp.concatenate(
        [low, stack, high, jnp.zeros((planes * rows, 4, wide - width), f32)], axis=2
    )
    origin = jnp.stack([lax.axis_index(a) * s for a, s in zip(AXES, spans)]).astype(f32)

    table = pltpu.VMEM((planes * rows * width, LANES), f32)
    points, zg_part, label, order, used = pl.pallas_call(
        functools.partial(density_kernel, spans, planes),
        out_shape=(
            jax.ShapeDtypeStruct((places, 8, LANES), f32),
            jax.ShapeDtypeStruct((planes * rows, wide), f32),
            jax.ShapeDtypeStruct((places,), jnp.int32),
            jax.ShapeDtypeStruct((places + 1,), jnp.int32),
            jax.ShapeDtypeStruct((1,), jnp.int32),
        ),
        in_specs=[VMEM, VMEM, SMEM],
        out_specs=(VMEM, VMEM, SMEM, SMEM, SMEM),
        scratch_shapes=[table] * 5 + [pltpu.VMEM((1, planes * rows, 1, wide), f32)],
        name="density",
    )(incoming, stack, origin)

    part = zg_part.reshape(planes, rows, wide)
    if sizes[0] == 2:
        part = part + swap(part[::-1], "gx", 0)
    else:
        low, high = trade(part[1], part[2], "gx")
        whole = part[0] + low + high
        part = jnp.stack([whole, *trade(whole, whole, "gx")])
    low, high = trade(part[:, :2], part[:, -2:], "gy")
    part = jnp.concatenate([part[:, :2] + low, part[:, 2:-2], part[:, -2:] + high], axis=1)
    edge = 2 * slots
    low, high = trade(part[..., :edge], part[..., width - edge : width], "gz")
    part = jnp.concatenate(
        [
            part[..., :edge] + low,
            part[..., edge : width - edge],
            part[..., width - edge : width] + high,
            jnp.zeros((planes, rows, wide - width), f32),
        ],
        axis=2,
    )
    zg_sum = part.reshape(planes * rows, wide)

    reply, grad_part = pl.pallas_call(
        functools.partial(gradient_kernel, spans, planes),
        out_shape=(
            jax.ShapeDtypeStruct((places, 4, LANES), f32),
            jax.ShapeDtypeStruct((4, planes * rows, wide), f32),
        ),
        in_specs=[VMEM, VMEM, VMEM, SMEM, SMEM, SMEM, SMEM],
        out_specs=(VMEM, VMEM),
        scratch_shapes=[table] * 9 + [pltpu.VMEM((4, planes * rows, 1, wide), f32)],
        name="gradient",
    )(points, stack, zg_sum, origin, label, order, used)

    answer = lax.all_to_all(reply, AXES, split_axis=0, concat_axis=0, tiled=True)
    point_out = pl.pallas_call(
        pick_kernel,
        out_shape=jax.ShapeDtypeStruct((blocks, 4, pts), f32),
        in_specs=[SMEM, VMEM],
        out_specs=VMEM,
        name="pick",
    )(send_slot, answer)

    grad = grad_part.reshape(4, planes, rows, wide)
    if sizes[0] == 2:
        grad = grad[:, 0] + swap(grad[:, 1], "gx", 0)
    else:
        low, high = trade(grad[:, 1], grad[:, 2], "gx")
        grad = grad[:, 0] + low + high
    low, high = trade(grad[:, :1], grad[:, -1:], "gy")
    grad = jnp.concatenate(
        [grad[:, 1:2] + low, grad[:, 2:-2], grad[:, -2:-1] + high], axis=1
    )
    low, high = trade(grad[..., :slots], grad[..., width - slots : width], "gz")
    grad = jnp.concatenate(
        [
            grad[..., slots : 2 * slots] + low,
            grad[..., 2 * slots : width - 2 * slots],
            grad[..., width - 2 * slots : width - slots] + high,
        ],
        axis=2,
    )
    grad = grad.reshape(4, span_y, span_z, slots).transpose(1, 2, 0, 3)[None]
    total_g = 1.0 + part[0, 1:-1, slots : width - slots].reshape(1, span_y, span_z, slots)
    opacity = jnp.where(
        present,
        kernel_width * sharp - kernel_width * jnp.log(total_g) - kernel_width * grad[..., 3, :],
        0.0,
    )
    gauss_grad = jnp.concatenate([grad[..., :3, :], opacity[..., None, :]], axis=3)
    return point_out, gauss_grad


def solution(mesh):
    return jax.shard_map(
        on_device,
        mesh=mesh,
        in_specs=(
            P(AXES, None, None),
            P(AXES, None),
            P(AXES),
            P(AXES),
            P("gx", "gy", "gz", None, None),
            P("gx", "gy", "gz", None),
            P("gx", "gy", "gz"),
        ),
        out_specs=(P(AXES, None, None), P("gx", "gy", "gz", None, None)),
        check_vma=False,
    )
```

time: 169 us -> 122 us (0.72)
  Pallas kernels: 91.3 us -> 51.8 us
  starting transfers between devices: 39.7 us -> 34 us
  waiting for transfers between devices: 27.1 us -> 24.1 us
    pallas_call x1, Pallas kernels: 41.4 us -> 18.4 us  [on_device(): pl.pallas_call(functools.partial(density_kernel, spans, planes), out_shap...]
    pallas_call x1, Pallas kernels: 46 us -> 29.4 us  [on_device(): pl.pallas_call(functools.partial(gradient_kernel, spans, planes), out_sha...]
    ppermute x15, starting transfers between devices: 28.4 us -> 22.7 us  [swap(): return lax.ppermute(value, axis, pairs)]
    ppermute x15, waiting for transfers between devices: 20.5 us -> 17.6 us  [swap(): return lax.ppermute(value, axis, pairs)]
  transfers between devices with their start and end apart: 17 -> 17, of which waited for: 10 -> 10; matrix products, arithmetic and copies ran while one was open for 2% -> 3% of each run, Pallas kernels for 1% -> 2%
where the time goes in v2:
time: 122 us; the launch traced here: 121 us
  Pallas kernels  51.8 us (42%)
  starting transfers between devices  34 us (28%)
  waiting for transfers between devices  24.1 us (20%)
  local copies, waits for them, and re-layouts  6.38 us (5%)
  other arithmetic  3.98 us (3%)
    pallas_call x1, Pallas kernels, on_device(): pl.pallas_call(functools.partial(gradient_kernel, spans, planes), out_sha...  29.4 us
    ppermute x15, starting transfers between devices, swap(): return lax.ppermute(value, axis, pairs)  22.7 us
    pallas_call x1, Pallas kernels, on_device(): pl.pallas_call(functools.partial(density_kernel, spans, planes), out_shap...  18.4 us
    ppermute x15, waiting for transfers between devices, swap(): return lax.ppermute(value, axis, pairs)  17.6 us
    all_to_all x1, waiting for transfers between devices, on_device(): lax.all_to_all(reply, AXES, split_axis=0, concat_axis=0, tiled=True)  6.39 us
    all_to_all x1, starting transfers between devices, on_device(): lax.all_to_all(reply, AXES, split_axis=0, concat_axis=0, tiled=True)  6.27 us
    all_to_all x1, starting transfers between devices, on_device(): lax.all_to_all(outgoing, AXES, split_axis=0, concat_axis=0, tiled=True)  5.01 us
    unnamed x10, local copies, waits for them, and re-layouts  3.4 us
  transfers between devices with their start and end apart: 17, of which 10 were waited for; matrix products, arithmetic and copies ran while one was open for 3% of the time, Pallas kernels for 2%

profile of v2, /device:TPU:0, one launch (start us, length us, event | category | flops | bytes accessed | tf_op | source)
XLA Modules:
  0.0 121.2 jit_solution(13177638033150234512)
XLA Ops:
  2.5 3.0 %collective-permute-start = (f32[4,4,512]{2,1,0:T(4,128)S(1)}, f32[4,4,512]{2,1,0:T(4,128)S(1)}, u32[]{:S(2)}, u32[]{:S(2)}) collective-permute-start(f32[4,4,512]{2,1,0:T(4,128)S(1)} %reshape.76), channel_id=1, source_target_pairs={{0,16},{16,0},{1,17},{17,1},{2,18},{18,2},{3,19},{19,3},{4,20},{20... | collective-permute-start | bytes 98312 | tf_op jit(solution)/shard_map/ppermute | solution.py:285
  5.7 1.8 %collective-permute-done = f32[4,4,512]{2,1,0:T(4,128)S(1)} collective-permute-done((f32[4,4,512]{2,1,0:T(4,128)S(1)}, f32[4,4,512]{2,1,0:T(4,128)S(1)}, u32[]{:S(2)}, u32[]{:S(2)}) %collective-permute-start) | collective-permute-done | bytes 32800 | tf_op jit(solution)/shard_map/ppermute | solution.py:285
  7.5 2.1 %collective-permute-start.1 = (f32[2,1,4,512]{3,2,1,0:T(4,128)S(1)}, f32[2,1,4,512]{3,2,1,0:T(4,128)S(1)}, u32[]{:S(2)}, u32[]{:S(2)}) collective-permute-start(f32[2,1,4,512]{3,2,1,0:T(4,128)S(1)} %get-tuple-element.25), channel_id=1, source_target_pairs={{4,8},{8,4},{0,12},{12,0},{5,9},{9,5},{1,13},{13,1},{6,10},{10,6},... | collective-permute-start | bytes 49160 | tf_op jit(solution)/shard_map/ppermute | solution.py:285
  10.4 2.3 %route.1 = (f32[64,1,640]{2,1,0:T(1,128)}, s32[48]{0:T(128)}) custom-call(s32[48]{0:T(128)} %cell_ref.1, s32[48]{0:T(128)} %count_ref.1, f32[48,3,128]{2,1,0:T(4,128)} %copy.12.xyz_ref, f32[48,128]{1,0:T(8,128)} %wt_ref.1), custom_call_target="tpu_custom_call" | custom-call | tf_op jit(solution)/shard_map/route/pallas_call | solution.py:312
  12.7 5.0 %all-to-all-start = ((f32[64,1,640]{2,1,0:T(1,128)}), f32[64,1,640]{2,1,0:T(1,128)S(1)}, u32[]{:S(2)}, u32[]{:S(2)}) async-start(f32[64,1,640]{2,1,0:T(1,128)} %get-tuple-element.12), calls=%async_computation | async-start | bytes 327680 | tf_op jit(solution)/shard_map/all_to_all | solution.py:323
  17.9 3.7 %collective-permute-start.3 = (f32[12,4,32]{2,1,0:T(4,128)S(1)}, f32[12,4,32]{2,1,0:T(4,128)S(1)}, u32[]{:S(2)}, u32[]{:S(2)}) collective-permute-start(f32[12,4,32]{2,1,0:T(4,128)S(1)} %get-tuple-element.28), channel_id=1, source_target_pairs={{1,2},{2,1},{0,3},{3,0},{5,6},{6,5},{4,7},{7,4},{9,10},{10,9},{8,1... | collective-permute-start | bytes 18440 | tf_op jit(solution)/shard_map/ppermute | solution.py:285
  22.3 3.6 %collective-permute-done.3 = f32[12,4,32]{2,1,0:T(4,128)S(1)} collective-permute-done((f32[12,4,32]{2,1,0:T(4,128)S(1)}, f32[12,4,32]{2,1,0:T(4,128)S(1)}, u32[]{:S(2)}, u32[]{:S(2)}) %collective-permute-start.3) | collective-permute-done | bytes 6176 | tf_op jit(solution)/shard_map/ppermute | solution.py:285
  27.5 18.4 %density.1 = (f32[64,8,128]{2,1,0:T(8,128)}, f32[12,640]{1,0:T(8,128)}, s32[64]{0:T(128)}, s32[65]{0:T(128)}, s32[1]{0:T(128)}) custom-call(f32[64,1,640]{2,1,0:T(1,128)} %copy-done, f32[12,4,640]{2,1,0:T(4,128)} %maximum_maximum_fusion.gauss_ref, f32[3]{0:T(128)} %add_convert_fusion.origin_ref), custom_call_target="tpu_custom_call" | custom-call | tf_op jit(solution)/shard_map/density/pallas_call | solution.py:345
  46.7 1.7 %collective-permute-start.5 = (f32[2,6,640]{2,1,0:T(8,128)S(1)}, f32[2,6,640]{2,1,0:T(8,128)S(1)}, u32[]{:S(2)}, u32[]{:S(2)}) collective-permute-start(f32[2,6,640]{2,1,0:T(8,128)S(1)} %rev.3), channel_id=1, source_target_pairs={{0,16},{16,0},{1,17},{17,1},{2,18},{18,2},{3,19},{19,3},{4,20},{20... | collective-permute-start | bytes 92168 | tf_op jit(solution)/shard_map/ppermute | solution.py:285
  48.5 2.3 %collective-permute-done.5 = f32[2,6,640]{2,1,0:T(8,128)S(1)} collective-permute-done((f32[2,6,640]{2,1,0:T(8,128)S(1)}, f32[2,6,640]{2,1,0:T(8,128)S(1)}, u32[]{:S(2)}, u32[]{:S(2)}) %collective-permute-start.5) | collective-permute-done | bytes 30752 | tf_op jit(solution)/shard_map/ppermute | solution.py:285
  50.9 1.5 %collective-permute-start.7 = (f32[2,2,640]{2,1,0:T(2,128)S(1)}, f32[2,2,640]{2,1,0:T(2,128)S(1)}, u32[]{:S(2)}, u32[]{:S(2)}) collective-permute-start(f32[2,2,640]{2,1,0:T(2,128)S(1)} %get-tuple-element.44), channel_id=1, source_target_pairs={{0,4},{4,0},{8,12},{12,8},{1,5},{5,1},{9,13},{13,9},{2,6},{6,2},{1... | collective-permute-start | bytes 30728 | tf_op jit(solution)/shard_map/ppermute | solution.py:285
  52.4 1.6 %collective-permute-done.6 = f32[2,2,640]{2,1,0:T(2,128)S(1)} collective-permute-done((f32[2,2,640]{2,1,0:T(2,128)S(1)}, f32[2,2,640]{2,1,0:T(2,128)S(1)}, u32[]{:S(2)}, u32[]{:S(2)}) %collective-permute-start.6) | collective-permute-done | bytes 10272 | tf_op jit(solution)/shard_map/ppermute | solution.py:285
  54.1 2.3 %collective-permute-start.9 = (f32[2,6,64]{2,1,0:T(8,128)S(1)}, f32[2,6,64]{2,1,0:T(8,128)S(1)}, u32[]{:S(2)}, u32[]{:S(2)}) collective-permute-start(f32[2,6,64]{2,1,0:T(8,128)S(1)} %broadcast_select_fusion.4), channel_id=1, source_target_pairs={{0,1},{1,0},{2,3},{3,2},{4,5},{5,4},{6,7},{7,6},{8,9},{9,8},{10,11... | collective-permute-start | bytes 9224 | tf_op jit(solution)/shard_map/ppermute | solution.py:285
  56.7 1.4 %collective-permute-done.9 = f32[2,6,64]{2,1,0:T(8,128)S(1)} collective-permute-done((f32[2,6,64]{2,1,0:T(8,128)S(1)}, f32[2,6,64]{2,1,0:T(8,128)S(1)}, u32[]{:S(2)}, u32[]{:S(2)}) %collective-permute-start.9) | collective-permute-done | bytes 3104 | tf_op jit(solution)/shard_map/ppermute | solution.py:285
  58.0 3.8 %collective-permute-done.8 = f32[2,6,64]{2,1,0:T(8,128)S(1)} collective-permute-done((f32[2,6,64]{2,1,0:T(8,128)S(1)}, f32[2,6,64]{2,1,0:T(8,128)S(1)}, u32[]{:S(2)}, u32[]{:S(2)}) %collective-permute-start.8) | collective-permute-done | bytes 3104 | tf_op jit(solution)/shard_map/ppermute | solution.py:285
  62.6 29.4 %gradient.1 = (f32[64,4,128]{2,1,0:T(4,128)}, f32[4,12,640]{2,1,0:T(8,128)}) custom-call(f32[64,8,128]{2,1,0:T(8,128)} %get-tuple-element.13.point_ref, f32[12,4,640]{2,1,0:T(4,128)} %maximum_maximum_fusion.gauss_ref, f32[12,640]{1,0:T(8,128)} %reshape.79.zg_ref, f32[3]{0:T(128)} %add_convert_fusion.origin_ref, s32[64]{0:T(128)} %get-tuple-element.15.label_ref, ...), custom_call_target="tpu_custom_call" | custom-call | tf_op jit(solution)/shard_map/gradient/pallas_call | solution.py:382
  92.0 1.0 copy.14
  93.0 2.7 %collective-permute-start.10 = (f32[4,6,640]{2,0,1:T(4,128)S(1)}, f32[4,6,640]{2,0,1:T(4,128)S(1)}, u32[]{:S(2)}, u32[]{:S(2)}) collective-permute-start(f32[4,6,640]{2,0,1:T(4,128)S(1)} %slice_bitcast_fusion), channel_id=1, source_target_pairs={{0,16},{16,0},{1,17},{17,1},{2,18},{18,2},{3,19},{19,3},{4,20},{20... | collective-permute-start | bytes 184328 | tf_op jit(solution)/shard_map/ppermute | solution.py:285
  95.6 2.2 %collective-permute-done.10 = f32[4,6,640]{2,0,1:T(4,128)S(1)} collective-permute-done((f32[4,6,640]{2,0,1:T(4,128)S(1)}, f32[4,6,640]{2,0,1:T(4,128)S(1)}, u32[]{:S(2)}, u32[]{:S(2)}) %collective-permute-start.10) | collective-permute-done | bytes 61472 | tf_op jit(solution)/shard_map/ppermute | solution.py:285
  97.9 2.3 %collective-permute-start.12 = (f32[4,1,640]{2,0,1:T(4,128)S(1)}, f32[4,1,640]{2,0,1:T(4,128)S(1)}, u32[]{:S(2)}, u32[]{:S(2)}) collective-permute-start(f32[4,1,640]{2,0,1:T(4,128)S(1)} %get-tuple-element.33), channel_id=1, source_target_pairs={{0,4},{4,0},{8,12},{12,8},{1,5},{5,1},{9,13},{13,9},{2,6},{6,2},{1... | collective-permute-start | bytes 30728 | tf_op jit(solution)/shard_map/ppermute | solution.py:285
  101.2 2.9 %collective-permute-start.14 = (f32[4,4,32]{2,0,1:T(4,128)S(1)}, f32[4,4,32]{2,0,1:T(4,128)S(1)}, u32[]{:S(2)}, u32[]{:S(2)}) collective-permute-start(f32[4,4,32]{2,0,1:T(4,128)S(1)} %get-tuple-element.41), channel_id=1, source_target_pairs={{0,1},{1,0},{2,3},{3,2},{4,5},{5,4},{6,7},{7,6},{8,9},{9,8},{10,11... | collective-permute-start | bytes 6152 | tf_op jit(solution)/shard_map/ppermute | solution.py:285
  104.2 6.3 %all-to-all-start.1 = ((f32[64,4,128]{2,1,0:T(4,128)}), f32[64,4,128]{2,1,0:T(4,128)S(1)}, u32[]{:S(2)}, u32[]{:S(2)}) async-start(f32[64,4,128]{2,1,0:T(4,128)} %get-tuple-element.18), calls=%async_computation.1 | async-start | bytes 262144 | tf_op jit(solution)/shard_map/all_to_all | solution.py:394
  112.5 6.4 %all-to-all-done.1.reply_ref = f32[64,4,128]{2,1,0:T(4,128)S(1)} async-done(((f32[64,4,128]{2,1,0:T(4,128)}), f32[64,4,128]{2,1,0:T(4,128)S(1)}, u32[]{:S(2)}, u32[]{:S(2)}) %all-to-all-start.1) | async-done | bytes 131104 | tf_op jit(solution)/shard_map/all_to_all | solution.py:394
  119.5 1.6 %pick.1 = f32[48,4,128]{2,1,0:T(4,128)} custom-call(s32[48]{0:T(128)} %get-tuple-element.11.slot_ref, f32[64,4,128]{2,1,0:T(4,128)} %copy-done.1), custom_call_target="tpu_custom_call" | custom-call | tf_op jit(solution)/shard_map/pick/pallas_call | solution.py:395
  (68 shorter events, 10.9 us)
Async XLA Ops:
  2.5 4.9 %collective-permute-start = (f32[4,4,512]{2,1,0:T(4,128)S(1)}, f32[4,4,512]{2,1,0:T(4,128)S(1)}, u32[]{:S(2)}, u32[]{:S(2)}) collective-permute-start(f32[4,4,512]{2,1,0:T(4,128)S(1)} %reshape.76), channel_id=1, source_target_pairs={{0,16},{16,0},{1,17},{17,1},{2,18},{18,2},{3,19},{19,3},{4,20},{20... | collective-permute-start | bytes 98312 | tf_op jit(solution)/shard_map/ppermute | solution.py:285
  7.4 2.3 %copy-start.2 = (f32[48,3,128]{2,0,1:T(8,128)S(1)}, f32[48,3,128]{2,0,1:T(8,128)}, u32[]{:S(2)}) copy-start(f32[48,3,128]{2,0,1:T(8,128)} %param.7) | copy-start | bytes 221188
  7.5 10.3 %collective-permute-start.2 = (f32[2,1,4,512]{3,2,1,0:T(4,128)S(1)}, f32[2,1,4,512]{3,2,1,0:T(4,128)S(1)}, u32[]{:S(2)}, u32[]{:S(2)}) collective-permute-start(f32[2,1,4,512]{3,2,1,0:T(4,128)S(1)} %broadcast_select_fusion.2), channel_id=1, source_target_pairs={{0,4},{4,0},{8,12},{12,8},{1,5},{5,1},{9,13},{13,9},{2,6},{6,2},{1... | collective-permute-start | bytes 49160 | tf_op jit(solution)/shard_map/ppermute | solution.py:285
  7.5 10.2 %collective-permute-start.1 = (f32[2,1,4,512]{3,2,1,0:T(4,128)S(1)}, f32[2,1,4,512]{3,2,1,0:T(4,128)S(1)}, u32[]{:S(2)}, u32[]{:S(2)}) collective-permute-start(f32[2,1,4,512]{3,2,1,0:T(4,128)S(1)} %get-tuple-element.25), channel_id=1, source_target_pairs={{4,8},{8,4},{0,12},{12,0},{5,9},{9,5},{1,13},{13,1},{6,10},{10,6},... | collective-permute-start | bytes 49160 | tf_op jit(solution)/shard_map/ppermute | solution.py:285
  12.7 14.1 %all-to-all-start = ((f32[64,1,640]{2,1,0:T(1,128)}), f32[64,1,640]{2,1,0:T(1,128)S(1)}, u32[]{:S(2)}, u32[]{:S(2)}) async-start(f32[64,1,640]{2,1,0:T(1,128)} %get-tuple-element.12), calls=%async_computation | async-start | bytes 327680 | tf_op jit(solution)/shard_map/all_to_all | solution.py:323
  17.9 7.9 %collective-permute-start.3 = (f32[12,4,32]{2,1,0:T(4,128)S(1)}, f32[12,4,32]{2,1,0:T(4,128)S(1)}, u32[]{:S(2)}, u32[]{:S(2)}) collective-permute-start(f32[12,4,32]{2,1,0:T(4,128)S(1)} %get-tuple-element.28), channel_id=1, source_target_pairs={{1,2},{2,1},{0,3},{3,0},{5,6},{6,5},{4,7},{7,4},{9,10},{10,9},{8,1... | collective-permute-start | bytes 18440 | tf_op jit(solution)/shard_map/ppermute | solution.py:285
  21.6 4.3 %collective-permute-start.4 = (f32[12,4,32]{2,1,0:T(4,128)S(1)}, f32[12,4,32]{2,1,0:T(4,128)S(1)}, u32[]{:S(2)}, u32[]{:S(2)}) collective-permute-start(f32[12,4,32]{2,1,0:T(4,128)S(1)} %get-tuple-element.29), channel_id=1, source_target_pairs={{0,1},{1,0},{2,3},{3,2},{4,5},{5,4},{6,7},{7,6},{8,9},{9,8},{10,11... | collective-permute-start | bytes 18440 | tf_op jit(solution)/shard_map/ppermute | solution.py:285
  26.8 0.7 copy-start
  46.7 4.1 %collective-permute-start.5 = (f32[2,6,640]{2,1,0:T(8,128)S(1)}, f32[2,6,640]{2,1,0:T(8,128)S(1)}, u32[]{:S(2)}, u32[]{:S(2)}) collective-permute-start(f32[2,6,640]{2,1,0:T(8,128)S(1)} %rev.3), channel_id=1, source_target_pairs={{0,16},{16,0},{1,17},{17,1},{2,18},{18,2},{3,19},{19,3},{4,20},{20... | collective-permute-start | bytes 92168 | tf_op jit(solution)/shard_map/ppermute | solution.py:285
  50.8 3.2 %collective-permute-start.6 = (f32[2,2,640]{2,1,0:T(2,128)S(1)}, f32[2,2,640]{2,1,0:T(2,128)S(1)}, u32[]{:S(2)}, u32[]{:S(2)}) collective-permute-start(f32[2,2,640]{2,1,0:T(2,128)S(1)} %get-tuple-element.43), channel_id=1, source_target_pairs={{4,8},{8,4},{0,12},{12,0},{5,9},{9,5},{1,13},{13,1},{6,10},{10,6},... | collective-permute-start | bytes 30728 | tf_op jit(solution)/shard_map/ppermute | solution.py:285
  50.9 3.1 %collective-permute-start.7 = (f32[2,2,640]{2,1,0:T(2,128)S(1)}, f32[2,2,640]{2,1,0:T(2,128)S(1)}, u32[]{:S(2)}, u32[]{:S(2)}) collective-permute-start(f32[2,2,640]{2,1,0:T(2,128)S(1)} %get-tuple-element.44), channel_id=1, source_target_pairs={{0,4},{4,0},{8,12},{12,8},{1,5},{5,1},{9,13},{13,9},{2,6},{6,2},{1... | collective-permute-start | bytes 30728 | tf_op jit(solution)/shard_map/ppermute | solution.py:285
  54.1 4.0 %collective-permute-start.9 = (f32[2,6,64]{2,1,0:T(8,128)S(1)}, f32[2,6,64]{2,1,0:T(8,128)S(1)}, u32[]{:S(2)}, u32[]{:S(2)}) collective-permute-start(f32[2,6,64]{2,1,0:T(8,128)S(1)} %broadcast_select_fusion.4), channel_id=1, source_target_pairs={{0,1},{1,0},{2,3},{3,2},{4,5},{5,4},{6,7},{7,6},{8,9},{9,8},{10,11... | collective-permute-start | bytes 9224 | tf_op jit(solution)/shard_map/ppermute | solution.py:285
  56.4 5.4 %collective-permute-start.8 = (f32[2,6,64]{2,1,0:T(8,128)S(1)}, f32[2,6,64]{2,1,0:T(8,128)S(1)}, u32[]{:S(2)}, u32[]{:S(2)}) collective-permute-start(f32[2,6,64]{2,1,0:T(8,128)S(1)} %get-tuple-element.22), channel_id=1, source_target_pairs={{1,2},{2,1},{0,3},{3,0},{5,6},{6,5},{4,7},{7,4},{9,10},{10,9},{8,1... | collective-permute-start | bytes 9224 | tf_op jit(solution)/shard_map/ppermute | solution.py:285
  93.0 4.9 %collective-permute-start.10 = (f32[4,6,640]{2,0,1:T(4,128)S(1)}, f32[4,6,640]{2,0,1:T(4,128)S(1)}, u32[]{:S(2)}, u32[]{:S(2)}) collective-permute-start(f32[4,6,640]{2,0,1:T(4,128)S(1)} %slice_bitcast_fusion), channel_id=1, source_target_pairs={{0,16},{16,0},{1,17},{17,1},{2,18},{18,2},{3,19},{19,3},{4,20},{20... | collective-permute-start | bytes 184328 | tf_op jit(solution)/shard_map/ppermute | solution.py:285
  97.9 3.2 %collective-permute-start.11 = (f32[4,1,640]{2,0,1:T(4,128)S(1)}, f32[4,1,640]{2,0,1:T(4,128)S(1)}, u32[]{:S(2)}, u32[]{:S(2)}) collective-permute-start(f32[4,1,640]{2,0,1:T(4,128)S(1)} %get-tuple-element.32), channel_id=1, source_target_pairs={{4,8},{8,4},{0,12},{12,0},{5,9},{9,5},{1,13},{13,1},{6,10},{10,6},... | collective-permute-start | bytes 30728 | tf_op jit(solution)/shard_map/ppermute | solution.py:285
  97.9 3.1 %collective-permute-start.12 = (f32[4,1,640]{2,0,1:T(4,128)S(1)}, f32[4,1,640]{2,0,1:T(4,128)S(1)}, u32[]{:S(2)}, u32[]{:S(2)}) collective-permute-start(f32[4,1,640]{2,0,1:T(4,128)S(1)} %get-tuple-element.33), channel_id=1, source_target_pairs={{0,4},{4,0},{8,12},{12,8},{1,5},{5,1},{9,13},{13,9},{2,6},{6,2},{1... | collective-permute-start | bytes 30728 | tf_op jit(solution)/shard_map/ppermute | solution.py:285
  101.1 9.5 %collective-permute-start.13 = (f32[4,4,32]{2,0,1:T(4,128)S(1)}, f32[4,4,32]{2,0,1:T(4,128)S(1)}, u32[]{:S(2)}, u32[]{:S(2)}) collective-permute-start(f32[4,4,32]{2,0,1:T(4,128)S(1)} %get-tuple-element.40), channel_id=1, source_target_pairs={{1,2},{2,1},{0,3},{3,0},{5,6},{6,5},{4,7},{7,4},{9,10},{10,9},{8,1... | collective-permute-start | bytes 6152 | tf_op jit(solution)/shard_map/ppermute | solution.py:285
  101.2 9.4 %collective-permute-start.14 = (f32[4,4,32]{2,0,1:T(4,128)S(1)}, f32[4,4,32]{2,0,1:T(4,128)S(1)}, u32[]{:S(2)}, u32[]{:S(2)}) collective-permute-start(f32[4,4,32]{2,0,1:T(4,128)S(1)} %get-tuple-element.41), channel_id=1, source_target_pairs={{0,1},{1,0},{2,3},{3,2},{4,5},{5,4},{6,7},{7,6},{8,9},{9,8},{10,11... | collective-permute-start | bytes 6152 | tf_op jit(solution)/shard_map/ppermute | solution.py:285
  104.2 14.7 %all-to-all-start.1 = ((f32[64,4,128]{2,1,0:T(4,128)}), f32[64,4,128]{2,1,0:T(4,128)S(1)}, u32[]{:S(2)}, u32[]{:S(2)}) async-start(f32[64,4,128]{2,1,0:T(4,128)} %get-tuple-element.18), calls=%async_computation.1 | async-start | bytes 262144 | tf_op jit(solution)/shard_map/all_to_all | solution.py:394
  111.0 0.7 copy-start.3
  118.9 0.6 copy-start.1

commit v3 on v2

v3 whole, which is shorter than its diff:
```python
import functools
import math

import jax
import jax.numpy as jnp
from jax import lax
from jax.experimental import pallas as pl
from jax.experimental.pallas import tpu as pltpu
from jax.sharding import PartitionSpec as P


MOST = 2
AXES = ("gx", "gy", "gz")
LANES = 128
SLOTS = 32

kernel_width = 0.05
cutoff_sq = 0.5
sharp = cutoff_sq / kernel_width
log2e = math.log2(math.e)
scale = math.sqrt(log2e / cutoff_sq)
gain = sharp * log2e
shift = math.log2(gain)
grad_unit = 2.0 / (gain * scale)

VMEM = pl.BlockSpec(memory_space=pltpu.VMEM)
SMEM = pl.BlockSpec(memory_space=pltpu.SMEM)


def div_rem(value, size):
    if size & (size - 1) == 0:
        return lax.shift_right_logical(value, size.bit_length() - 1), value & (size - 1)
    return lax.div(value, size), lax.rem(value, size)


def route_kernel(spans, sizes, cell_ref, count_ref, xyz_ref, wt_ref, out_ref, slot_ref, used_ref):
    blocks, _, pts = xyz_ref.shape
    bricks = sizes[0] * sizes[1] * sizes[2]
    lane = lax.broadcasted_iota(jnp.int32, (1, pts), 1)
    out_ref[:, :, : 4 * pts] = jnp.zeros((out_ref.shape[0], 1, 4 * pts), jnp.float32)
    out_ref[:, :, 4 * pts :] = jnp.full((out_ref.shape[0], 1, LANES), -1.0, jnp.float32)

    def clear(i, carry):
        used_ref[i] = 0
        return carry

    lax.fori_loop(0, bricks, clear, 0, unroll=8)

    def one(b, carry):
        rest, along_z = div_rem(cell_ref[b], spans[2] * sizes[2])
        along_x, along_y = div_rem(rest, spans[1] * sizes[1])
        brick_x, in_x = div_rem(along_x, spans[0])
        brick_y, in_y = div_rem(along_y, spans[1])
        brick_z, in_z = div_rem(along_z, spans[2])
        target = (brick_x * sizes[1] + brick_y) * sizes[2] + brick_z
        local = (in_x * spans[1] + in_y) * spans[2] + in_z
        before = used_ref[target]
        used_ref[target] = before + 1
        slot = target * MOST + before
        slot_ref[b] = slot
        count = count_ref[b]
        for f in range(3):
            out_ref[slot, :, f * pts : (f + 1) * pts] = xyz_ref[b, f : f + 1, :]
        out_ref[slot, :, 3 * pts : 4 * pts] = jnp.where(lane < count, wt_ref[pl.ds(b, 1), :], 0.0)
        out_ref[slot, :, 4 * pts :] = jnp.full((1, LANES), local, jnp.int32).astype(jnp.float32)
        return carry

    lax.fori_loop(0, blocks, one, 0, unroll=4)


def lane_ids(shape):
    return lax.broadcasted_iota(jnp.int32, shape, len(shape) - 1)


def sub_ids(shape):
    return lax.broadcasted_iota(jnp.int32, shape, len(shape) - 2)


def bases_of(label, spans, rows, planes):
    in_y, in_z = div_rem(label, spans[2])
    cells = spans[2] + 2
    return [
        pl.multiple_of(((p * rows + in_y + dy) * cells + in_z) * SLOTS, SLOTS)
        for p in range(planes)
        for dy in range(3)
    ]


def gather_sum(acc_ref, base, height):
    lane = lane_ids((8, LANES))
    sub = sub_ids((8, LANES))
    total = None
    for t in range(height // 8):
        at = pl.ds(pl.multiple_of(base + 8 * t, 8), 8)
        part = jnp.sum(acc_ref[at, :], axis=1, keepdims=True)
        part = jnp.where(lane == sub + 8 * t, part, 0.0)
        total = part if total is None else total + part
    return jnp.sum(total, axis=0, keepdims=True)


def fold8(value):
    return jnp.sum(value.reshape(value.shape[0] // 8, 8, value.shape[1]), axis=0)


def pieces(value):
    first = value.astype(jnp.bfloat16).astype(jnp.float32)
    rest = value - first
    second = rest.astype(jnp.bfloat16).astype(jnp.float32)
    return first, second, rest - second


def cross_rows(x, y, z, twice):
    rows = []
    split = [pieces(v) for v in (x, y, z)]
    for one in split:
        rows += list(one) if twice else [one[0]] * 3
    for one in split:
        rows += list(one[:2]) if twice else [one[1]] * 2
    for one in split:
        rows += [one[0]] if twice else [one[2]]
    return [v + v for v in rows] if twice else rows


PIECE_ROWS = ((0, 9, 15), (3, 11, 16), (6, 13, 17), (24, 25, 26))


def selector(fields):
    shape = (LANES, LANES * len(fields))
    row = sub_ids(shape)
    lane = lane_ids(shape)
    pick = None
    for n, f in enumerate(fields):
        hit = (row == PIECE_ROWS[f][0]) | (row == PIECE_ROWS[f][1]) | (row == PIECE_ROWS[f][2])
        hit = hit & (lane >= n * LANES) & (lane < (n + 1) * LANES)
        pick = hit if pick is None else pick | hit
    return jnp.where(pick, 1.0, 0.0).astype(jnp.bfloat16)


def product(left, right):
    return jnp.dot(left, right, preferred_element_type=jnp.float32)


def fill(slot, t_ref, label_ref, pair_ref, feat_ref, spans, rows, planes):
    label = label_ref[slot]
    _, in_z = div_rem(label, spans[2])
    near, _ = div_rem(in_z, 4)
    part = pair_ref[pl.ds(pl.multiple_of(slot * 32, 32), 32), :]
    right = jnp.concatenate([part] * 4, axis=0)
    right = jnp.where(lax.shift_right_logical(sub_ids(right.shape), 5) == near, right, 0.0)
    right = right.astype(jnp.bfloat16)
    left = [feat_ref[pl.ds(base, 96), :] for base in bases_of(label, spans, rows, planes)]
    t_ref[...] = product(jnp.concatenate(left, axis=0), right)


def in_turn(used, list_ref, ta_ref, tb_ref, load, use):
    load(list_ref[0], ta_ref)

    def two(i, carry):
        first = list_ref[2 * i]
        second = list_ref[2 * i + 1]
        load(second, tb_ref)
        use(first, ta_ref)
        load(list_ref[2 * i + 2], ta_ref)
        use(second, tb_ref)
        return carry

    lax.fori_loop(0, lax.shift_right_logical(used + 1, 1), two, 0)


def density_kernel(
    spans, planes, in_ref, gauss_ref,
    feat_ref, point_ref, pair_ref, zg_ref, zr_ref, label_ref, list_ref, used_ref,
    raw_ref, fs_ref, ma_ref, acc_ref, line_ref, ta_ref, tb_ref,
):
    slots = in_ref.shape[0]
    pts = LANES
    rows = spans[1] + 2
    width = (spans[2] + 2) * SLOTS
    chunks = -(-width // LANES)
    here = [lax.axis_index(a) * s for a, s in zip(AXES, spans)]
    ref_x = here[0].astype(jnp.float32) + 0.5 * spans[0]
    ref_y = here[1].astype(jnp.float32) + 0.5 * spans[1]
    ref_z = here[2].astype(jnp.float32) + 2.0

    for s in range(slots):
        label_ref[s] = in_ref[s, :, 4 * pts :].astype(jnp.int32)[0, 0]
        for f in range(5):
            raw_ref[f, s : s + 1, :] = in_ref[s, :, f * pts : (f + 1) * pts]
    for f in range(5):
        raw_ref[f, slots : slots + 8, :] = jnp.zeros((8, pts), jnp.float32)
    label_ref[slots] = 0

    def order(s, n):
        list_ref[n] = s
        return n + (label_ref[s] >= 0).astype(jnp.int32)

    used = lax.fori_loop(0, slots, order, 0)
    for n in range(3):
        list_ref[used + n] = slots
    used_ref[0] = used

    for g in range(slots // 8 + 1):
        x, y, z, w, lab = (raw_ref[f, 8 * g : 8 * g + 8, :] for f in range(5))
        lab = jnp.maximum(lab, 0.0)
        in_z = lab - jnp.floor((lab + 0.5) * (1.0 / spans[2])) * spans[2]
        near = jnp.floor((in_z + 0.5) * 0.25) * 4.0
        x = (x - ref_x) * scale
        y = (y - ref_y) * scale
        at_z = (z - (ref_z + near)) * scale
        z = (z - ref_z) * scale
        one = jnp.ones_like(x)
        lines = cross_rows(x, y, at_z, True) + [one] * 3
        lines += list(pieces(0.0 - (x * x + y * y + at_z * at_z)))
        lines += [jnp.zeros_like(x)] * 8
        for k, v in enumerate(lines):
            pair_ref[pl.ds(g * 256 + k, 8, stride=32), :] = v
        for f, v in enumerate((x, y, z, w, one, one, one, one)):
            point_ref[pl.ds(g * 64 + f, 8, stride=8), :] = v

    tall = planes * 8
    fs_ref[...] = jnp.zeros(fs_ref.shape, jnp.float32)
    for c in range(chunks):
        height = min(LANES, width - c * LANES)
        lanes = slice(c * LANES, (c + 1) * LANES)
        for p in range(planes):
            x, y, z, a = (gauss_ref[f, p, :, lanes] for f in range(4))
            x = (x - ref_x) * scale
            y = (y - ref_y) * scale
            plane_sq = x * x + y * y
            for q in range(4):
                at_z = (z - (ref_z + 4.0 * q)) * scale
                lines = cross_rows(x, y, at_z, False)
                lines += list(pieces(shift - (plane_sq + at_z * at_z)))
                lines += [jnp.ones_like(x)] * 3
                if q == 0:
                    lines += list(pieces(a))
                for k, v in enumerate(lines):
                    top = (32 * q + k) * tall + 8 * p
                    fs_ref[top : top + rows, :] = v
        for p in range(planes):
            for r in range(rows):
                block = jnp.concatenate(
                    [fs_ref[pl.ds(8 * t * tall + 8 * p + r, 8, stride=tall), :] for t in range(16)], axis=0
                )
                block = block.T.astype(jnp.bfloat16)
                top = (p * rows + r) * width + c * LANES
                feat_ref[top : top + height, :] = block[:height]
    pick = selector((3,))
    for r in range(planes * rows):
        ma_ref[r * width : (r + 1) * width, :] = product(feat_ref[r * width : (r + 1) * width, :], pick)
    acc_ref[...] = jnp.zeros(acc_ref.shape, jnp.float32)

    def load(slot, t_ref):
        fill(slot, t_ref, label_ref, pair_ref, feat_ref, spans, rows, planes)

    def use(slot, t_ref):
        w = point_ref[pl.ds(pl.multiple_of(slot * 8, 8), 8), :][3:4]
        total = jnp.zeros((8, LANES), jnp.float32)
        for j, base in enumerate(bases_of(label_ref[slot], spans, rows, planes)):
            for c in range(3):
                at = pl.ds(pl.multiple_of(base + c * SLOTS, SLOTS), SLOTS)
                top = j * 96 + c * SLOTS
                kern = jnp.exp2(jnp.exp2(t_ref[top : top + SLOTS, :]))
                total = total + fold8(kern * ma_ref[at, :])
                acc_ref[at, :] += kern * w
        here = pl.ds(pl.multiple_of(slot * 8, 8), 8)
        zp = 1.0 + jnp.sum(total, axis=0, keepdims=True)
        old = point_ref[here, :]
        point_ref[here, :] = jnp.where(sub_ids(old.shape) == 4, zp, old)

    in_turn(used, list_ref, ta_ref, tb_ref, load, use)

    def sum_row(r, carry):
        for c in range(chunks):
            height = min(LANES, width - c * LANES)
            line_ref[0, r, :, c * LANES : (c + 1) * LANES] = gather_sum(
                acc_ref, r * width + c * LANES, height
            )
        return carry

    lax.fori_loop(0, planes * rows, sum_row, 0)
    for p in range(planes):
        for r in range(rows):
            zg_ref[p, r : r + 1, :] = line_ref[0, p * rows + r]
            zr_ref[planes - 1 - p, r : r + 1, :] = line_ref[0, p * rows + r]


def gradient_kernel(
    spans, planes, feat_ref, point_ref, pair_ref, zg_ref, label_ref, list_ref, used_ref,
    reply_ref, grad_ref, other_ref,
    mx_ref, my_ref, mz_ref, ma_ref, mb_ref, ax_ref, ay_ref, az_ref, ad_ref, line_ref, t_ref,
):
    rows = spans[1] + 2
    width = (spans[2] + 2) * SLOTS
    chunks = -(-width // LANES)
    pick = selector((0, 1, 2, 3))
    for r in range(planes * rows):
        at = slice(r * width, (r + 1) * width)
        both = product(feat_ref[at, :], pick)
        for f, ref in enumerate((mx_ref, my_ref, mz_ref, ma_ref)):
            ref[at, :] = both[:, f * LANES : (f + 1) * LANES]
    for c in range(chunks):
        height = min(LANES, width - c * LANES)
        lanes = slice(c * LANES, (c + 1) * LANES)
        block = []
        for p in range(planes):
            block.append(1.0 / (1.0 + zg_ref[p, :, lanes]))
            block.append(jnp.ones((8 - rows, LANES), jnp.float32))
        block = jnp.concatenate(block, axis=0).T
        for p in range(planes):
            for r in range(rows):
                top = (p * rows + r) * width + c * LANES
                at = slice(top, top + height)
                n = p * 8 + r
                mb_ref[at, :] = ma_ref[at, :] * block[:height, n : n + 1]
    for ref in (ax_ref, ay_ref, az_ref, ad_ref):
        ref[...] = jnp.zeros(ref.shape, jnp.float32)

    def use(i, carry):
        slot = list_ref[i]
        x, y, z, w, zp = (point_ref[slot, f : f + 1, :] for f in range(5))
        ip = 1.0 / zp
        px = py = pz = jnp.zeros((8, LANES), jnp.float32)
        for base in bases_of(label_ref[slot], spans, rows, planes):
            for c in range(3):
                at = pl.ds(pl.multiple_of(base + c * SLOTS, SLOTS), SLOTS)
                ex = x - mx_ref[at, :]
                ey = y - my_ref[at, :]
                ez = z - mz_ref[at, :]
                fall = jnp.exp2(shift - (ex * ex + ey * ey + ez * ez))
                wk = jnp.exp2(fall) * w
                h = wk * fall * (ma_ref[at, :] * ip + mb_ref[at, :])
                dx = h * ex
                dy = h * ey
                dz = h * ez
                px = px + fold8(dx)
                py = py + fold8(dy)
                pz = pz + fold8(dz)
                ax_ref[at, :] += dx
                ay_ref[at, :] += dy
                az_ref[at, :] += dz
                ad_ref[at, :] += wk * ip
        loss = jnp.where(w > 0.0, kernel_width * sharp - kernel_width * jnp.log(zp), 0.0)
        reply_ref[slot, 0:1, :] = loss
        for f, v in enumerate((px, py, pz)):
            reply_ref[slot, f + 1 : f + 2, :] = jnp.sum(v, axis=0, keepdims=True) * grad_unit
        return carry

    lax.fori_loop(0, used_ref[0], use, 0)

    def sum_row(r, carry):
        for f, ref in enumerate((ax_ref, ay_ref, az_ref, ad_ref)):
            unit = -grad_unit if f < 3 else 1.0
            for c in range(chunks):
                height = min(LANES, width - c * LANES)
                line_ref[f, r, :, c * LANES : (c + 1) * LANES] = (
                    gather_sum(ref, r * width + c * LANES, height) * unit
                )
        return carry

    lax.fori_loop(0, planes * rows, sum_row, 0)
    for f in range(4):
        for p in range(planes):
            for r in range(rows):
                if p == 0:
                    grad_ref[f, r : r + 1, :] = line_ref[f, r]
                else:
                    other_ref[p - 1, f, r : r + 1, :] = line_ref[f, p * rows + r]


def pick_kernel(slot_ref, reply_ref, out_ref):
    def one(b, carry):
        out_ref[b] = reply_ref[slot_ref[b]]
        return carry

    lax.fori_loop(0, out_ref.shape[0], one, 0, unroll=4)


def swap(value, axis, odd):
    count = lax.axis_size(axis)
    pairs = []
    for i in range(odd, count - 1, 2):
        pairs += [(i, i + 1), (i + 1, i)]
    if odd and count % 2 == 0 and count > 2:
        pairs += [(0, count - 1), (count - 1, 0)]
    return lax.ppermute(value, axis, pairs)


def trade(low, high, axis):
    count = lax.axis_size(axis)
    here = lax.axis_index(axis)
    even = here % 2 == 0
    first = swap(jnp.where(even, high, low), axis, 0)
    second = swap(jnp.where(even, low, high), axis, 1) if count > 2 else jnp.zeros_like(first)
    from_low = jnp.where(here > 0, jnp.where(even, second, first), 0.0)
    from_high = jnp.where(here < count - 1, jnp.where(even, first, second), 0.0)
    return from_low, from_high


def step(
    point_xyz, point_weight, block_cell, block_count, gauss_mean, gauss_opacity, gauss_count
):
    blocks, _, pts = point_xyz.shape
    span_x, span_y, span_z, _, slots = gauss_mean.shape
    spans = (span_x, span_y, span_z)
    sizes = tuple(lax.axis_size(a) for a in AXES)
    if span_x != 1 or slots != SLOTS or pts != LANES or span_y < 2 or span_z % 4:
        raise ValueError("unsupported brick")
    bricks = sizes[0] * sizes[1] * sizes[2]
    places = bricks * MOST
    f32 = jnp.float32

    outgoing, send_slot = pl.pallas_call(
        functools.partial(route_kernel, spans, sizes),
        out_shape=(
            jax.ShapeDtypeStruct((places, 1, 5 * pts), f32),
            jax.ShapeDtypeStruct((blocks,), jnp.int32),
        ),
        in_specs=[SMEM, SMEM, VMEM, VMEM],
        out_specs=(VMEM, SMEM),
        scratch_shapes=[pltpu.SMEM((bricks,), jnp.int32)],
        cost_estimate=pl.CostEstimate(flops=3000000*1000, bytes_accessed=1 << 18, transcendentals=0),
        name="route",
    )(block_cell, block_count, point_xyz, point_weight)
    incoming = lax.all_to_all(outgoing, AXES, split_axis=0, concat_axis=0, tiled=True)

    present = jnp.arange(slots, dtype=jnp.int32) < gauss_count[..., None]
    own = jnp.concatenate([gauss_mean, jnp.where(present, gauss_opacity, 0.0)[..., None, :]], axis=3)
    own = own[0].transpose(2, 0, 1, 3).reshape(4, 1, span_y, span_z * slots)
    if sizes[0] == 2:
        stack = jnp.concatenate([own, swap(own, "gx", 0)], axis=1)
    else:
        stack = jnp.concatenate([own, *trade(own, own, "gx")], axis=1)
    planes = stack.shape[1]
    rows = span_y + 2
    low, high = trade(stack[:, :, :1], stack[:, :, -1:], "gy")
    stack = jnp.concatenate([low, stack, high], axis=2)
    low, high = trade(stack[..., :slots], stack[..., -slots:], "gz")
    width = (span_z + 2) * slots
    wide = -(-width // LANES) * LANES
    stack = jnp.concatenate(
        [low, stack, high, jnp.zeros((4, planes, rows, wide - width), f32)], axis=3
    )

    table = pltpu.VMEM((planes * rows * width, LANES), f32)
    turn = pltpu.VMEM((planes * 3 * 96, LANES), f32)
    feats, points, pairs, part, mirror, label, order, used = pl.pallas_call(
        functools.partial(density_kernel, spans, planes),
        out_shape=(
            jax.ShapeDtypeStruct((planes * rows * width, LANES), jnp.bfloat16),
            jax.ShapeDtypeStruct(((places + 8) * 8, LANES), f32),
            jax.ShapeDtypeStruct(((places + 8) * 32, LANES), f32),
            jax.ShapeDtypeStruct((planes, rows, wide), f32),
            jax.ShapeDtypeStruct((planes, rows, wide), f32),
            jax.ShapeDtypeStruct((places + 1,), jnp.int32),
            jax.ShapeDtypeStruct((places + 3,), jnp.int32),
            jax.ShapeDtypeStruct((1,), jnp.int32),
        ),
        in_specs=[VMEM, VMEM],
        out_specs=(VMEM, VMEM, VMEM, VMEM, VMEM, SMEM, SMEM, SMEM),
        scratch_shapes=[
            pltpu.VMEM((5, places + 8, LANES), f32),
            pltpu.VMEM((LANES * planes * 8, LANES), f32),
            table,
            table,
            pltpu.VMEM((1, planes * rows, 1, wide), f32),
            turn,
            turn,
        ],
        cost_estimate=pl.CostEstimate(flops=15000000*1000, bytes_accessed=1 << 18, transcendentals=0),
        name="density",
    )(incoming, stack)

    if sizes[0] == 2:
        part = part + swap(mirror, "gx", 0)
    else:
        low, high = trade(part[1], part[2], "gx")
        whole = part[0] + low + high
        part = jnp.stack([whole, *trade(whole, whole, "gx")])
    low, high = trade(part[:, :2], part[:, -2:], "gy")
    part = jnp.concatenate([part[:, :2] + low, part[:, 2:-2], part[:, -2:] + high], axis=1)
    edge = 2 * slots
    low, high = trade(part[..., :edge], part[..., width - edge : width], "gz")
    part = jnp.concatenate(
        [
            part[..., :edge] + low,
            part[..., edge : width - edge],
            part[..., width - edge : width] + high,
            jnp.zeros((planes, rows, wide - width), f32),
        ],
        axis=2,
    )
    reply, grad, other = pl.pallas_call(
        functools.partial(gradient_kernel, spans, planes),
        out_shape=(
            jax.ShapeDtypeStruct((places, 4, LANES), f32),
            jax.ShapeDtypeStruct((4, rows, wide), f32),
            jax.ShapeDtypeStruct((planes - 1, 4, rows, wide), f32),
        ),
        in_specs=[VMEM, VMEM, VMEM, VMEM, SMEM, SMEM, SMEM],
        out_specs=(VMEM, VMEM, VMEM),
        scratch_shapes=[table] * 9
        + [pltpu.VMEM((4, planes * rows, 1, wide), f32), pltpu.VMEM((2, planes * 3 * 96, LANES), f32)],
        cost_estimate=pl.CostEstimate(flops=28000000*1000, bytes_accessed=1 << 18, transcendentals=0),
        name="gradient",
    )(feats, points.reshape(places + 8, 8, LANES), pairs, part, label, order, used)

    answer = lax.all_to_all(reply, AXES, split_axis=0, concat_axis=0, tiled=True)
    point_out = pl.pallas_call(
        pick_kernel,
        out_shape=jax.ShapeDtypeStruct((blocks, 4, pts), f32),
        in_specs=[SMEM, VMEM],
        out_specs=VMEM,
        cost_estimate=pl.CostEstimate(flops=2000000*1000, bytes_accessed=1 << 18, transcendentals=0),
        name="pick",
    )(send_slot, answer)

    if sizes[0] == 2:
        grad = grad + swap(other[0], "gx", 0)
    else:
        low, high = trade(other[0], other[1], "gx")
        grad = grad + low + high
    low, high = trade(grad[:, :1], grad[:, -1:], "gy")
    grad = jnp.concatenate(
        [grad[:, 1:2] + low, grad[:, 2:-2], grad[:, -2:-1] + high], axis=1
    )
    low, high = trade(grad[..., :slots], grad[..., width - slots : width], "gz")
    grad = jnp.concatenate(
        [
            grad[..., slots : 2 * slots] + low,
            grad[..., 2 * slots : width - 2 * slots],
            grad[..., width - 2 * slots : width - slots] + high,
        ],
        axis=2,
    )
    grad = grad.reshape(4, span_y, span_z, slots).transpose(1, 2, 0, 3)[None]
    total_g = 1.0 + part[0, 1:-1, slots : width - slots].reshape(1, span_y, span_z, slots)
    opacity = jnp.where(
        present,
        kernel_width * sharp - kernel_width * jnp.log(total_g) - kernel_width * grad[..., 3, :],
        0.0,
    )
    gauss_grad = jnp.concatenate([grad[..., :3, :], opacity[..., None, :]], axis=3)
    return point_out, gauss_grad


def solution(mesh):
    return jax.shard_map(
        step,
        mesh=mesh,
        in_specs=(
            P(AXES, None, None),
            P(AXES, None),
            P(AXES),
            P(AXES),
            P("gx", "gy", "gz", None, None),
            P("gx", "gy", "gz", None),
            P("gx", "gy", "gz"),
        ),
        out_specs=(P(AXES, None, None), P("gx", "gy", "gz", None, None)),
        check_vma=False,
    )
```

time: 122 us -> 116 us (0.951)
  Pallas kernels: 51.8 us -> 42.2 us
  waiting for transfers between devices: 24.1 us -> 30 us
  local copies, waits for them, and re-layouts: 6.38 us -> 3.46 us
  other arithmetic: 3.98 us -> 6.57 us
  starting transfers between devices: 34 us -> 32.2 us
    pallas_call x4, Pallas kernels: 51.8 us -> 42.2 us  [the longest x1 24.1 us: step(): pl.pallas_call(functools.partial(gradient_kernel, spans, planes), out_sha...]
    all_to_all x2, waiting for transfers between devices: 6.52 us -> 14.8 us  [the longest x1 7.87 us: step(): lax.all_to_all(outgoing, AXES, split_axis=0, concat_axis=0, tiled=True)]
    all_to_all x2, starting transfers between devices: 11.3 us -> 8.16 us  [the longest x1 4.18 us: step(): lax.all_to_all(outgoing, AXES, split_axis=0, concat_axis=0, tiled=True)]
    ppermute x15, waiting for transfers between devices: 17.6 us -> 15.1 us  [swap(): return lax.ppermute(value, axis, pairs)]
    add x6, other arithmetic: 0.14 us -> 1.83 us  [the longest x1 0.91 us: step(): grad = grad + swap(other[0], 'gx', 0)]
    concatenate x7 -> x6, other arithmetic: 1.1 us -> 2.5 us  [the longest x1 0.86 us: step(): jnp.concatenate([low, stack, high, jnp.zeros((4, planes, rows, wide - wid...]
    ppermute x15, starting transfers between devices: 22.7 us -> 24.1 us  [swap(): return lax.ppermute(value, axis, pairs)]
    reshape x4, local copies, waits for them, and re-layouts: 1.62 us -> 0.32 us  [the longest x2 0.19 us: step(): grad = grad.reshape(4, span_y, span_z, slots).transpose(1, 2, 0, 3)[None]]
  transfers between devices with their start and end apart: 17 -> 17, of which waited for: 10 -> 9; matrix products, arithmetic and copies ran while one was open for 3% -> 4% of each run, Pallas kernels for 2% -> 2%
where the time goes in v3:
time: 116 us; the launch traced here: 115 us
  Pallas kernels  42.2 us (36%)
  starting transfers between devices  32.2 us (28%)
  waiting for transfers between devices  30 us (26%)
  other arithmetic  6.57 us (6%)
  local copies, waits for them, and re-layouts  3.46 us (3%)
    pallas_call x1, Pallas kernels, step(): pl.pallas_call(functools.partial(gradient_kernel, spans, planes), out_sha...  24.1 us
    ppermute x15, starting transfers between devices, swap(): return lax.ppermute(value, axis, pairs)  24.1 us
    ppermute x15, waiting for transfers between devices, swap(): return lax.ppermute(value, axis, pairs)  15.1 us
    pallas_call x1, Pallas kernels, step(): pl.pallas_call(functools.partial(density_kernel, spans, planes), out_shap...  14.3 us
    all_to_all x1, waiting for transfers between devices, step(): lax.all_to_all(outgoing, AXES, split_axis=0, concat_axis=0, tiled=True)  7.87 us
    all_to_all x1, waiting for transfers between devices, step(): lax.all_to_all(reply, AXES, split_axis=0, concat_axis=0, tiled=True)  6.95 us
    all_to_all x1, starting transfers between devices, step(): lax.all_to_all(outgoing, AXES, split_axis=0, concat_axis=0, tiled=True)  4.18 us
    all_to_all x1, starting transfers between devices, step(): lax.all_to_all(reply, AXES, split_axis=0, concat_axis=0, tiled=True)  3.99 us
  transfers between devices with their start and end apart: 17, of which 9 were waited for; matrix products, arithmetic and copies ran while one was open for 4% of the time, Pallas kernels for 2%

profile of v3, /device:TPU:0, one launch (start us, length us, event | category | flops | bytes accessed | tf_op | source)
XLA Modules:
  0.0 115.2 jit_solution(15475113238310975118)
XLA Ops:
  1.5 0.9 maximum_bitcast_fusion
  2.5 3.0 %collective-permute-start = (f32[4,1,4,512]{3,2,1,0:T(4,128)S(1)}, f32[4,1,4,512]{3,2,1,0:T(4,128)S(1)}, u32[]{:S(2)}, u32[]{:S(2)}) collective-permute-start(f32[4,1,4,512]{3,2,1,0:T(4,128)S(1)} %get-tuple-element.52), channel_id=1, source_target_pairs={{0,16},{16,0},{1,17},{17,1},{2,18},{18,2},{3,19},{19,3},{4,20},{20... | collective-permute-start | bytes 98312 | tf_op jit(solution)/shard_map/ppermute | solution.py:386
  5.6 1.9 %collective-permute-done = f32[4,1,4,512]{3,2,1,0:T(4,128)S(1)} collective-permute-done((f32[4,1,4,512]{3,2,1,0:T(4,128)S(1)}, f32[4,1,4,512]{3,2,1,0:T(4,128)S(1)}, u32[]{:S(2)}, u32[]{:S(2)}) %collective-permute-start) | collective-permute-done | bytes 32800 | tf_op jit(solution)/shard_map/ppermute | solution.py:386
  7.9 1.8 %collective-permute-start.2 = (f32[4,2,1,512]{3,2,1,0:T(1,128)S(1)}, f32[4,2,1,512]{3,2,1,0:T(1,128)S(1)}, u32[]{:S(2)}, u32[]{:S(2)}) collective-permute-start(f32[4,2,1,512]{3,2,1,0:T(1,128)S(1)} %get-tuple-element.40), channel_id=1, source_target_pairs={{0,4},{4,0},{8,12},{12,8},{1,5},{5,1},{9,13},{13,9},{2,6},{6,2},{1... | collective-permute-start | bytes 49160 | tf_op jit(solution)/shard_map/ppermute | solution.py:386
  9.7 1.6 %copy.9.xyz_ref = f32[48,3,128]{2,1,0:T(4,128)} copy(f32[48,3,128]{2,0,1:T(8,128)} %param.7) | data formatting | bytes 147456 | tf_op args[0]
  11.4 3.7 %collective-permute-start.3 = (f32[4,2,6,32]{3,2,1,0:T(8,128)S(1)}, f32[4,2,6,32]{3,2,1,0:T(8,128)S(1)}, u32[]{:S(2)}, u32[]{:S(2)}) collective-permute-start(f32[4,2,6,32]{3,2,1,0:T(8,128)S(1)} %get-tuple-element.33), channel_id=1, source_target_pairs={{1,2},{2,1},{0,3},{3,0},{5,6},{6,5},{4,7},{7,4},{9,10},{10,9},{8,1... | collective-permute-start | bytes 18440 | tf_op jit(solution)/shard_map/ppermute | solution.py:386
  15.2 2.1 %route.1 = (f32[64,1,640]{2,1,0:T(1,128)}, s32[48]{0:T(128)}) custom-call(s32[48]{0:T(128)} %cell_ref.1, s32[48]{0:T(128)} %count_ref.1, f32[48,3,128]{2,1,0:T(4,128)} %copy.9.xyz_ref, f32[48,128]{1,0:T(8,128)} %wt_ref.1), custom_call_target="tpu_custom_call" | custom-call | flops 3000000000 | bytes 262144 | tf_op jit(solution)/shard_map/route/pallas_call | solution.py:413
  17.3 4.2 %all-to-all-start = ((f32[64,1,640]{2,1,0:T(1,128)}), f32[64,1,640]{2,1,0:T(1,128)S(1)}, u32[]{:S(2)}, u32[]{:S(2)}) async-start(f32[64,1,640]{2,1,0:T(1,128)} %get-tuple-element.16), calls=%async_computation | async-start | bytes 327680 | tf_op jit(solution)/shard_map/all_to_all | solution.py:425
  22.4 7.9 %all-to-all-done.in_ref = f32[64,1,640]{2,1,0:T(1,128)S(1)} async-done(((f32[64,1,640]{2,1,0:T(1,128)}), f32[64,1,640]{2,1,0:T(1,128)S(1)}, u32[]{:S(2)}, u32[]{:S(2)}) %all-to-all-start) | async-done | bytes 163872 | tf_op jit(solution)/shard_map/all_to_all | solution.py:425
  31.0 14.3 %density.1 = (bf16[6912,128]{1,0:T(8,128)(2,1)}, f32[576,128]{1,0:T(8,128)}, f32[2304,128]{1,0:T(8,128)}, f32[2,6,640]{2,1,0:T(8,128)}, f32[2,6,640]{2,1,0:T(8,1...) custom-call(f32[64,1,640]{2,1,0:T(1,128)} %copy-done, f32[4,2,6,640]{3,2,1,0:T(8,128)} %maximum_maximum_fusion.gauss_ref), custom_call_target="tpu_custom_call" | custom-call | flops 15000000512 | bytes 262144 | tf_op jit(solution)/shard_map/density/pallas_call | solution.py:447
  45.3 1.2 %collective-permute-start.5 = (f32[2,6,640]{2,1,0:T(8,128)}, f32[2,6,640]{2,1,0:T(8,128)S(1)}, u32[]{:S(2)}, u32[]{:S(2)}) collective-permute-start(f32[2,6,640]{2,1,0:T(8,128)} %get-tuple-element.21), channel_id=1, source_target_pairs={{0,16},{16,0},{1,17},{17,1},{2,18},{18,2},{3,19},{19,3},{4,20},{20... | collective-permute-start | bytes 92168 | tf_op jit(solution)/shard_map/ppermute | solution.py:386
  46.4 3.1 %collective-permute-done.5 = f32[2,6,640]{2,1,0:T(8,128)S(1)} collective-permute-done((f32[2,6,640]{2,1,0:T(8,128)}, f32[2,6,640]{2,1,0:T(8,128)S(1)}, u32[]{:S(2)}, u32[]{:S(2)}) %collective-permute-start.5) | collective-permute-done | bytes 30752 | tf_op jit(solution)/shard_map/ppermute | solution.py:386
  51.3 2.2 %collective-permute-done.6 = f32[2,2,640]{2,1,0:T(2,128)S(1)} collective-permute-done((f32[2,2,640]{2,1,0:T(2,128)S(1)}, f32[2,2,640]{2,1,0:T(2,128)S(1)}, u32[]{:S(2)}, u32[]{:S(2)}) %collective-permute-start.6) | collective-permute-done | bytes 10272 | tf_op jit(solution)/shard_map/ppermute | solution.py:386
  53.6 2.5 %collective-permute-start.8 = (f32[2,6,64]{2,1,0:T(8,128)S(1)}, f32[2,6,64]{2,1,0:T(8,128)S(1)}, u32[]{:S(2)}, u32[]{:S(2)}) collective-permute-start(f32[2,6,64]{2,1,0:T(8,128)S(1)} %get-tuple-element.28), channel_id=1, source_target_pairs={{1,2},{2,1},{0,3},{3,0},{5,6},{6,5},{4,7},{7,4},{9,10},{10,9},{8,1... | collective-permute-start | bytes 9224 | tf_op jit(solution)/shard_map/ppermute | solution.py:386
  56.2 2.9 %collective-permute-done.8 = f32[2,6,64]{2,1,0:T(8,128)S(1)} collective-permute-done((f32[2,6,64]{2,1,0:T(8,128)S(1)}, f32[2,6,64]{2,1,0:T(8,128)S(1)}, u32[]{:S(2)}, u32[]{:S(2)}) %collective-permute-start.8) | collective-permute-done | bytes 3104 | tf_op jit(solution)/shard_map/ppermute | solution.py:386
  60.4 24.1 %gradient.1 = (f32[64,4,128]{2,1,0:T(4,128)}, f32[4,6,640]{2,1,0:T(8,128)}, f32[1,4,6,640]{3,2,1,0:T(8,128)}) custom-call(bf16[6912,128]{1,0:T(8,128)(2,1)} %get-tuple-element.17.feat_ref, f32[72,8,128]{2,1,0:T(8,128)} %bitcast.28, f32[2304,128]{1,0:T(8,128)} %get-tuple-element.19.pair_ref, f32[2,6,640]{2,1,0:T(8,128)} %pad_maximum_fusion.1.zg_ref, ...), custom_call_target="tpu_custom_call" | custom-call | flops 28000000000 | bytes 262144 | tf_op jit(solution)/shard_map/gradient/pallas_call | solution.py:493
  84.5 1.1 collective-permute-start.10
  85.6 3.6 %collective-permute-done.10 = f32[4,6,640]{2,1,0:T(8,128)S(1)} collective-permute-done((f32[4,6,640]{2,1,0:T(8,128)}, f32[4,6,640]{2,1,0:T(8,128)S(1)}, u32[]{:S(2)}, u32[]{:S(2)}) %collective-permute-start.10) | collective-permute-done | bytes 61472 | tf_op jit(solution)/shard_map/ppermute | solution.py:386
  89.2 0.9 add.64
  90.2 2.3 %collective-permute-start.12 = (f32[4,1,640]{2,1,0:T(1,128)S(1)}, f32[4,1,640]{2,1,0:T(1,128)S(1)}, u32[]{:S(2)}, u32[]{:S(2)}) collective-permute-start(f32[4,1,640]{2,1,0:T(1,128)S(1)} %get-tuple-element.36), channel_id=1, source_target_pairs={{0,4},{4,0},{8,12},{12,8},{1,5},{5,1},{9,13},{13,9},{2,6},{6,2},{1... | collective-permute-start | bytes 30728 | tf_op jit(solution)/shard_map/ppermute | solution.py:386
  93.4 7.0 %collective-permute-start.13 = (f32[4,4,32]{2,1,0:T(4,128)S(1)}, f32[4,4,32]{2,1,0:T(4,128)S(1)}, u32[]{:S(2)}, u32[]{:S(2)}) collective-permute-start(f32[4,4,32]{2,1,0:T(4,128)S(1)} %get-tuple-element.45), channel_id=1, source_target_pairs={{1,2},{2,1},{0,3},{3,0},{5,6},{6,5},{4,7},{7,4},{9,10},{10,9},{8,1... | collective-permute-start | bytes 6152 | tf_op jit(solution)/shard_map/ppermute | solution.py:386
  100.6 4.0 %all-to-all-start.1 = ((f32[64,4,128]{2,1,0:T(4,128)}), f32[64,4,128]{2,1,0:T(4,128)S(1)}, u32[]{:S(2)}, u32[]{:S(2)}) async-start(f32[64,4,128]{2,1,0:T(4,128)} %get-tuple-element.25), calls=%async_computation.1 | async-start | bytes 262144 | tf_op jit(solution)/shard_map/all_to_all | solution.py:508
  106.0 6.9 %all-to-all-done.1.reply_ref = f32[64,4,128]{2,1,0:T(4,128)S(1)} async-done(((f32[64,4,128]{2,1,0:T(4,128)}), f32[64,4,128]{2,1,0:T(4,128)S(1)}, u32[]{:S(2)}, u32[]{:S(2)}) %all-to-all-start.1) | async-done | bytes 131104 | tf_op jit(solution)/shard_map/all_to_all | solution.py:508
  113.6 1.6 %pick.1 = f32[48,4,128]{2,1,0:T(4,128)} custom-call(s32[48]{0:T(128)} %get-tuple-element.15.slot_ref, f32[64,4,128]{2,1,0:T(4,128)} %copy-done.1), custom_call_target="tpu_custom_call" | custom-call | flops 2000000000 | bytes 262144 | tf_op jit(solution)/shard_map/pick/pallas_call | solution.py:509
  (57 shorter events, 9.6 us)
Async XLA Ops:
  2.5 4.9 %collective-permute-start = (f32[4,1,4,512]{3,2,1,0:T(4,128)S(1)}, f32[4,1,4,512]{3,2,1,0:T(4,128)S(1)}, u32[]{:S(2)}, u32[]{:S(2)}) collective-permute-start(f32[4,1,4,512]{3,2,1,0:T(4,128)S(1)} %get-tuple-element.52), channel_id=1, source_target_pairs={{0,16},{16,0},{1,17},{17,1},{2,18},{18,2},{3,19},{19,3},{4,20},{20... | collective-permute-start | bytes 98312 | tf_op jit(solution)/shard_map/ppermute | solution.py:386
  7.5 3.8 %collective-permute-start.1 = (f32[4,2,1,512]{3,2,1,0:T(1,128)S(1)}, f32[4,2,1,512]{3,2,1,0:T(1,128)S(1)}, u32[]{:S(2)}, u32[]{:S(2)}) collective-permute-start(f32[4,2,1,512]{3,2,1,0:T(1,128)S(1)} %get-tuple-element.39), channel_id=1, source_target_pairs={{4,8},{8,4},{0,12},{12,0},{5,9},{9,5},{1,13},{13,1},{6,10},{10,6},... | collective-permute-start | bytes 49160 | tf_op jit(solution)/shard_map/ppermute | solution.py:386
  7.9 3.4 %collective-permute-start.2 = (f32[4,2,1,512]{3,2,1,0:T(1,128)S(1)}, f32[4,2,1,512]{3,2,1,0:T(1,128)S(1)}, u32[]{:S(2)}, u32[]{:S(2)}) collective-permute-start(f32[4,2,1,512]{3,2,1,0:T(1,128)S(1)} %get-tuple-element.40), channel_id=1, source_target_pairs={{0,4},{4,0},{8,12},{12,8},{1,5},{5,1},{9,13},{13,9},{2,6},{6,2},{1... | collective-permute-start | bytes 49160 | tf_op jit(solution)/shard_map/ppermute | solution.py:386
  11.4 10.1 %collective-permute-start.3 = (f32[4,2,6,32]{3,2,1,0:T(8,128)S(1)}, f32[4,2,6,32]{3,2,1,0:T(8,128)S(1)}, u32[]{:S(2)}, u32[]{:S(2)}) collective-permute-start(f32[4,2,6,32]{3,2,1,0:T(8,128)S(1)} %get-tuple-element.33), channel_id=1, source_target_pairs={{1,2},{2,1},{0,3},{3,0},{5,6},{6,5},{4,7},{7,4},{9,10},{10,9},{8,1... | collective-permute-start | bytes 18440 | tf_op jit(solution)/shard_map/ppermute | solution.py:386
  15.2 6.4 %collective-permute-start.4 = (f32[4,2,6,32]{3,2,1,0:T(8,128)S(1)}, f32[4,2,6,32]{3,2,1,0:T(8,128)S(1)}, u32[]{:S(2)}, u32[]{:S(2)}) collective-permute-start(f32[4,2,6,32]{3,2,1,0:T(8,128)S(1)} %get-tuple-element.34), channel_id=1, source_target_pairs={{0,1},{1,0},{2,3},{3,2},{4,5},{5,4},{6,7},{7,6},{8,9},{9,8},{10,11... | collective-permute-start | bytes 18440 | tf_op jit(solution)/shard_map/ppermute | solution.py:386
  17.3 13.0 %all-to-all-start = ((f32[64,1,640]{2,1,0:T(1,128)}), f32[64,1,640]{2,1,0:T(1,128)S(1)}, u32[]{:S(2)}, u32[]{:S(2)}) async-start(f32[64,1,640]{2,1,0:T(1,128)} %get-tuple-element.16), calls=%async_computation | async-start | bytes 327680 | tf_op jit(solution)/shard_map/all_to_all | solution.py:425
  30.3 0.7 copy-start
  45.3 4.3 %collective-permute-start.5 = (f32[2,6,640]{2,1,0:T(8,128)}, f32[2,6,640]{2,1,0:T(8,128)S(1)}, u32[]{:S(2)}, u32[]{:S(2)}) collective-permute-start(f32[2,6,640]{2,1,0:T(8,128)} %get-tuple-element.21), channel_id=1, source_target_pairs={{0,16},{16,0},{1,17},{17,1},{2,18},{18,2},{3,19},{19,3},{4,20},{20... | collective-permute-start | bytes 92168 | tf_op jit(solution)/shard_map/ppermute | solution.py:386
  50.4 3.2 %collective-permute-start.6 = (f32[2,2,640]{2,1,0:T(2,128)S(1)}, f32[2,2,640]{2,1,0:T(2,128)S(1)}, u32[]{:S(2)}, u32[]{:S(2)}) collective-permute-start(f32[2,2,640]{2,1,0:T(2,128)S(1)} %get-tuple-element.48), channel_id=1, source_target_pairs={{4,8},{8,4},{0,12},{12,0},{5,9},{9,5},{1,13},{13,1},{6,10},{10,6},... | collective-permute-start | bytes 30728 | tf_op jit(solution)/shard_map/ppermute | solution.py:386
  50.4 3.1 %collective-permute-start.7 = (f32[2,2,640]{2,1,0:T(2,128)S(1)}, f32[2,2,640]{2,1,0:T(2,128)S(1)}, u32[]{:S(2)}, u32[]{:S(2)}) collective-permute-start(f32[2,2,640]{2,1,0:T(2,128)S(1)} %get-tuple-element.49), channel_id=1, source_target_pairs={{0,4},{4,0},{8,12},{12,8},{1,5},{5,1},{9,13},{13,9},{2,6},{6,2},{1... | collective-permute-start | bytes 30728 | tf_op jit(solution)/shard_map/ppermute | solution.py:386
  53.6 5.5 %collective-permute-start.8 = (f32[2,6,64]{2,1,0:T(8,128)S(1)}, f32[2,6,64]{2,1,0:T(8,128)S(1)}, u32[]{:S(2)}, u32[]{:S(2)}) collective-permute-start(f32[2,6,64]{2,1,0:T(8,128)S(1)} %get-tuple-element.28), channel_id=1, source_target_pairs={{1,2},{2,1},{0,3},{3,0},{5,6},{6,5},{4,7},{7,4},{9,10},{10,9},{8,1... | collective-permute-start | bytes 9224 | tf_op jit(solution)/shard_map/ppermute | solution.py:386
  56.0 3.7 %collective-permute-start.9 = (f32[2,6,64]{2,1,0:T(8,128)S(1)}, f32[2,6,64]{2,1,0:T(8,128)S(1)}, u32[]{:S(2)}, u32[]{:S(2)}) collective-permute-start(f32[2,6,64]{2,1,0:T(8,128)S(1)} %broadcast_select_fusion.16), channel_id=1, source_target_pairs={{0,1},{1,0},{2,3},{3,2},{4,5},{5,4},{6,7},{7,6},{8,9},{9,8},{10,11... | collective-permute-start | bytes 9224 | tf_op jit(solution)/shard_map/ppermute | solution.py:386
  60.4 44.7 %copy-start.2 = (s32[1,4,16]{2,1,0:T(4,128)S(1)}, s32[1,4,16]{2,1,0:T(4,128)}, u32[]{:S(2)}) copy-start(s32[1,4,16]{2,1,0:T(4,128)} %param.13) | copy-start | bytes 772
  84.5 4.7 %collective-permute-start.10 = (f32[4,6,640]{2,1,0:T(8,128)}, f32[4,6,640]{2,1,0:T(8,128)S(1)}, u32[]{:S(2)}, u32[]{:S(2)}) collective-permute-start(f32[4,6,640]{2,1,0:T(8,128)} %bitcast.27), channel_id=1, source_target_pairs={{0,16},{16,0},{1,17},{17,1},{2,18},{18,2},{3,19},{19,3},{4,20},{20... | collective-permute-start | bytes 184328 | tf_op jit(solution)/shard_map/ppermute | solution.py:386
  90.1 3.2 %collective-permute-start.11 = (f32[4,1,640]{2,1,0:T(1,128)S(1)}, f32[4,1,640]{2,1,0:T(1,128)S(1)}, u32[]{:S(2)}, u32[]{:S(2)}) collective-permute-start(f32[4,1,640]{2,1,0:T(1,128)S(1)} %get-tuple-element.35), channel_id=1, source_target_pairs={{4,8},{8,4},{0,12},{12,0},{5,9},{9,5},{1,13},{13,1},{6,10},{10,6},... | collective-permute-start | bytes 30728 | tf_op jit(solution)/shard_map/ppermute | solution.py:386
  90.2 3.1 %collective-permute-start.12 = (f32[4,1,640]{2,1,0:T(1,128)S(1)}, f32[4,1,640]{2,1,0:T(1,128)S(1)}, u32[]{:S(2)}, u32[]{:S(2)}) collective-permute-start(f32[4,1,640]{2,1,0:T(1,128)S(1)} %get-tuple-element.36), channel_id=1, source_target_pairs={{0,4},{4,0},{8,12},{12,8},{1,5},{5,1},{9,13},{13,9},{2,6},{6,2},{1... | collective-permute-start | bytes 30728 | tf_op jit(solution)/shard_map/ppermute | solution.py:386
  93.4 11.3 %collective-permute-start.13 = (f32[4,4,32]{2,1,0:T(4,128)S(1)}, f32[4,4,32]{2,1,0:T(4,128)S(1)}, u32[]{:S(2)}, u32[]{:S(2)}) collective-permute-start(f32[4,4,32]{2,1,0:T(4,128)S(1)} %get-tuple-element.45), channel_id=1, source_target_pairs={{1,2},{2,1},{0,3},{3,0},{5,6},{6,5},{4,7},{7,4},{9,10},{10,9},{8,1... | collective-permute-start | bytes 6152 | tf_op jit(solution)/shard_map/ppermute | solution.py:386
  100.5 4.3 %collective-permute-start.14 = (f32[4,4,32]{2,1,0:T(4,128)S(1)}, f32[4,4,32]{2,1,0:T(4,128)S(1)}, u32[]{:S(2)}, u32[]{:S(2)}) collective-permute-start(f32[4,4,32]{2,1,0:T(4,128)S(1)} %get-tuple-element.46), channel_id=1, source_target_pairs={{0,1},{1,0},{2,3},{3,2},{4,5},{5,4},{6,7},{7,6},{8,9},{9,8},{10,11... | collective-permute-start | bytes 6152 | tf_op jit(solution)/shard_map/ppermute | solution.py:386
  100.6 12.4 %all-to-all-start.1 = ((f32[64,4,128]{2,1,0:T(4,128)}), f32[64,4,128]{2,1,0:T(4,128)S(1)}, u32[]{:S(2)}, u32[]{:S(2)}) async-start(f32[64,4,128]{2,1,0:T(4,128)} %get-tuple-element.25), calls=%async_computation.1 | async-start | bytes 262144 | tf_op jit(solution)/shard_map/all_to_all | solution.py:508
  112.9 0.6 copy-start.1

commit v4 on v3

--- a/solution.py
+++ b/solution.py
@@ -34,7 +34,7 @@
 
 
 def route_kernel(spans, sizes, cell_ref, count_ref, xyz_ref, wt_ref, out_ref, slot_ref, used_ref):
-    blocks, _, pts = xyz_ref.shape
+    _, blocks, pts = xyz_ref.shape
     bricks = sizes[0] * sizes[1] * sizes[2]
     lane = lax.broadcasted_iota(jnp.int32, (1, pts), 1)
     out_ref[:, :, : 4 * pts] = jnp.zeros((out_ref.shape[0], 1, 4 * pts), jnp.float32)
@@ -60,12 +60,31 @@
         slot_ref[b] = slot
         count = count_ref[b]
         for f in range(3):
-            out_ref[slot, :, f * pts : (f + 1) * pts] = xyz_ref[b, f : f + 1, :]
+            out_ref[slot, :, f * pts : (f + 1) * pts] = xyz_ref[f, pl.ds(b, 1), :]
         out_ref[slot, :, 3 * pts : 4 * pts] = jnp.where(lane < count, wt_ref[pl.ds(b, 1), :], 0.0)
         out_ref[slot, :, 4 * pts :] = jnp.full((1, LANES), local, jnp.int32).astype(jnp.float32)
         return carry
 
     lax.fori_loop(0, blocks, one, 0, unroll=4)
+
+
+def route(spans, sizes, point_xyz, point_weight, block_cell, block_count):
+    blocks, _, pts = point_xyz.shape
+    bricks = sizes[0] * sizes[1] * sizes[2]
+    places = bricks * MOST
+    f32 = jnp.float32
+    return pl.pallas_call(
+        functools.partial(route_kernel, spans, sizes),
+        out_shape=(
+            jax.ShapeDtypeStruct((places, 1, 5 * pts), f32),
+            jax.ShapeDtypeStruct((blocks,), jnp.int32),
+        ),
+        in_specs=[SMEM, SMEM, VMEM, VMEM],
+        out_specs=(VMEM, SMEM),
+        scratch_shapes=[pltpu.SMEM((bricks,), jnp.int32)],
+        cost_estimate=pl.CostEstimate(flops=3000000*1000, bytes_accessed=1 << 18, transcendentals=0),
+        name="route",
+    )(block_cell, block_count, point_xyz.transpose(1, 0, 2), point_weight)
 
 
 def lane_ids(shape):
@@ -98,6 +117,18 @@
     return jnp.sum(total, axis=0, keepdims=True)
 
 
+def clear(refs):
+    step = 96
+
+    def some(i, carry):
+        at = pl.ds(pl.multiple_of(i * step, 8), step)
+        for ref in refs:
+            ref[at, :] = jnp.zeros((step, ref.shape[1]), jnp.float32)
+        return carry
+
+    lax.fori_loop(0, refs[0].shape[0] // step, some, 0)
+
+
 def fold8(value):
     return jnp.sum(value.reshape(value.shape[0] // 8, 8, value.shape[1]), axis=0)
 
@@ -169,8 +200,8 @@
 
 def density_kernel(
     spans, planes, in_ref, gauss_ref,
-    feat_ref, point_ref, pair_ref, zg_ref, zr_ref, label_ref, list_ref, used_ref,
-    raw_ref, fs_ref, ma_ref, acc_ref, line_ref, ta_ref, tb_ref,
+    feat_ref, point_ref, zg_ref, zr_ref, label_ref, list_ref, used_ref,
+    pair_ref, raw_ref, fs_ref, ma_ref, acc_ref, line_ref, ta_ref, tb_ref,
 ):
     slots = in_ref.shape[0]
     pts = LANES
@@ -248,7 +279,7 @@
     pick = selector((3,))
     for r in range(planes * rows):
         ma_ref[r * width : (r + 1) * width, :] = product(feat_ref[r * width : (r + 1) * width, :], pick)
-    acc_ref[...] = jnp.zeros(acc_ref.shape, jnp.float32)
+    clear((acc_ref,))
 
     def load(slot, t_ref):
         fill(slot, t_ref, label_ref, pair_ref, feat_ref, spans, rows, planes)
@@ -286,7 +317,7 @@
 
 
 def gradient_kernel(
-    spans, planes, feat_ref, point_ref, pair_ref, zg_ref, label_ref, list_ref, used_ref,
+    spans, planes, feat_ref, point_ref, zg_ref, label_ref, list_ref, used_ref,
     reply_ref, grad_ref, other_ref,
     mx_ref, my_ref, mz_ref, ma_ref, mb_ref, ax_ref, ay_ref, az_ref, ad_ref, line_ref, t_ref,
 ):
@@ -313,8 +344,7 @@
                 at = slice(top, top + height)
                 n = p * 8 + r
                 mb_ref[at, :] = ma_ref[at, :] * block[:height, n : n + 1]
-    for ref in (ax_ref, ay_ref, az_ref, ad_ref):
-        ref[...] = jnp.zeros(ref.shape, jnp.float32)
+    clear((ax_ref, ay_ref, az_ref, ad_ref))
 
     def use(i, carry):
         slot = list_ref[i]
@@ -410,25 +440,15 @@
     places = bricks * MOST
     f32 = jnp.float32
 
-    outgoing, send_slot = pl.pallas_call(
-        functools.partial(route_kernel, spans, sizes),
-        out_shape=(
-            jax.ShapeDtypeStruct((places, 1, 5 * pts), f32),
-            jax.ShapeDtypeStruct((blocks,), jnp.int32),
-        ),
-        in_specs=[SMEM, SMEM, VMEM, VMEM],
-        out_specs=(VMEM, SMEM),
-        scratch_shapes=[pltpu.SMEM((bricks,), jnp.int32)],
-        cost_estimate=pl.CostEstimate(flops=3000000*1000, bytes_accessed=1 << 18, transcendentals=0),
-        name="route",
-    )(block_cell, block_count, point_xyz, point_weight)
+    outgoing, send_slot = route(spans, sizes, point_xyz, point_weight, block_cell, block_count)
     incoming = lax.all_to_all(outgoing, AXES, split_axis=0, concat_axis=0, tiled=True)
 
     present = jnp.arange(slots, dtype=jnp.int32) < gauss_count[..., None]
     own = jnp.concatenate([gauss_mean, jnp.where(present, gauss_opacity, 0.0)[..., None, :]], axis=3)
     own = own[0].transpose(2, 0, 1, 3).reshape(4, 1, span_y, span_z * slots)
     if sizes[0] == 2:
-        stack = jnp.concatenate([own, swap(own, "gx", 0)], axis=1)
+        other = swap(own, "gx", 0)
+        stack = jnp.concatenate([own, other], axis=1)
     else:
         stack = jnp.concatenate([own, *trade(own, own, "gx")], axis=1)
     planes = stack.shape[1]
@@ -444,12 +464,11 @@
 
     table = pltpu.VMEM((planes * rows * width, LANES), f32)
     turn = pltpu.VMEM((planes * 3 * 96, LANES), f32)
-    feats, points, pairs, part, mirror, label, order, used = pl.pallas_call(
+    feats, points, part, mirror, label, order, used = pl.pallas_call(
         functools.partial(density_kernel, spans, planes),
         out_shape=(
             jax.ShapeDtypeStruct((planes * rows * width, LANES), jnp.bfloat16),
             jax.ShapeDtypeStruct(((places + 8) * 8, LANES), f32),
-            jax.ShapeDtypeStruct(((places + 8) * 32, LANES), f32),
             jax.ShapeDtypeStruct((planes, rows, wide), f32),
             jax.ShapeDtypeStruct((planes, rows, wide), f32),
             jax.ShapeDtypeStruct((places + 1,), jnp.int32),
@@ -457,8 +476,9 @@
             jax.ShapeDtypeStruct((1,), jnp.int32),
         ),
         in_specs=[VMEM, VMEM],
-        out_specs=(VMEM, VMEM, VMEM, VMEM, VMEM, SMEM, SMEM, SMEM),
+        out_specs=(VMEM, VMEM, VMEM, VMEM, SMEM, SMEM, SMEM),
         scratch_shapes=[
+            pltpu.VMEM(((places + 8) * 32, LANES), f32),
             pltpu.VMEM((5, places + 8, LANES), f32),
             pltpu.VMEM((LANES * planes * 8, LANES), f32),
             table,
@@ -497,13 +517,13 @@
             jax.ShapeDtypeStruct((4, rows, wide), f32),
             jax.ShapeDtypeStruct((planes - 1, 4, rows, wide), f32),
         ),
-        in_specs=[VMEM, VMEM, VMEM, VMEM, SMEM, SMEM, SMEM],
+        in_specs=[VMEM, VMEM, VMEM, SMEM, SMEM, SMEM],
         out_specs=(VMEM, VMEM, VMEM),
         scratch_shapes=[table] * 9
         + [pltpu.VMEM((4, planes * rows, 1, wide), f32), pltpu.VMEM((2, planes * 3 * 96, LANES), f32)],
         cost_estimate=pl.CostEstimate(flops=28000000*1000, bytes_accessed=1 << 18, transcendentals=0),
         name="gradient",
-    )(feats, points.reshape(places + 8, 8, LANES), pairs, part, label, order, used)
+    )(feats, points.reshape(places + 8, 8, LANES), part, label, order, used)
 
     answer = lax.all_to_all(reply, AXES, split_axis=0, concat_axis=0, tiled=True)
     point_out = pl.pallas_call(

time: 116 us -> 116 us (level)
  local copies, waits for them, and re-layouts: 3.46 us -> 1.88 us
    unnamed x7 -> x6, local copies, waits for them, and re-layouts: 2.89 us -> 1.3 us
  transfers between devices with their start and end apart: 17 -> 17, of which waited for: 9 -> 10; matrix products, arithmetic and copies ran while one was open for 4% -> 2% of each run, Pallas kernels for 2% -> 2%
where the time goes in v4:
time: 116 us; the launch traced here: 115 us
  Pallas kernels  42.1 us (36%)
  starting transfers between devices  32.8 us (28%)
  waiting for transfers between devices  31 us (27%)
  other arithmetic  6.58 us (6%)
  local copies, waits for them, and re-layouts  1.88 us (2%)
    ppermute x15, starting transfers between devices, swap(): return lax.ppermute(value, axis, pairs)  24.6 us
    pallas_call x1, Pallas kernels, step(): pl.pallas_call(functools.partial(gradient_kernel, spans, planes), out_sha...  24 us
    ppermute x15, waiting for transfers between devices, swap(): return lax.ppermute(value, axis, pairs)  16.2 us
    pallas_call x1, Pallas kernels, step(): pl.pallas_call(functools.partial(density_kernel, spans, planes), out_shap...  14.4 us
    all_to_all x1, waiting for transfers between devices, step(): lax.all_to_all(outgoing, AXES, split_axis=0, concat_axis=0, tiled=True)  7.86 us
    all_to_all x1, waiting for transfers between devices, step(): lax.all_to_all(reply, AXES, split_axis=0, concat_axis=0, tiled=True)  6.95 us
    all_to_all x1, starting transfers between devices, step(): lax.all_to_all(outgoing, AXES, split_axis=0, concat_axis=0, tiled=True)  4.18 us
    all_to_all x1, starting transfers between devices, step(): lax.all_to_all(reply, AXES, split_axis=0, concat_axis=0, tiled=True)  3.99 us
  transfers between devices with their start and end apart: 17, of which 10 were waited for; matrix products, arithmetic and copies ran while one was open for 2% of the time, Pallas kernels for 2%

profile of v4, /device:TPU:0, one launch (start us, length us, event | category | flops | bytes accessed | tf_op | source)
XLA Modules:
  0.0 115.2 jit_solution(11334738018946309622)
XLA Ops:
  1.5 0.9 maximum_bitcast_fusion
  2.5 3.0 %collective-permute-start = (f32[4,1,4,512]{3,2,1,0:T(4,128)S(1)}, f32[4,1,4,512]{3,2,1,0:T(4,128)S(1)}, u32[]{:S(2)}, u32[]{:S(2)}) collective-permute-start(f32[4,1,4,512]{3,2,1,0:T(4,128)S(1)} %get-tuple-element.50), channel_id=1, source_target_pairs={{0,16},{16,0},{1,17},{17,1},{2,18},{18,2},{3,19},{19,3},{4,20},{20... | collective-permute-start | bytes 98312 | tf_op jit(solution)/shard_map/ppermute | solution.py:416
  5.6 1.9 %collective-permute-done = f32[4,1,4,512]{3,2,1,0:T(4,128)S(1)} collective-permute-done((f32[4,1,4,512]{3,2,1,0:T(4,128)S(1)}, f32[4,1,4,512]{3,2,1,0:T(4,128)S(1)}, u32[]{:S(2)}, u32[]{:S(2)}) %collective-permute-start) | collective-permute-done | bytes 32800 | tf_op jit(solution)/shard_map/ppermute | solution.py:416
  7.9 1.8 %collective-permute-start.2 = (f32[4,2,1,512]{3,2,1,0:T(1,128)S(1)}, f32[4,2,1,512]{3,2,1,0:T(1,128)S(1)}, u32[]{:S(2)}, u32[]{:S(2)}) collective-permute-start(f32[4,2,1,512]{3,2,1,0:T(1,128)S(1)} %get-tuple-element.38), channel_id=1, source_target_pairs={{0,4},{4,0},{8,12},{12,8},{1,5},{5,1},{9,13},{13,9},{2,6},{6,2},{1... | collective-permute-start | bytes 49160 | tf_op jit(solution)/shard_map/ppermute | solution.py:416
  9.7 1.0 collective-permute-done.1
  10.9 4.3 %collective-permute-start.3 = (f32[4,2,6,32]{3,2,1,0:T(8,128)S(1)}, f32[4,2,6,32]{3,2,1,0:T(8,128)S(1)}, u32[]{:S(2)}, u32[]{:S(2)}) collective-permute-start(f32[4,2,6,32]{3,2,1,0:T(8,128)S(1)} %get-tuple-element.31), channel_id=1, source_target_pairs={{1,2},{2,1},{0,3},{3,0},{5,6},{6,5},{4,7},{7,4},{9,10},{10,9},{8,1... | collective-permute-start | bytes 18440 | tf_op jit(solution)/shard_map/ppermute | solution.py:416
  15.2 2.1 %route.1 = (f32[64,1,640]{2,1,0:T(1,128)}, s32[48]{0:T(128)}) custom-call(s32[48]{0:T(128)} %cell_ref.1, s32[48]{0:T(128)} %count_ref.1, f32[3,48,128]{2,1,0:T(8,128)} %bitcast.29, f32[48,128]{1,0:T(8,128)} %wt_ref.1), custom_call_target="tpu_custom_call" | custom-call | flops 3000000000 | bytes 262144 | tf_op jit(solution)/shard_map/route/pallas_call | solution.py:76
  17.3 4.2 %all-to-all-start = ((f32[64,1,640]{2,1,0:T(1,128)}), f32[64,1,640]{2,1,0:T(1,128)S(1)}, u32[]{:S(2)}, u32[]{:S(2)}) async-start(f32[64,1,640]{2,1,0:T(1,128)} %get-tuple-element.15), calls=%async_computation | async-start | bytes 327680 | tf_op jit(solution)/shard_map/all_to_all | solution.py:444
  22.4 7.9 %all-to-all-done.in_ref = f32[64,1,640]{2,1,0:T(1,128)S(1)} async-done(((f32[64,1,640]{2,1,0:T(1,128)}), f32[64,1,640]{2,1,0:T(1,128)S(1)}, u32[]{:S(2)}, u32[]{:S(2)}) %all-to-all-start) | async-done | bytes 163872 | tf_op jit(solution)/shard_map/all_to_all | solution.py:444
  30.9 14.4 %density.1 = (bf16[6912,128]{1,0:T(8,128)(2,1)}, f32[576,128]{1,0:T(8,128)}, f32[2,6,640]{2,1,0:T(8,128)}, f32[2,6,640]{2,1,0:T(8,128)}, s32[65]{0:T(128)}, /*index=5*/s32[67]{0:T(128)}, s32[1]{0:T(128)}) custom-call(f32[64,1,640]{2,1,0:T(1,128)} %copy-done, f32[4,2,6,640]{3,2,1,0:T(8,128)} %maximum_maximum_fusion.gauss_ref), custom_call_target="tpu_custom_call" | custom-call | flops 15000000512 | bytes 262144 | tf_op jit(solution)/shard_map/density/pallas_call | solution.py:467
  45.3 1.2 %collective-permute-start.5 = (f32[2,6,640]{2,1,0:T(8,128)}, f32[2,6,640]{2,1,0:T(8,128)S(1)}, u32[]{:S(2)}, u32[]{:S(2)}) collective-permute-start(f32[2,6,640]{2,1,0:T(8,128)} %get-tuple-element.19), channel_id=1, source_target_pairs={{0,16},{16,0},{1,17},{17,1},{2,18},{18,2},{3,19},{19,3},{4,20},{20... | collective-permute-start | bytes 92168 | tf_op jit(solution)/shard_map/ppermute | solution.py:416
  46.5 3.1 %collective-permute-done.5 = f32[2,6,640]{2,1,0:T(8,128)S(1)} collective-permute-done((f32[2,6,640]{2,1,0:T(8,128)}, f32[2,6,640]{2,1,0:T(8,128)S(1)}, u32[]{:S(2)}, u32[]{:S(2)}) %collective-permute-start.5) | collective-permute-done | bytes 30752 | tf_op jit(solution)/shard_map/ppermute | solution.py:416
  51.4 2.2 %collective-permute-done.6 = f32[2,2,640]{2,1,0:T(2,128)S(1)} collective-permute-done((f32[2,2,640]{2,1,0:T(2,128)S(1)}, f32[2,2,640]{2,1,0:T(2,128)S(1)}, u32[]{:S(2)}, u32[]{:S(2)}) %collective-permute-start.6) | collective-permute-done | bytes 10272 | tf_op jit(solution)/shard_map/ppermute | solution.py:416
  53.6 2.5 %collective-permute-start.8 = (f32[2,6,64]{2,1,0:T(8,128)S(1)}, f32[2,6,64]{2,1,0:T(8,128)S(1)}, u32[]{:S(2)}, u32[]{:S(2)}) collective-permute-start(f32[2,6,64]{2,1,0:T(8,128)S(1)} %get-tuple-element.26), channel_id=1, source_target_pairs={{1,2},{2,1},{0,3},{3,0},{5,6},{6,5},{4,7},{7,4},{9,10},{10,9},{8,1... | collective-permute-start | bytes 9224 | tf_op jit(solution)/shard_map/ppermute | solution.py:416
  56.2 2.9 %collective-permute-done.8 = f32[2,6,64]{2,1,0:T(8,128)S(1)} collective-permute-done((f32[2,6,64]{2,1,0:T(8,128)S(1)}, f32[2,6,64]{2,1,0:T(8,128)S(1)}, u32[]{:S(2)}, u32[]{:S(2)}) %collective-permute-start.8) | collective-permute-done | bytes 3104 | tf_op jit(solution)/shard_map/ppermute | solution.py:416
  60.5 24.0 %gradient.1 = (f32[64,4,128]{2,1,0:T(4,128)}, f32[4,6,640]{2,1,0:T(8,128)}, f32[1,4,6,640]{3,2,1,0:T(8,128)}) custom-call(bf16[6912,128]{1,0:T(8,128)(2,1)} %get-tuple-element.16.feat_ref, f32[72,8,128]{2,1,0:T(8,128)} %bitcast.30, f32[2,6,640]{2,1,0:T(8,128)} %pad_maximum_fusion.1.zg_ref, s32[65]{0:T(128)} %get-tuple-element.20.label_ref, ...), custom_call_target="tpu_custom_call" | custom-call | flops 28000000000 | bytes 262144 | tf_op jit(solution)/shard_map/gradient/pallas_call | solution.py:513
  84.5 1.0 collective-permute-start.10
  85.6 3.6 %collective-permute-done.10 = f32[4,6,640]{2,1,0:T(8,128)S(1)} collective-permute-done((f32[4,6,640]{2,1,0:T(8,128)}, f32[4,6,640]{2,1,0:T(8,128)S(1)}, u32[]{:S(2)}, u32[]{:S(2)}) %collective-permute-start.10) | collective-permute-done | bytes 61472 | tf_op jit(solution)/shard_map/ppermute | solution.py:416
  89.2 0.9 add.64
  90.2 2.3 %collective-permute-start.12 = (f32[4,1,640]{2,1,0:T(1,128)S(1)}, f32[4,1,640]{2,1,0:T(1,128)S(1)}, u32[]{:S(2)}, u32[]{:S(2)}) collective-permute-start(f32[4,1,640]{2,1,0:T(1,128)S(1)} %get-tuple-element.34), channel_id=1, source_target_pairs={{0,4},{4,0},{8,12},{12,8},{1,5},{5,1},{9,13},{13,9},{2,6},{6,2},{1... | collective-permute-start | bytes 30728 | tf_op jit(solution)/shard_map/ppermute | solution.py:416
  93.4 7.0 %collective-permute-start.13 = (f32[4,4,32]{2,1,0:T(4,128)S(1)}, f32[4,4,32]{2,1,0:T(4,128)S(1)}, u32[]{:S(2)}, u32[]{:S(2)}) collective-permute-start(f32[4,4,32]{2,1,0:T(4,128)S(1)} %get-tuple-element.43), channel_id=1, source_target_pairs={{1,2},{2,1},{0,3},{3,0},{5,6},{6,5},{4,7},{7,4},{9,10},{10,9},{8,1... | collective-permute-start | bytes 6152 | tf_op jit(solution)/shard_map/ppermute | solution.py:416
  100.5 4.0 %all-to-all-start.1 = ((f32[64,4,128]{2,1,0:T(4,128)}), f32[64,4,128]{2,1,0:T(4,128)S(1)}, u32[]{:S(2)}, u32[]{:S(2)}) async-start(f32[64,4,128]{2,1,0:T(4,128)} %get-tuple-element.23), calls=%async_computation.1 | async-start | bytes 262144 | tf_op jit(solution)/shard_map/all_to_all | solution.py:528
  106.0 6.9 %all-to-all-done.1.reply_ref = f32[64,4,128]{2,1,0:T(4,128)S(1)} async-done(((f32[64,4,128]{2,1,0:T(4,128)}), f32[64,4,128]{2,1,0:T(4,128)S(1)}, u32[]{:S(2)}, u32[]{:S(2)}) %all-to-all-start.1) | async-done | bytes 131104 | tf_op jit(solution)/shard_map/all_to_all | solution.py:528
  113.6 1.6 %pick.1 = f32[48,4,128]{2,1,0:T(4,128)} custom-call(s32[48]{0:T(128)} %get-tuple-element.14.slot_ref, f32[64,4,128]{2,1,0:T(4,128)} %copy-done.1), custom_call_target="tpu_custom_call" | custom-call | flops 2000000000 | bytes 262144 | tf_op jit(solution)/shard_map/pick/pallas_call | solution.py:529
  (56 shorter events, 9.6 us)
Async XLA Ops:
  2.5 4.9 %collective-permute-start = (f32[4,1,4,512]{3,2,1,0:T(4,128)S(1)}, f32[4,1,4,512]{3,2,1,0:T(4,128)S(1)}, u32[]{:S(2)}, u32[]{:S(2)}) collective-permute-start(f32[4,1,4,512]{3,2,1,0:T(4,128)S(1)} %get-tuple-element.50), channel_id=1, source_target_pairs={{0,16},{16,0},{1,17},{17,1},{2,18},{18,2},{3,19},{19,3},{4,20},{20... | collective-permute-start | bytes 98312 | tf_op jit(solution)/shard_map/ppermute | solution.py:416
  7.5 3.2 %collective-permute-start.1 = (f32[4,2,1,512]{3,2,1,0:T(1,128)S(1)}, f32[4,2,1,512]{3,2,1,0:T(1,128)S(1)}, u32[]{:S(2)}, u32[]{:S(2)}) collective-permute-start(f32[4,2,1,512]{3,2,1,0:T(1,128)S(1)} %get-tuple-element.37), channel_id=1, source_target_pairs={{4,8},{8,4},{0,12},{12,0},{5,9},{9,5},{1,13},{13,1},{6,10},{10,6},... | collective-permute-start | bytes 49160 | tf_op jit(solution)/shard_map/ppermute | solution.py:416
  7.9 2.8 %collective-permute-start.2 = (f32[4,2,1,512]{3,2,1,0:T(1,128)S(1)}, f32[4,2,1,512]{3,2,1,0:T(1,128)S(1)}, u32[]{:S(2)}, u32[]{:S(2)}) collective-permute-start(f32[4,2,1,512]{3,2,1,0:T(1,128)S(1)} %get-tuple-element.38), channel_id=1, source_target_pairs={{0,4},{4,0},{8,12},{12,8},{1,5},{5,1},{9,13},{13,9},{2,6},{6,2},{1... | collective-permute-start | bytes 49160 | tf_op jit(solution)/shard_map/ppermute | solution.py:416
  10.9 10.7 %collective-permute-start.3 = (f32[4,2,6,32]{3,2,1,0:T(8,128)S(1)}, f32[4,2,6,32]{3,2,1,0:T(8,128)S(1)}, u32[]{:S(2)}, u32[]{:S(2)}) collective-permute-start(f32[4,2,6,32]{3,2,1,0:T(8,128)S(1)} %get-tuple-element.31), channel_id=1, source_target_pairs={{1,2},{2,1},{0,3},{3,0},{5,6},{6,5},{4,7},{7,4},{9,10},{10,9},{8,1... | collective-permute-start | bytes 18440 | tf_op jit(solution)/shard_map/ppermute | solution.py:416
  15.2 6.4 %collective-permute-start.4 = (f32[4,2,6,32]{3,2,1,0:T(8,128)S(1)}, f32[4,2,6,32]{3,2,1,0:T(8,128)S(1)}, u32[]{:S(2)}, u32[]{:S(2)}) collective-permute-start(f32[4,2,6,32]{3,2,1,0:T(8,128)S(1)} %get-tuple-element.32), channel_id=1, source_target_pairs={{0,1},{1,0},{2,3},{3,2},{4,5},{5,4},{6,7},{7,6},{8,9},{9,8},{10,11... | collective-permute-start | bytes 18440 | tf_op jit(solution)/shard_map/ppermute | solution.py:416
  17.3 13.0 %all-to-all-start = ((f32[64,1,640]{2,1,0:T(1,128)}), f32[64,1,640]{2,1,0:T(1,128)S(1)}, u32[]{:S(2)}, u32[]{:S(2)}) async-start(f32[64,1,640]{2,1,0:T(1,128)} %get-tuple-element.15), calls=%async_computation | async-start | bytes 327680 | tf_op jit(solution)/shard_map/all_to_all | solution.py:444
  30.3 0.7 copy-start
  45.3 4.3 %collective-permute-start.5 = (f32[2,6,640]{2,1,0:T(8,128)}, f32[2,6,640]{2,1,0:T(8,128)S(1)}, u32[]{:S(2)}, u32[]{:S(2)}) collective-permute-start(f32[2,6,640]{2,1,0:T(8,128)} %get-tuple-element.19), channel_id=1, source_target_pairs={{0,16},{16,0},{1,17},{17,1},{2,18},{18,2},{3,19},{19,3},{4,20},{20... | collective-permute-start | bytes 92168 | tf_op jit(solution)/shard_map/ppermute | solution.py:416
  50.4 3.2 %collective-permute-start.6 = (f32[2,2,640]{2,1,0:T(2,128)S(1)}, f32[2,2,640]{2,1,0:T(2,128)S(1)}, u32[]{:S(2)}, u32[]{:S(2)}) collective-permute-start(f32[2,2,640]{2,1,0:T(2,128)S(1)} %get-tuple-element.46), channel_id=1, source_target_pairs={{4,8},{8,4},{0,12},{12,0},{5,9},{9,5},{1,13},{13,1},{6,10},{10,6},... | collective-permute-start | bytes 30728 | tf_op jit(solution)/shard_map/ppermute | solution.py:416
  50.5 3.1 %collective-permute-start.7 = (f32[2,2,640]{2,1,0:T(2,128)S(1)}, f32[2,2,640]{2,1,0:T(2,128)S(1)}, u32[]{:S(2)}, u32[]{:S(2)}) collective-permute-start(f32[2,2,640]{2,1,0:T(2,128)S(1)} %get-tuple-element.47), channel_id=1, source_target_pairs={{0,4},{4,0},{8,12},{12,8},{1,5},{5,1},{9,13},{13,9},{2,6},{6,2},{1... | collective-permute-start | bytes 30728 | tf_op jit(solution)/shard_map/ppermute | solution.py:416
  53.6 5.5 %collective-permute-start.8 = (f32[2,6,64]{2,1,0:T(8,128)S(1)}, f32[2,6,64]{2,1,0:T(8,128)S(1)}, u32[]{:S(2)}, u32[]{:S(2)}) collective-permute-start(f32[2,6,64]{2,1,0:T(8,128)S(1)} %get-tuple-element.26), channel_id=1, source_target_pairs={{1,2},{2,1},{0,3},{3,0},{5,6},{6,5},{4,7},{7,4},{9,10},{10,9},{8,1... | collective-permute-start | bytes 9224 | tf_op jit(solution)/shard_map/ppermute | solution.py:416
  56.1 3.7 %collective-permute-start.9 = (f32[2,6,64]{2,1,0:T(8,128)S(1)}, f32[2,6,64]{2,1,0:T(8,128)S(1)}, u32[]{:S(2)}, u32[]{:S(2)}) collective-permute-start(f32[2,6,64]{2,1,0:T(8,128)S(1)} %broadcast_select_fusion.16), channel_id=1, source_target_pairs={{0,1},{1,0},{2,3},{3,2},{4,5},{5,4},{6,7},{7,6},{8,9},{9,8},{10,11... | collective-permute-start | bytes 9224 | tf_op jit(solution)/shard_map/ppermute | solution.py:416
  60.5 44.6 %copy-start.2 = (s32[1,4,16]{2,1,0:T(4,128)S(1)}, s32[1,4,16]{2,1,0:T(4,128)}, u32[]{:S(2)}) copy-start(s32[1,4,16]{2,1,0:T(4,128)} %param.13) | copy-start | bytes 772
  84.5 4.7 %collective-permute-start.10 = (f32[4,6,640]{2,1,0:T(8,128)}, f32[4,6,640]{2,1,0:T(8,128)S(1)}, u32[]{:S(2)}, u32[]{:S(2)}) collective-permute-start(f32[4,6,640]{2,1,0:T(8,128)} %bitcast.28), channel_id=1, source_target_pairs={{0,16},{16,0},{1,17},{17,1},{2,18},{18,2},{3,19},{19,3},{4,20},{20... | collective-permute-start | bytes 184328 | tf_op jit(solution)/shard_map/ppermute | solution.py:416
  90.1 3.2 %collective-permute-start.11 = (f32[4,1,640]{2,1,0:T(1,128)S(1)}, f32[4,1,640]{2,1,0:T(1,128)S(1)}, u32[]{:S(2)}, u32[]{:S(2)}) collective-permute-start(f32[4,1,640]{2,1,0:T(1,128)S(1)} %get-tuple-element.33), channel_id=1, source_target_pairs={{4,8},{8,4},{0,12},{12,0},{5,9},{9,5},{1,13},{13,1},{6,10},{10,6},... | collective-permute-start | bytes 30728 | tf_op jit(solution)/shard_map/ppermute | solution.py:416
  90.2 3.1 %collective-permute-start.12 = (f32[4,1,640]{2,1,0:T(1,128)S(1)}, f32[4,1,640]{2,1,0:T(1,128)S(1)}, u32[]{:S(2)}, u32[]{:S(2)}) collective-permute-start(f32[4,1,640]{2,1,0:T(1,128)S(1)} %get-tuple-element.34), channel_id=1, source_target_pairs={{0,4},{4,0},{8,12},{12,8},{1,5},{5,1},{9,13},{13,9},{2,6},{6,2},{1... | collective-permute-start | bytes 30728 | tf_op jit(solution)/shard_map/ppermute | solution.py:416
  93.4 11.3 %collective-permute-start.13 = (f32[4,4,32]{2,1,0:T(4,128)S(1)}, f32[4,4,32]{2,1,0:T(4,128)S(1)}, u32[]{:S(2)}, u32[]{:S(2)}) collective-permute-start(f32[4,4,32]{2,1,0:T(4,128)S(1)} %get-tuple-element.43), channel_id=1, source_target_pairs={{1,2},{2,1},{0,3},{3,0},{5,6},{6,5},{4,7},{7,4},{9,10},{10,9},{8,1... | collective-permute-start | bytes 6152 | tf_op jit(solution)/shard_map/ppermute | solution.py:416
  100.4 4.3 %collective-permute-start.14 = (f32[4,4,32]{2,1,0:T(4,128)S(1)}, f32[4,4,32]{2,1,0:T(4,128)S(1)}, u32[]{:S(2)}, u32[]{:S(2)}) collective-permute-start(f32[4,4,32]{2,1,0:T(4,128)S(1)} %get-tuple-element.44), channel_id=1, source_target_pairs={{0,1},{1,0},{2,3},{3,2},{4,5},{5,4},{6,7},{7,6},{8,9},{9,8},{10,11... | collective-permute-start | bytes 6152 | tf_op jit(solution)/shard_map/ppermute | solution.py:416
  100.5 12.4 %all-to-all-start.1 = ((f32[64,4,128]{2,1,0:T(4,128)}), f32[64,4,128]{2,1,0:T(4,128)S(1)}, u32[]{:S(2)}, u32[]{:S(2)}) async-start(f32[64,4,128]{2,1,0:T(4,128)} %get-tuple-element.23), calls=%async_computation.1 | async-start | bytes 262144 | tf_op jit(solution)/shard_map/all_to_all | solution.py:528
  112.9 0.6 copy-start.1

commit v5 on v4

--- a/solution.py
+++ b/solution.py
@@ -175,8 +175,10 @@
     label = label_ref[slot]
     _, in_z = div_rem(label, spans[2])
     near, _ = div_rem(in_z, 4)
-    part = pair_ref[pl.ds(pl.multiple_of(slot * 32, 32), 32), :]
-    right = jnp.concatenate([part] * 4, axis=0)
+    pitch = pair_ref.shape[0] // 24
+    part = [pair_ref[pl.ds(8 * t * pitch + slot, 8, stride=pitch), :] for t in range(3)]
+    part.append(jnp.zeros((8, LANES), jnp.float32))
+    right = jnp.concatenate(part * 4, axis=0)
     right = jnp.where(lax.shift_right_logical(sub_ids(right.shape), 5) == near, right, 0.0)
     right = right.astype(jnp.bfloat16)
     left = [feat_ref[pl.ds(base, 96), :] for base in bases_of(label, spans, rows, planes)]
@@ -242,9 +244,9 @@
         one = jnp.ones_like(x)
         lines = cross_rows(x, y, at_z, True) + [one] * 3
         lines += list(pieces(0.0 - (x * x + y * y + at_z * at_z)))
-        lines += [jnp.zeros_like(x)] * 8
         for k, v in enumerate(lines):
-            pair_ref[pl.ds(g * 256 + k, 8, stride=32), :] = v
+            top = k * (slots + 8) + 8 * g
+            pair_ref[top : top + 8, :] = v
         for f, v in enumerate((x, y, z, w, one, one, one, one)):
             point_ref[pl.ds(g * 64 + f, 8, stride=8), :] = v
 
@@ -317,8 +319,8 @@
 
 
 def gradient_kernel(
-    spans, planes, feat_ref, point_ref, zg_ref, label_ref, list_ref, used_ref,
-    reply_ref, grad_ref, other_ref,
+    spans, planes, feat_ref, point_ref, zg_ref, first_ref, second_ref, label_ref, list_ref, used_ref,
+    reply_ref, grad_ref, other_ref, whole_ref,
     mx_ref, my_ref, mz_ref, ma_ref, mb_ref, ax_ref, ay_ref, az_ref, ad_ref, line_ref, t_ref,
 ):
     rows = spans[1] + 2
@@ -330,20 +332,39 @@
         both = product(feat_ref[at, :], pick)
         for f, ref in enumerate((mx_ref, my_ref, mz_ref, ma_ref)):
             ref[at, :] = both[:, f * LANES : (f + 1) * LANES]
+    tall = planes * 8
+    spare = jnp.zeros((LANES - 3 * tall, LANES), jnp.float32)
+    here = lax.axis_index("gz")
+    odd = (here & 1).astype(jnp.float32)
+    lower = jnp.where(here > 0, 1.0, 0.0)
+    upper = jnp.where(here < lax.axis_size("gz") - 1, 1.0, 0.0)
+    edge = jnp.zeros((rows, LANES - 2 * SLOTS), jnp.float32)
+    columns = []
     for c in range(chunks):
-        height = min(LANES, width - c * LANES)
         lanes = slice(c * LANES, (c + 1) * LANES)
         block = []
         for p in range(planes):
-            block.append(1.0 / (1.0 + zg_ref[p, :, lanes]))
+            total = zg_ref[p, :, lanes]
+            from_first = odd if c == 0 else 1.0 - odd
+            if c in (0, chunks - 1):
+                came = first_ref[p] * from_first + second_ref[p] * (1.0 - from_first)
+                came = came * (lower if c == 0 else upper)
+                total = total + jnp.concatenate([came, edge], axis=1)
+            total = 1.0 + total
+            if p == 0:
+                whole_ref[:, lanes] = total
+            block.append(1.0 / total)
             block.append(jnp.ones((8 - rows, LANES), jnp.float32))
-        block = jnp.concatenate(block, axis=0).T
-        for p in range(planes):
-            for r in range(rows):
-                top = (p * rows + r) * width + c * LANES
-                at = slice(top, top + height)
-                n = p * 8 + r
-                mb_ref[at, :] = ma_ref[at, :] * block[:height, n : n + 1]
+        block = jnp.concatenate(block, axis=0)
+        columns.append(jnp.concatenate([*pieces(block), spare], axis=0).T.astype(jnp.bfloat16))
+    columns = jnp.concatenate(columns, axis=0)[:width]
+    line = sub_ids((LANES, LANES))
+    for p in range(planes):
+        for r in range(rows):
+            n = p * 8 + r
+            at = slice((p * rows + r) * width, (p * rows + r + 1) * width)
+            hit = (line == n) | (line == n + tall) | (line == n + 2 * tall)
+            mb_ref[at, :] = ma_ref[at, :] * product(columns, jnp.where(hit, 1.0, 0.0).astype(jnp.bfloat16))
     clear((ax_ref, ay_ref, az_ref, ad_ref))
 
     def use(i, carry):
@@ -406,6 +427,17 @@
     lax.fori_loop(0, out_ref.shape[0], one, 0, unroll=4)
 
 
+def pick(send_slot, answer):
+    return pl.pallas_call(
+        pick_kernel,
+        out_shape=jax.ShapeDtypeStruct((send_slot.shape[0],) + answer.shape[1:], jnp.float32),
+        in_specs=[SMEM, VMEM],
+        out_specs=VMEM,
+        cost_estimate=pl.CostEstimate(flops=2000000000, bytes_accessed=1 << 18, transcendentals=0),
+        name="pick",
+    )(send_slot, answer)
+
+
 def swap(value, axis, odd):
     count = lax.axis_size(axis)
     pairs = []
@@ -416,12 +448,19 @@
     return lax.ppermute(value, axis, pairs)
 
 
+def trade_raw(low, high, axis):
+    even = lax.axis_index(axis) % 2 == 0
+    first = swap(jnp.where(even, high, low), axis, 0)
+    if lax.axis_size(axis) == 2:
+        return first, jnp.zeros_like(first)
+    return first, swap(jnp.where(even, low, high), axis, 1)
+
+
 def trade(low, high, axis):
     count = lax.axis_size(axis)
     here = lax.axis_index(axis)
     even = here % 2 == 0
-    first = swap(jnp.where(even, high, low), axis, 0)
-    second = swap(jnp.where(even, low, high), axis, 1) if count > 2 else jnp.zeros_like(first)
+    first, second = trade_raw(low, high, axis)
     from_low = jnp.where(here > 0, jnp.where(even, second, first), 0.0)
     from_high = jnp.where(here < count - 1, jnp.where(even, first, second), 0.0)
     return from_low, from_high
@@ -430,7 +469,7 @@
 def step(
     point_xyz, point_weight, block_cell, block_count, gauss_mean, gauss_opacity, gauss_count
 ):
-    blocks, _, pts = point_xyz.shape
+    _, _, pts = point_xyz.shape
     span_x, span_y, span_z, _, slots = gauss_mean.shape
     spans = (span_x, span_y, span_z)
     sizes = tuple(lax.axis_size(a) for a in AXES)
@@ -478,7 +517,7 @@
         in_specs=[VMEM, VMEM],
         out_specs=(VMEM, VMEM, VMEM, VMEM, SMEM, SMEM, SMEM),
         scratch_shapes=[
-            pltpu.VMEM(((places + 8) * 32, LANES), f32),
+            pltpu.VMEM((24 * (places + 8), LANES), f32),
             pltpu.VMEM((5, places + 8, LANES), f32),
             pltpu.VMEM((LANES * planes * 8, LANES), f32),
             table,
@@ -500,41 +539,26 @@
     low, high = trade(part[:, :2], part[:, -2:], "gy")
     part = jnp.concatenate([part[:, :2] + low, part[:, 2:-2], part[:, -2:] + high], axis=1)
     edge = 2 * slots
-    low, high = trade(part[..., :edge], part[..., width - edge : width], "gz")
-    part = jnp.concatenate(
-        [
-            part[..., :edge] + low,
-            part[..., edge : width - edge],
-            part[..., width - edge : width] + high,
-            jnp.zeros((planes, rows, wide - width), f32),
-        ],
-        axis=2,
-    )
-    reply, grad, other = pl.pallas_call(
+    first, second = trade_raw(part[..., :edge], part[..., width - edge : width], "gz")
+
+    reply, grad, other, whole = pl.pallas_call(
         functools.partial(gradient_kernel, spans, planes),
         out_shape=(
             jax.ShapeDtypeStruct((places, 4, LANES), f32),
             jax.ShapeDtypeStruct((4, rows, wide), f32),
             jax.ShapeDtypeStruct((planes - 1, 4, rows, wide), f32),
+            jax.ShapeDtypeStruct((rows, wide), f32),
         ),
-        in_specs=[VMEM, VMEM, VMEM, SMEM, SMEM, SMEM],
-        out_specs=(VMEM, VMEM, VMEM),
+        in_specs=[VMEM, VMEM, VMEM, VMEM, VMEM, SMEM, SMEM, SMEM],
+        out_specs=(VMEM, VMEM, VMEM, VMEM),
         scratch_shapes=[table] * 9
         + [pltpu.VMEM((4, planes * rows, 1, wide), f32), pltpu.VMEM((2, planes * 3 * 96, LANES), f32)],
         cost_estimate=pl.CostEstimate(flops=28000000*1000, bytes_accessed=1 << 18, transcendentals=0),
         name="gradient",
-    )(feats, points.reshape(places + 8, 8, LANES), part, label, order, used)
+    )(feats, points.reshape(places + 8, 8, LANES), part, first, second, label, order, used)
 
     answer = lax.all_to_all(reply, AXES, split_axis=0, concat_axis=0, tiled=True)
-    point_out = pl.pallas_call(
-        pick_kernel,
-        out_shape=jax.ShapeDtypeStruct((blocks, 4, pts), f32),
-        in_specs=[SMEM, VMEM],
-        out_specs=VMEM,
-        cost_estimate=pl.CostEstimate(flops=2000000*1000, bytes_accessed=1 << 18, transcendentals=0),
-        name="pick",
-    )(send_slot, answer)
-
+    point_out = pick(send_slot, answer)
     if sizes[0] == 2:
         grad = grad + swap(other[0], "gx", 0)
     else:
@@ -554,7 +578,7 @@
         axis=2,
     )
     grad = grad.reshape(4, span_y, span_z, slots).transpose(1, 2, 0, 3)[None]
-    total_g = 1.0 + part[0, 1:-1, slots : width - slots].reshape(1, span_y, span_z, slots)
+    total_g = whole[1:-1, slots : width - slots].reshape(1, span_y, span_z, slots)
     opacity = jnp.where(
         present,
         kernel_width * sharp - kernel_width * jnp.log(total_g) - kernel_width * grad[..., 3, :],

time: 116 us -> 116 us (level)
  transfers between devices with their start and end apart: 17 -> 17, of which waited for: 10 -> 10; matrix products, arithmetic and copies ran while one was open for 2% -> 3% of each run, Pallas kernels for 2% -> 2%
where the time goes in v5:
time: 116 us
  Pallas kernels  41.9 us (36%)
  starting transfers between devices  32.8 us (28%)
  waiting for transfers between devices  31 us (27%)
  other arithmetic  6.52 us (6%)
  local copies, waits for them, and re-layouts  2.47 us (2%)
    ppermute x15, starting transfers between devices, swap(): return lax.ppermute(value, axis, pairs)  24.6 us
    pallas_call x1, Pallas kernels, step(): pl.pallas_call(functools.partial(gradient_kernel, spans, planes), out_sha...  24.4 us
    ppermute x15, waiting for transfers between devices, swap(): return lax.ppermute(value, axis, pairs)  16.2 us
    pallas_call x1, Pallas kernels, step(): pl.pallas_call(functools.partial(density_kernel, spans, planes), out_shap...  13.7 us
    all_to_all x1, waiting for transfers between devices, step(): lax.all_to_all(outgoing, AXES, split_axis=0, concat_axis=0, tiled=True)  7.86 us
    all_to_all x1, waiting for transfers between devices, step(): lax.all_to_all(reply, AXES, split_axis=0, concat_axis=0, tiled=True)  6.95 us
    all_to_all x1, starting transfers between devices, step(): lax.all_to_all(outgoing, AXES, split_axis=0, concat_axis=0, tiled=True)  4.18 us
    all_to_all x1, starting transfers between devices, step(): lax.all_to_all(reply, AXES, split_axis=0, concat_axis=0, tiled=True)  3.99 us
  transfers between devices with their start and end apart: 17, of which 10 were waited for; matrix products, arithmetic and copies ran while one was open for 3% of the time, Pallas kernels for 2%

profile of v5, /device:TPU:0, one launch (start us, length us, event | category | flops | bytes accessed | tf_op | source)
XLA Modules:
  0.0 115.5 jit_solution(1146953410678823159)
XLA Ops:
  1.5 0.9 maximum_bitcast_fusion
  2.5 3.0 %collective-permute-start = (f32[4,1,4,512]{3,2,1,0:T(4,128)S(1)}, f32[4,1,4,512]{3,2,1,0:T(4,128)S(1)}, u32[]{:S(2)}, u32[]{:S(2)}) collective-permute-start(f32[4,1,4,512]{3,2,1,0:T(4,128)S(1)} %get-tuple-element.51), channel_id=1, source_target_pairs={{0,16},{16,0},{1,17},{17,1},{2,18},{18,2},{3,19},{19,3},{4,20},{20... | collective-permute-start | bytes 98312 | tf_op jit(solution)/shard_map/ppermute | solution.py:448
  5.6 1.9 %collective-permute-done = f32[4,1,4,512]{3,2,1,0:T(4,128)S(1)} collective-permute-done((f32[4,1,4,512]{3,2,1,0:T(4,128)S(1)}, f32[4,1,4,512]{3,2,1,0:T(4,128)S(1)}, u32[]{:S(2)}, u32[]{:S(2)}) %collective-permute-start) | collective-permute-done | bytes 32800 | tf_op jit(solution)/shard_map/ppermute | solution.py:448
  7.9 1.8 %collective-permute-start.2 = (f32[4,2,1,512]{3,2,1,0:T(1,128)S(1)}, f32[4,2,1,512]{3,2,1,0:T(1,128)S(1)}, u32[]{:S(2)}, u32[]{:S(2)}) collective-permute-start(f32[4,2,1,512]{3,2,1,0:T(1,128)S(1)} %get-tuple-element.37), channel_id=1, source_target_pairs={{0,4},{4,0},{8,12},{12,8},{1,5},{5,1},{9,13},{13,9},{2,6},{6,2},{1... | collective-permute-start | bytes 49160 | tf_op jit(solution)/shard_map/ppermute | solution.py:448
  9.7 1.0 collective-permute-done.1
  10.9 4.3 %collective-permute-start.3 = (f32[4,2,6,32]{3,2,1,0:T(8,128)S(1)}, f32[4,2,6,32]{3,2,1,0:T(8,128)S(1)}, u32[]{:S(2)}, u32[]{:S(2)}) collective-permute-start(f32[4,2,6,32]{3,2,1,0:T(8,128)S(1)} %get-tuple-element.30), channel_id=1, source_target_pairs={{1,2},{2,1},{0,3},{3,0},{5,6},{6,5},{4,7},{7,4},{9,10},{10,9},{8,1... | collective-permute-start | bytes 18440 | tf_op jit(solution)/shard_map/ppermute | solution.py:448
  15.2 2.1 %route.1 = (f32[64,1,640]{2,1,0:T(1,128)}, s32[48]{0:T(128)}) custom-call(s32[48]{0:T(128)} %cell_ref.1, s32[48]{0:T(128)} %count_ref.1, f32[3,48,128]{2,1,0:T(8,128)} %bitcast.29, f32[48,128]{1,0:T(8,128)} %wt_ref.1), custom_call_target="tpu_custom_call" | custom-call | flops 3000000000 | bytes 262144 | tf_op jit(solution)/shard_map/route/pallas_call | solution.py:76
  17.3 4.2 %all-to-all-start = ((f32[64,1,640]{2,1,0:T(1,128)}), f32[64,1,640]{2,1,0:T(1,128)S(1)}, u32[]{:S(2)}, u32[]{:S(2)}) async-start(f32[64,1,640]{2,1,0:T(1,128)} %get-tuple-element.16), calls=%async_computation | async-start | bytes 327680 | tf_op jit(solution)/shard_map/all_to_all | solution.py:483
  22.4 7.9 %all-to-all-done.in_ref = f32[64,1,640]{2,1,0:T(1,128)S(1)} async-done(((f32[64,1,640]{2,1,0:T(1,128)}), f32[64,1,640]{2,1,0:T(1,128)S(1)}, u32[]{:S(2)}, u32[]{:S(2)}) %all-to-all-start) | async-done | bytes 163872 | tf_op jit(solution)/shard_map/all_to_all | solution.py:483
  31.0 13.7 %density.1 = (bf16[6912,128]{1,0:T(8,128)(2,1)}, f32[576,128]{1,0:T(8,128)}, f32[2,6,640]{2,1,0:T(8,128)}, f32[2,6,640]{2,1,0:T(8,128)}, s32[65]{0:T(128)}, /*index=5*/s32[67]{0:T(128)}, s32[1]{0:T(128)}) custom-call(f32[64,1,640]{2,1,0:T(1,128)} %copy-done, f32[4,2,6,640]{3,2,1,0:T(8,128)} %maximum_maximum_fusion.gauss_ref), custom_call_target="tpu_custom_call" | custom-call | flops 15000000512 | bytes 262144 | tf_op jit(solution)/shard_map/density/pallas_call | solution.py:506
  44.6 1.2 %collective-permute-start.5 = (f32[2,6,640]{2,1,0:T(8,128)}, f32[2,6,640]{2,1,0:T(8,128)S(1)}, u32[]{:S(2)}, u32[]{:S(2)}) collective-permute-start(f32[2,6,640]{2,1,0:T(8,128)} %get-tuple-element.20), channel_id=1, source_target_pairs={{0,16},{16,0},{1,17},{17,1},{2,18},{18,2},{3,19},{19,3},{4,20},{20... | collective-permute-start | bytes 92168 | tf_op jit(solution)/shard_map/ppermute | solution.py:448
  45.8 3.1 %collective-permute-done.5 = f32[2,6,640]{2,1,0:T(8,128)S(1)} collective-permute-done((f32[2,6,640]{2,1,0:T(8,128)}, f32[2,6,640]{2,1,0:T(8,128)S(1)}, u32[]{:S(2)}, u32[]{:S(2)}) %collective-permute-start.5) | collective-permute-done | bytes 30752 | tf_op jit(solution)/shard_map/ppermute | solution.py:448
  50.7 2.2 %collective-permute-done.6 = f32[2,2,640]{2,1,0:T(2,128)S(1)} collective-permute-done((f32[2,2,640]{2,1,0:T(2,128)S(1)}, f32[2,2,640]{2,1,0:T(2,128)S(1)}, u32[]{:S(2)}, u32[]{:S(2)}) %collective-permute-start.6) | collective-permute-done | bytes 10272 | tf_op jit(solution)/shard_map/ppermute | solution.py:448
  53.0 2.5 %collective-permute-start.9 = (f32[2,6,64]{2,1,0:T(8,128)S(1)}, f32[2,6,64]{2,1,0:T(8,128)S(1)}, u32[]{:S(2)}, u32[]{:S(2)}) collective-permute-start(f32[2,6,64]{2,1,0:T(8,128)S(1)} %get-tuple-element.44), channel_id=1, source_target_pairs={{1,2},{2,1},{0,3},{3,0},{5,6},{6,5},{4,7},{7,4},{9,10},{10,9},{8,1... | collective-permute-start | bytes 9224 | tf_op jit(solution)/shard_map/ppermute | solution.py:448
  55.5 3.0 %collective-permute-done.9.second_ref = f32[2,6,64]{2,1,0:T(8,128)S(1)} collective-permute-done((f32[2,6,64]{2,1,0:T(8,128)S(1)}, f32[2,6,64]{2,1,0:T(8,128)S(1)}, u32[]{:S(2)}, u32[]{:S(2)}) %collective-permute-start.9) | collective-permute-done | bytes 3104 | tf_op jit(solution)/shard_map/ppermute | solution.py:448
  59.7 24.4 %gradient.1 = (f32[64,4,128]{2,1,0:T(4,128)}, f32[4,6,640]{2,1,0:T(8,128)}, f32[1,4,6,640]{3,2,1,0:T(8,128)}, f32[6,640]{1,0:T(8,128)}) custom-call(bf16[6912,128]{1,0:T(8,128)(2,1)} %get-tuple-element.17.feat_ref, f32[72,8,128]{2,1,0:T(8,128)} %bitcast.30, f32[2,6,640]{2,1,0:T(8,128)} %copy-done.2, f32[2,6,64]{2,1,0:T(8,128)} %copy-done.5, ...), custom_call_target="tpu_custom_call" | custom-call | flops 28000000000 | bytes 262144 | tf_op jit(solution)/shard_map/gradient/pallas_call | solution.py:544
  84.1 1.1 collective-permute-start.10
  85.2 3.6 %collective-permute-done.10 = f32[4,6,640]{2,1,0:T(8,128)S(1)} collective-permute-done((f32[4,6,640]{2,1,0:T(8,128)}, f32[4,6,640]{2,1,0:T(8,128)S(1)}, u32[]{:S(2)}, u32[]{:S(2)}) %collective-permute-start.10) | collective-permute-done | bytes 61472 | tf_op jit(solution)/shard_map/ppermute | solution.py:448
  88.8 0.9 add.45
  89.8 2.3 %collective-permute-start.12 = (f32[4,1,640]{2,1,0:T(1,128)S(1)}, f32[4,1,640]{2,1,0:T(1,128)S(1)}, u32[]{:S(2)}, u32[]{:S(2)}) collective-permute-start(f32[4,1,640]{2,1,0:T(1,128)S(1)} %get-tuple-element.33), channel_id=1, source_target_pairs={{0,4},{4,0},{8,12},{12,8},{1,5},{5,1},{9,13},{13,9},{2,6},{6,2},{1... | collective-permute-start | bytes 30728 | tf_op jit(solution)/shard_map/ppermute | solution.py:448
  93.0 7.0 %collective-permute-start.13 = (f32[4,4,32]{2,1,0:T(4,128)S(1)}, f32[4,4,32]{2,1,0:T(4,128)S(1)}, u32[]{:S(2)}, u32[]{:S(2)}) collective-permute-start(f32[4,4,32]{2,1,0:T(4,128)S(1)} %get-tuple-element.42), channel_id=1, source_target_pairs={{1,2},{2,1},{0,3},{3,0},{5,6},{6,5},{4,7},{7,4},{9,10},{10,9},{8,1... | collective-permute-start | bytes 6152 | tf_op jit(solution)/shard_map/ppermute | solution.py:448
  100.9 4.0 %all-to-all-start.1 = ((f32[64,4,128]{2,1,0:T(4,128)}), f32[64,4,128]{2,1,0:T(4,128)S(1)}, u32[]{:S(2)}, u32[]{:S(2)}) async-start(f32[64,4,128]{2,1,0:T(4,128)} %get-tuple-element.24), calls=%async_computation.1 | async-start | bytes 262144 | tf_op jit(solution)/shard_map/all_to_all | solution.py:560
  106.3 6.9 %all-to-all-done.1.reply_ref = f32[64,4,128]{2,1,0:T(4,128)S(1)} async-done(((f32[64,4,128]{2,1,0:T(4,128)}), f32[64,4,128]{2,1,0:T(4,128)S(1)}, u32[]{:S(2)}, u32[]{:S(2)}) %all-to-all-start.1) | async-done | bytes 131104 | tf_op jit(solution)/shard_map/all_to_all | solution.py:560
  113.9 1.6 %pick.1 = f32[48,4,128]{2,1,0:T(4,128)} custom-call(s32[48]{0:T(128)} %get-tuple-element.15.slot_ref, f32[64,4,128]{2,1,0:T(4,128)} %copy-done.1), custom_call_target="tpu_custom_call" | custom-call | flops 2000000000 | bytes 262144 | tf_op jit(solution)/shard_map/pick/pallas_call | solution.py:431
  (58 shorter events, 10.1 us)
Async XLA Ops:
  2.5 4.9 %collective-permute-start = (f32[4,1,4,512]{3,2,1,0:T(4,128)S(1)}, f32[4,1,4,512]{3,2,1,0:T(4,128)S(1)}, u32[]{:S(2)}, u32[]{:S(2)}) collective-permute-start(f32[4,1,4,512]{3,2,1,0:T(4,128)S(1)} %get-tuple-element.51), channel_id=1, source_target_pairs={{0,16},{16,0},{1,17},{17,1},{2,18},{18,2},{3,19},{19,3},{4,20},{20... | collective-permute-start | bytes 98312 | tf_op jit(solution)/shard_map/ppermute | solution.py:448
  7.5 3.2 %collective-permute-start.1 = (f32[4,2,1,512]{3,2,1,0:T(1,128)S(1)}, f32[4,2,1,512]{3,2,1,0:T(1,128)S(1)}, u32[]{:S(2)}, u32[]{:S(2)}) collective-permute-start(f32[4,2,1,512]{3,2,1,0:T(1,128)S(1)} %get-tuple-element.36), channel_id=1, source_target_pairs={{4,8},{8,4},{0,12},{12,0},{5,9},{9,5},{1,13},{13,1},{6,10},{10,6},... | collective-permute-start | bytes 49160 | tf_op jit(solution)/shard_map/ppermute | solution.py:448
  7.9 2.8 %collective-permute-start.2 = (f32[4,2,1,512]{3,2,1,0:T(1,128)S(1)}, f32[4,2,1,512]{3,2,1,0:T(1,128)S(1)}, u32[]{:S(2)}, u32[]{:S(2)}) collective-permute-start(f32[4,2,1,512]{3,2,1,0:T(1,128)S(1)} %get-tuple-element.37), channel_id=1, source_target_pairs={{0,4},{4,0},{8,12},{12,8},{1,5},{5,1},{9,13},{13,9},{2,6},{6,2},{1... | collective-permute-start | bytes 49160 | tf_op jit(solution)/shard_map/ppermute | solution.py:448
  10.9 10.7 %collective-permute-start.3 = (f32[4,2,6,32]{3,2,1,0:T(8,128)S(1)}, f32[4,2,6,32]{3,2,1,0:T(8,128)S(1)}, u32[]{:S(2)}, u32[]{:S(2)}) collective-permute-start(f32[4,2,6,32]{3,2,1,0:T(8,128)S(1)} %get-tuple-element.30), channel_id=1, source_target_pairs={{1,2},{2,1},{0,3},{3,0},{5,6},{6,5},{4,7},{7,4},{9,10},{10,9},{8,1... | collective-permute-start | bytes 18440 | tf_op jit(solution)/shard_map/ppermute | solution.py:448
  15.2 6.4 %collective-permute-start.4 = (f32[4,2,6,32]{3,2,1,0:T(8,128)S(1)}, f32[4,2,6,32]{3,2,1,0:T(8,128)S(1)}, u32[]{:S(2)}, u32[]{:S(2)}) collective-permute-start(f32[4,2,6,32]{3,2,1,0:T(8,128)S(1)} %get-tuple-element.31), channel_id=1, source_target_pairs={{0,1},{1,0},{2,3},{3,2},{4,5},{5,4},{6,7},{7,6},{8,9},{9,8},{10,11... | collective-permute-start | bytes 18440 | tf_op jit(solution)/shard_map/ppermute | solution.py:448
  17.3 13.0 %all-to-all-start = ((f32[64,1,640]{2,1,0:T(1,128)}), f32[64,1,640]{2,1,0:T(1,128)S(1)}, u32[]{:S(2)}, u32[]{:S(2)}) async-start(f32[64,1,640]{2,1,0:T(1,128)} %get-tuple-element.16), calls=%async_computation | async-start | bytes 327680 | tf_op jit(solution)/shard_map/all_to_all | solution.py:483
  30.3 0.7 copy-start
  44.6 4.3 %collective-permute-start.5 = (f32[2,6,640]{2,1,0:T(8,128)}, f32[2,6,640]{2,1,0:T(8,128)S(1)}, u32[]{:S(2)}, u32[]{:S(2)}) collective-permute-start(f32[2,6,640]{2,1,0:T(8,128)} %get-tuple-element.20), channel_id=1, source_target_pairs={{0,16},{16,0},{1,17},{17,1},{2,18},{18,2},{3,19},{19,3},{4,20},{20... | collective-permute-start | bytes 92168 | tf_op jit(solution)/shard_map/ppermute | solution.py:448
  49.7 3.2 %collective-permute-start.6 = (f32[2,2,640]{2,1,0:T(2,128)S(1)}, f32[2,2,640]{2,1,0:T(2,128)S(1)}, u32[]{:S(2)}, u32[]{:S(2)}) collective-permute-start(f32[2,2,640]{2,1,0:T(2,128)S(1)} %get-tuple-element.47), channel_id=1, source_target_pairs={{4,8},{8,4},{0,12},{12,0},{5,9},{9,5},{1,13},{13,1},{6,10},{10,6},... | collective-permute-start | bytes 30728 | tf_op jit(solution)/shard_map/ppermute | solution.py:448
  49.8 3.1 %collective-permute-start.7 = (f32[2,2,640]{2,1,0:T(2,128)S(1)}, f32[2,2,640]{2,1,0:T(2,128)S(1)}, u32[]{:S(2)}, u32[]{:S(2)}) collective-permute-start(f32[2,2,640]{2,1,0:T(2,128)S(1)} %get-tuple-element.48), channel_id=1, source_target_pairs={{0,4},{4,0},{8,12},{12,8},{1,5},{5,1},{9,13},{13,9},{2,6},{6,2},{1... | collective-permute-start | bytes 30728 | tf_op jit(solution)/shard_map/ppermute | solution.py:448
  52.9 6.2 %copy-start.2 = (f32[2,6,640]{2,1,0:T(8,128)}, f32[2,6,640]{2,1,0:T(8,128)S(1)}, u32[]{:S(2)}) copy-start(f32[2,6,640]{2,1,0:T(8,128)S(1)} %pad_maximum_fusion.1.zg_ref) | copy-start | bytes 92164
  53.0 5.5 %collective-permute-start.9 = (f32[2,6,64]{2,1,0:T(8,128)S(1)}, f32[2,6,64]{2,1,0:T(8,128)S(1)}, u32[]{:S(2)}, u32[]{:S(2)}) collective-permute-start(f32[2,6,64]{2,1,0:T(8,128)S(1)} %get-tuple-element.44), channel_id=1, source_target_pairs={{1,2},{2,1},{0,3},{3,0},{5,6},{6,5},{4,7},{7,4},{9,10},{10,9},{8,1... | collective-permute-start | bytes 9224 | tf_op jit(solution)/shard_map/ppermute | solution.py:448
  55.5 3.7 %collective-permute-start.8 = (f32[2,6,64]{2,1,0:T(8,128)S(1)}, f32[2,6,64]{2,1,0:T(8,128)S(1)}, u32[]{:S(2)}, u32[]{:S(2)}) collective-permute-start(f32[2,6,64]{2,1,0:T(8,128)S(1)} %get-tuple-element.45), channel_id=1, source_target_pairs={{0,1},{1,0},{2,3},{3,2},{4,5},{5,4},{6,7},{7,6},{8,9},{9,8},{10,11... | collective-permute-start | bytes 9224 | tf_op jit(solution)/shard_map/ppermute | solution.py:448
  58.5 0.6 copy-start.4
  59.1 0.6 copy-start.5
  59.7 45.7 %copy-start.3 = (s32[1,4,16]{2,1,0:T(4,128)S(1)}, s32[1,4,16]{2,1,0:T(4,128)}, u32[]{:S(2)}) copy-start(s32[1,4,16]{2,1,0:T(4,128)} %param.13) | copy-start | bytes 772
  84.1 4.7 %collective-permute-start.10 = (f32[4,6,640]{2,1,0:T(8,128)}, f32[4,6,640]{2,1,0:T(8,128)S(1)}, u32[]{:S(2)}, u32[]{:S(2)}) collective-permute-start(f32[4,6,640]{2,1,0:T(8,128)} %bitcast.28), channel_id=1, source_target_pairs={{0,16},{16,0},{1,17},{17,1},{2,18},{18,2},{3,19},{19,3},{4,20},{20... | collective-permute-start | bytes 184328 | tf_op jit(solution)/shard_map/ppermute | solution.py:448
  89.7 3.2 %collective-permute-start.11 = (f32[4,1,640]{2,1,0:T(1,128)S(1)}, f32[4,1,640]{2,1,0:T(1,128)S(1)}, u32[]{:S(2)}, u32[]{:S(2)}) collective-permute-start(f32[4,1,640]{2,1,0:T(1,128)S(1)} %get-tuple-element.32), channel_id=1, source_target_pairs={{4,8},{8,4},{0,12},{12,0},{5,9},{9,5},{1,13},{13,1},{6,10},{10,6},... | collective-permute-start | bytes 30728 | tf_op jit(solution)/shard_map/ppermute | solution.py:448
  89.8 3.1 %collective-permute-start.12 = (f32[4,1,640]{2,1,0:T(1,128)S(1)}, f32[4,1,640]{2,1,0:T(1,128)S(1)}, u32[]{:S(2)}, u32[]{:S(2)}) collective-permute-start(f32[4,1,640]{2,1,0:T(1,128)S(1)} %get-tuple-element.33), channel_id=1, source_target_pairs={{0,4},{4,0},{8,12},{12,8},{1,5},{5,1},{9,13},{13,9},{2,6},{6,2},{1... | collective-permute-start | bytes 30728 | tf_op jit(solution)/shard_map/ppermute | solution.py:448
  93.0 12.0 %collective-permute-start.13 = (f32[4,4,32]{2,1,0:T(4,128)S(1)}, f32[4,4,32]{2,1,0:T(4,128)S(1)}, u32[]{:S(2)}, u32[]{:S(2)}) collective-permute-start(f32[4,4,32]{2,1,0:T(4,128)S(1)} %get-tuple-element.42), channel_id=1, source_target_pairs={{1,2},{2,1},{0,3},{3,0},{5,6},{6,5},{4,7},{7,4},{9,10},{10,9},{8,1... | collective-permute-start | bytes 6152 | tf_op jit(solution)/shard_map/ppermute | solution.py:448
  100.1 5.0 %collective-permute-start.14 = (f32[4,4,32]{2,1,0:T(4,128)S(1)}, f32[4,4,32]{2,1,0:T(4,128)S(1)}, u32[]{:S(2)}, u32[]{:S(2)}) collective-permute-start(f32[4,4,32]{2,1,0:T(4,128)S(1)} %get-tuple-element.43), channel_id=1, source_target_pairs={{0,1},{1,0},{2,3},{3,2},{4,5},{5,4},{6,7},{7,6},{8,9},{9,8},{10,11... | collective-permute-start | bytes 6152 | tf_op jit(solution)/shard_map/ppermute | solution.py:448
  100.9 12.4 %all-to-all-start.1 = ((f32[64,4,128]{2,1,0:T(4,128)}), f32[64,4,128]{2,1,0:T(4,128)S(1)}, u32[]{:S(2)}, u32[]{:S(2)}) async-start(f32[64,4,128]{2,1,0:T(4,128)} %get-tuple-element.24), calls=%async_computation.1 | async-start | bytes 262144 | tf_op jit(solution)/shard_map/all_to_all | solution.py:560
  113.3 0.6 copy-start.1

commit v6 on v5

--- a/solution.py
+++ b/solution.py
@@ -188,16 +188,15 @@
 def in_turn(used, list_ref, ta_ref, tb_ref, load, use):
     load(list_ref[0], ta_ref)
 
-    def two(i, carry):
-        first = list_ref[2 * i]
-        second = list_ref[2 * i + 1]
-        load(second, tb_ref)
-        use(first, ta_ref)
-        load(list_ref[2 * i + 2], ta_ref)
-        use(second, tb_ref)
-        return carry
-
-    lax.fori_loop(0, lax.shift_right_logical(used + 1, 1), two, 0)
+    def four(i, carry):
+        turn = [list_ref[4 * i + n] for n in range(5)]
+        tables = (ta_ref, tb_ref)
+        for n in range(4):
+            load(turn[n + 1], tables[(n + 1) % 2])
+            use(turn[n], tables[n % 2])
+        return carry
+
+    lax.fori_loop(0, lax.shift_right_logical(used + 3, 2), four, 0)
 
 
 def density_kernel(
@@ -228,7 +227,7 @@
         return n + (label_ref[s] >= 0).astype(jnp.int32)
 
     used = lax.fori_loop(0, slots, order, 0)
-    for n in range(3):
+    for n in range(5):
         list_ref[used + n] = slots
     used_ref[0] = used
 
@@ -365,7 +364,8 @@
             at = slice((p * rows + r) * width, (p * rows + r + 1) * width)
             hit = (line == n) | (line == n + tall) | (line == n + 2 * tall)
             mb_ref[at, :] = ma_ref[at, :] * product(columns, jnp.where(hit, 1.0, 0.0).astype(jnp.bfloat16))
-    clear((ax_ref, ay_ref, az_ref, ad_ref))
+            for ref in (ax_ref, ay_ref, az_ref, ad_ref):
+                ref[at, :] = jnp.zeros((width, LANES), jnp.float32)
 
     def use(i, carry):
         slot = list_ref[i]
@@ -511,7 +511,7 @@
             jax.ShapeDtypeStruct((planes, rows, wide), f32),
             jax.ShapeDtypeStruct((planes, rows, wide), f32),
             jax.ShapeDtypeStruct((places + 1,), jnp.int32),
-            jax.ShapeDtypeStruct((places + 3,), jnp.int32),
+            jax.ShapeDtypeStruct((places + 5,), jnp.int32),
             jax.ShapeDtypeStruct((1,), jnp.int32),
         ),
         in_specs=[VMEM, VMEM],

time: 116 us -> 116 us (level)
  no operation moved by 1% of the time
where the time goes in v6:
time: 116 us; the launch traced here: 115 us
  Pallas kernels  41.7 us (36%)
  starting transfers between devices  32.3 us (28%)
  waiting for transfers between devices  31.2 us (27%)
  other arithmetic  6.52 us (6%)
  local copies, waits for them, and re-layouts  2.47 us (2%)
    pallas_call x1, Pallas kernels, step(): pl.pallas_call(functools.partial(gradient_kernel, spans, planes), out_sha...  24.3 us
    ppermute x15, starting transfers between devices, swap(): return lax.ppermute(value, axis, pairs)  24.1 us
    ppermute x15, waiting for transfers between devices, swap(): return lax.ppermute(value, axis, pairs)  16.4 us
    pallas_call x1, Pallas kernels, step(): pl.pallas_call(functools.partial(density_kernel, spans, planes), out_shap...  13.6 us
    all_to_all x1, waiting for transfers between devices, step(): lax.all_to_all(outgoing, AXES, split_axis=0, concat_axis=0, tiled=True)  7.86 us
    all_to_all x1, waiting for transfers between devices, step(): lax.all_to_all(reply, AXES, split_axis=0, concat_axis=0, tiled=True)  6.95 us
    all_to_all x1, starting transfers between devices, step(): lax.all_to_all(outgoing, AXES, split_axis=0, concat_axis=0, tiled=True)  4.18 us
    all_to_all x1, starting transfers between devices, step(): lax.all_to_all(reply, AXES, split_axis=0, concat_axis=0, tiled=True)  3.99 us
  transfers between devices with their start and end apart: 17, of which 10 were waited for; matrix products, arithmetic and copies ran while one was open for 3% of the time, Pallas kernels for 2%

profile of v6, /device:TPU:0, one launch (start us, length us, event | category | flops | bytes accessed | tf_op | source)
XLA Modules:
  0.0 115.0 jit_solution(17302770951495063711)
XLA Ops:
  1.5 0.9 maximum_bitcast_fusion
  2.5 3.0 %collective-permute-start = (f32[4,1,4,512]{3,2,1,0:T(4,128)S(1)}, f32[4,1,4,512]{3,2,1,0:T(4,128)S(1)}, u32[]{:S(2)}, u32[]{:S(2)}) collective-permute-start(f32[4,1,4,512]{3,2,1,0:T(4,128)S(1)} %get-tuple-element.51), channel_id=1, source_target_pairs={{0,16},{16,0},{1,17},{17,1},{2,18},{18,2},{3,19},{19,3},{4,20},{20... | collective-permute-start | bytes 98312 | tf_op jit(solution)/shard_map/ppermute | solution.py:448
  5.6 1.9 %collective-permute-done = f32[4,1,4,512]{3,2,1,0:T(4,128)S(1)} collective-permute-done((f32[4,1,4,512]{3,2,1,0:T(4,128)S(1)}, f32[4,1,4,512]{3,2,1,0:T(4,128)S(1)}, u32[]{:S(2)}, u32[]{:S(2)}) %collective-permute-start) | collective-permute-done | bytes 32800 | tf_op jit(solution)/shard_map/ppermute | solution.py:448
  7.9 1.8 %collective-permute-start.2 = (f32[4,2,1,512]{3,2,1,0:T(1,128)S(1)}, f32[4,2,1,512]{3,2,1,0:T(1,128)S(1)}, u32[]{:S(2)}, u32[]{:S(2)}) collective-permute-start(f32[4,2,1,512]{3,2,1,0:T(1,128)S(1)} %get-tuple-element.37), channel_id=1, source_target_pairs={{0,4},{4,0},{8,12},{12,8},{1,5},{5,1},{9,13},{13,9},{2,6},{6,2},{1... | collective-permute-start | bytes 49160 | tf_op jit(solution)/shard_map/ppermute | solution.py:448
  9.7 1.0 collective-permute-done.1
  10.9 4.3 %collective-permute-start.3 = (f32[4,2,6,32]{3,2,1,0:T(8,128)S(1)}, f32[4,2,6,32]{3,2,1,0:T(8,128)S(1)}, u32[]{:S(2)}, u32[]{:S(2)}) collective-permute-start(f32[4,2,6,32]{3,2,1,0:T(8,128)S(1)} %get-tuple-element.30), channel_id=1, source_target_pairs={{1,2},{2,1},{0,3},{3,0},{5,6},{6,5},{4,7},{7,4},{9,10},{10,9},{8,1... | collective-permute-start | bytes 18440 | tf_op jit(solution)/shard_map/ppermute | solution.py:448
  15.2 2.1 %route.1 = (f32[64,1,640]{2,1,0:T(1,128)}, s32[48]{0:T(128)}) custom-call(s32[48]{0:T(128)} %cell_ref.1, s32[48]{0:T(128)} %count_ref.1, f32[3,48,128]{2,1,0:T(8,128)} %bitcast.29, f32[48,128]{1,0:T(8,128)} %wt_ref.1), custom_call_target="tpu_custom_call" | custom-call | flops 3000000000 | bytes 262144 | tf_op jit(solution)/shard_map/route/pallas_call | solution.py:76
  17.3 4.2 %all-to-all-start = ((f32[64,1,640]{2,1,0:T(1,128)}), f32[64,1,640]{2,1,0:T(1,128)S(1)}, u32[]{:S(2)}, u32[]{:S(2)}) async-start(f32[64,1,640]{2,1,0:T(1,128)} %get-tuple-element.16), calls=%async_computation | async-start | bytes 327680 | tf_op jit(solution)/shard_map/all_to_all | solution.py:483
  22.4 7.9 %all-to-all-done.in_ref = f32[64,1,640]{2,1,0:T(1,128)S(1)} async-done(((f32[64,1,640]{2,1,0:T(1,128)}), f32[64,1,640]{2,1,0:T(1,128)S(1)}, u32[]{:S(2)}, u32[]{:S(2)}) %all-to-all-start) | async-done | bytes 163872 | tf_op jit(solution)/shard_map/all_to_all | solution.py:483
  31.0 13.6 %density.1 = (bf16[6912,128]{1,0:T(8,128)(2,1)}, f32[576,128]{1,0:T(8,128)}, f32[2,6,640]{2,1,0:T(8,128)}, f32[2,6,640]{2,1,0:T(8,128)}, s32[65]{0:T(128)}, /*index=5*/s32[69]{0:T(128)}, s32[1]{0:T(128)}) custom-call(f32[64,1,640]{2,1,0:T(1,128)} %copy-done, f32[4,2,6,640]{3,2,1,0:T(8,128)} %maximum_maximum_fusion.gauss_ref), custom_call_target="tpu_custom_call" | custom-call | flops 15000000512 | bytes 262144 | tf_op jit(solution)/shard_map/density/pallas_call | solution.py:506
  44.6 0.9 collective-permute-start.5
  45.5 3.4 %collective-permute-done.5 = f32[2,6,640]{2,1,0:T(8,128)S(1)} collective-permute-done((f32[2,6,640]{2,1,0:T(8,128)}, f32[2,6,640]{2,1,0:T(8,128)S(1)}, u32[]{:S(2)}, u32[]{:S(2)}) %collective-permute-start.5) | collective-permute-done | bytes 30752 | tf_op jit(solution)/shard_map/ppermute | solution.py:448
  50.6 2.2 %collective-permute-done.6 = f32[2,2,640]{2,1,0:T(2,128)S(1)} collective-permute-done((f32[2,2,640]{2,1,0:T(2,128)S(1)}, f32[2,2,640]{2,1,0:T(2,128)S(1)}, u32[]{:S(2)}, u32[]{:S(2)}) %collective-permute-start.6) | collective-permute-done | bytes 10272 | tf_op jit(solution)/shard_map/ppermute | solution.py:448
  52.9 2.1 %collective-permute-start.9 = (f32[2,6,64]{2,1,0:T(8,128)S(1)}, f32[2,6,64]{2,1,0:T(8,128)S(1)}, u32[]{:S(2)}, u32[]{:S(2)}) collective-permute-start(f32[2,6,64]{2,1,0:T(8,128)S(1)} %get-tuple-element.44), channel_id=1, source_target_pairs={{1,2},{2,1},{0,3},{3,0},{5,6},{6,5},{4,7},{7,4},{9,10},{10,9},{8,1... | collective-permute-start | bytes 9224 | tf_op jit(solution)/shard_map/ppermute | solution.py:448
  55.0 3.4 %collective-permute-done.9.second_ref = f32[2,6,64]{2,1,0:T(8,128)S(1)} collective-permute-done((f32[2,6,64]{2,1,0:T(8,128)S(1)}, f32[2,6,64]{2,1,0:T(8,128)S(1)}, u32[]{:S(2)}, u32[]{:S(2)}) %collective-permute-start.9) | collective-permute-done | bytes 3104 | tf_op jit(solution)/shard_map/ppermute | solution.py:448
  59.3 24.3 %gradient.1 = (f32[64,4,128]{2,1,0:T(4,128)}, f32[4,6,640]{2,1,0:T(8,128)}, f32[1,4,6,640]{3,2,1,0:T(8,128)}, f32[6,640]{1,0:T(8,128)}) custom-call(bf16[6912,128]{1,0:T(8,128)(2,1)} %get-tuple-element.17.feat_ref, f32[72,8,128]{2,1,0:T(8,128)} %bitcast.30, f32[2,6,640]{2,1,0:T(8,128)} %copy-done.2, f32[2,6,64]{2,1,0:T(8,128)} %copy-done.5, ...), custom_call_target="tpu_custom_call" | custom-call | flops 28000000000 | bytes 262144 | tf_op jit(solution)/shard_map/gradient/pallas_call | solution.py:544
  83.6 1.2 %collective-permute-start.10 = (f32[4,6,640]{2,1,0:T(8,128)}, f32[4,6,640]{2,1,0:T(8,128)S(1)}, u32[]{:S(2)}, u32[]{:S(2)}) collective-permute-start(f32[4,6,640]{2,1,0:T(8,128)} %bitcast.28), channel_id=1, source_target_pairs={{0,16},{16,0},{1,17},{17,1},{2,18},{18,2},{3,19},{19,3},{4,20},{20... | collective-permute-start | bytes 184328 | tf_op jit(solution)/shard_map/ppermute | solution.py:448
  84.8 3.5 %collective-permute-done.10 = f32[4,6,640]{2,1,0:T(8,128)S(1)} collective-permute-done((f32[4,6,640]{2,1,0:T(8,128)}, f32[4,6,640]{2,1,0:T(8,128)S(1)}, u32[]{:S(2)}, u32[]{:S(2)}) %collective-permute-start.10) | collective-permute-done | bytes 61472 | tf_op jit(solution)/shard_map/ppermute | solution.py:448
  88.3 0.9 add.45
  89.3 2.3 %collective-permute-start.12 = (f32[4,1,640]{2,1,0:T(1,128)S(1)}, f32[4,1,640]{2,1,0:T(1,128)S(1)}, u32[]{:S(2)}, u32[]{:S(2)}) collective-permute-start(f32[4,1,640]{2,1,0:T(1,128)S(1)} %get-tuple-element.33), channel_id=1, source_target_pairs={{0,4},{4,0},{8,12},{12,8},{1,5},{5,1},{9,13},{13,9},{2,6},{6,2},{1... | collective-permute-start | bytes 30728 | tf_op jit(solution)/shard_map/ppermute | solution.py:448
  92.5 7.0 %collective-permute-start.13 = (f32[4,4,32]{2,1,0:T(4,128)S(1)}, f32[4,4,32]{2,1,0:T(4,128)S(1)}, u32[]{:S(2)}, u32[]{:S(2)}) collective-permute-start(f32[4,4,32]{2,1,0:T(4,128)S(1)} %get-tuple-element.42), channel_id=1, source_target_pairs={{1,2},{2,1},{0,3},{3,0},{5,6},{6,5},{4,7},{7,4},{9,10},{10,9},{8,1... | collective-permute-start | bytes 6152 | tf_op jit(solution)/shard_map/ppermute | solution.py:448
  100.4 4.0 %all-to-all-start.1 = ((f32[64,4,128]{2,1,0:T(4,128)}), f32[64,4,128]{2,1,0:T(4,128)S(1)}, u32[]{:S(2)}, u32[]{:S(2)}) async-start(f32[64,4,128]{2,1,0:T(4,128)} %get-tuple-element.24), calls=%async_computation.1 | async-start | bytes 262144 | tf_op jit(solution)/shard_map/all_to_all | solution.py:560
  105.8 6.9 %all-to-all-done.1.reply_ref = f32[64,4,128]{2,1,0:T(4,128)S(1)} async-done(((f32[64,4,128]{2,1,0:T(4,128)}), f32[64,4,128]{2,1,0:T(4,128)S(1)}, u32[]{:S(2)}, u32[]{:S(2)}) %all-to-all-start.1) | async-done | bytes 131104 | tf_op jit(solution)/shard_map/all_to_all | solution.py:560
  113.4 1.6 %pick.1 = f32[48,4,128]{2,1,0:T(4,128)} custom-call(s32[48]{0:T(128)} %get-tuple-element.15.slot_ref, f32[64,4,128]{2,1,0:T(4,128)} %copy-done.1), custom_call_target="tpu_custom_call" | custom-call | flops 2000000000 | bytes 262144 | tf_op jit(solution)/shard_map/pick/pallas_call | solution.py:431
  (58 shorter events, 9.7 us)
Async XLA Ops:
  2.5 4.9 %collective-permute-start = (f32[4,1,4,512]{3,2,1,0:T(4,128)S(1)}, f32[4,1,4,512]{3,2,1,0:T(4,128)S(1)}, u32[]{:S(2)}, u32[]{:S(2)}) collective-permute-start(f32[4,1,4,512]{3,2,1,0:T(4,128)S(1)} %get-tuple-element.51), channel_id=1, source_target_pairs={{0,16},{16,0},{1,17},{17,1},{2,18},{18,2},{3,19},{19,3},{4,20},{20... | collective-permute-start | bytes 98312 | tf_op jit(solution)/shard_map/ppermute | solution.py:448
  7.5 3.2 %collective-permute-start.1 = (f32[4,2,1,512]{3,2,1,0:T(1,128)S(1)}, f32[4,2,1,512]{3,2,1,0:T(1,128)S(1)}, u32[]{:S(2)}, u32[]{:S(2)}) collective-permute-start(f32[4,2,1,512]{3,2,1,0:T(1,128)S(1)} %get-tuple-element.36), channel_id=1, source_target_pairs={{4,8},{8,4},{0,12},{12,0},{5,9},{9,5},{1,13},{13,1},{6,10},{10,6},... | collective-permute-start | bytes 49160 | tf_op jit(solution)/shard_map/ppermute | solution.py:448
  7.9 2.8 %collective-permute-start.2 = (f32[4,2,1,512]{3,2,1,0:T(1,128)S(1)}, f32[4,2,1,512]{3,2,1,0:T(1,128)S(1)}, u32[]{:S(2)}, u32[]{:S(2)}) collective-permute-start(f32[4,2,1,512]{3,2,1,0:T(1,128)S(1)} %get-tuple-element.37), channel_id=1, source_target_pairs={{0,4},{4,0},{8,12},{12,8},{1,5},{5,1},{9,13},{13,9},{2,6},{6,2},{1... | collective-permute-start | bytes 49160 | tf_op jit(solution)/shard_map/ppermute | solution.py:448
  10.9 10.7 %collective-permute-start.3 = (f32[4,2,6,32]{3,2,1,0:T(8,128)S(1)}, f32[4,2,6,32]{3,2,1,0:T(8,128)S(1)}, u32[]{:S(2)}, u32[]{:S(2)}) collective-permute-start(f32[4,2,6,32]{3,2,1,0:T(8,128)S(1)} %get-tuple-element.30), channel_id=1, source_target_pairs={{1,2},{2,1},{0,3},{3,0},{5,6},{6,5},{4,7},{7,4},{9,10},{10,9},{8,1... | collective-permute-start | bytes 18440 | tf_op jit(solution)/shard_map/ppermute | solution.py:448
  15.2 6.4 %collective-permute-start.4 = (f32[4,2,6,32]{3,2,1,0:T(8,128)S(1)}, f32[4,2,6,32]{3,2,1,0:T(8,128)S(1)}, u32[]{:S(2)}, u32[]{:S(2)}) collective-permute-start(f32[4,2,6,32]{3,2,1,0:T(8,128)S(1)} %get-tuple-element.31), channel_id=1, source_target_pairs={{0,1},{1,0},{2,3},{3,2},{4,5},{5,4},{6,7},{7,6},{8,9},{9,8},{10,11... | collective-permute-start | bytes 18440 | tf_op jit(solution)/shard_map/ppermute | solution.py:448
  17.3 13.0 %all-to-all-start = ((f32[64,1,640]{2,1,0:T(1,128)}), f32[64,1,640]{2,1,0:T(1,128)S(1)}, u32[]{:S(2)}, u32[]{:S(2)}) async-start(f32[64,1,640]{2,1,0:T(1,128)} %get-tuple-element.16), calls=%async_computation | async-start | bytes 327680 | tf_op jit(solution)/shard_map/all_to_all | solution.py:483
  30.3 0.7 copy-start
  44.6 4.3 %collective-permute-start.5 = (f32[2,6,640]{2,1,0:T(8,128)}, f32[2,6,640]{2,1,0:T(8,128)S(1)}, u32[]{:S(2)}, u32[]{:S(2)}) collective-permute-start(f32[2,6,640]{2,1,0:T(8,128)} %get-tuple-element.20), channel_id=1, source_target_pairs={{0,16},{16,0},{1,17},{17,1},{2,18},{18,2},{3,19},{19,3},{4,20},{20... | collective-permute-start | bytes 92168 | tf_op jit(solution)/shard_map/ppermute | solution.py:448
  49.7 3.2 %collective-permute-start.6 = (f32[2,2,640]{2,1,0:T(2,128)S(1)}, f32[2,2,640]{2,1,0:T(2,128)S(1)}, u32[]{:S(2)}, u32[]{:S(2)}) collective-permute-start(f32[2,2,640]{2,1,0:T(2,128)S(1)} %get-tuple-element.47), channel_id=1, source_target_pairs={{4,8},{8,4},{0,12},{12,0},{5,9},{9,5},{1,13},{13,1},{6,10},{10,6},... | collective-permute-start | bytes 30728 | tf_op jit(solution)/shard_map/ppermute | solution.py:448
  49.7 3.1 %collective-permute-start.7 = (f32[2,2,640]{2,1,0:T(2,128)S(1)}, f32[2,2,640]{2,1,0:T(2,128)S(1)}, u32[]{:S(2)}, u32[]{:S(2)}) collective-permute-start(f32[2,2,640]{2,1,0:T(2,128)S(1)} %get-tuple-element.48), channel_id=1, source_target_pairs={{0,4},{4,0},{8,12},{12,8},{1,5},{5,1},{9,13},{13,9},{2,6},{6,2},{1... | collective-permute-start | bytes 30728 | tf_op jit(solution)/shard_map/ppermute | solution.py:448
  52.9 5.8 %copy-start.2 = (f32[2,6,640]{2,1,0:T(8,128)}, f32[2,6,640]{2,1,0:T(8,128)S(1)}, u32[]{:S(2)}) copy-start(f32[2,6,640]{2,1,0:T(8,128)S(1)} %pad_maximum_fusion.1.zg_ref) | copy-start | bytes 92164
  52.9 5.5 %collective-permute-start.9 = (f32[2,6,64]{2,1,0:T(8,128)S(1)}, f32[2,6,64]{2,1,0:T(8,128)S(1)}, u32[]{:S(2)}, u32[]{:S(2)}) collective-permute-start(f32[2,6,64]{2,1,0:T(8,128)S(1)} %get-tuple-element.44), channel_id=1, source_target_pairs={{1,2},{2,1},{0,3},{3,0},{5,6},{6,5},{4,7},{7,4},{9,10},{10,9},{8,1... | collective-permute-start | bytes 9224 | tf_op jit(solution)/shard_map/ppermute | solution.py:448
  55.0 3.7 %collective-permute-start.8 = (f32[2,6,64]{2,1,0:T(8,128)S(1)}, f32[2,6,64]{2,1,0:T(8,128)S(1)}, u32[]{:S(2)}, u32[]{:S(2)}) collective-permute-start(f32[2,6,64]{2,1,0:T(8,128)S(1)} %get-tuple-element.45), channel_id=1, source_target_pairs={{0,1},{1,0},{2,3},{3,2},{4,5},{5,4},{6,7},{7,6},{8,9},{9,8},{10,11... | collective-permute-start | bytes 9224 | tf_op jit(solution)/shard_map/ppermute | solution.py:448
  58.4 0.6 copy-start.4
  58.7 0.6 copy-start.5
  59.3 45.6 %copy-start.3 = (s32[1,4,16]{2,1,0:T(4,128)S(1)}, s32[1,4,16]{2,1,0:T(4,128)}, u32[]{:S(2)}) copy-start(s32[1,4,16]{2,1,0:T(4,128)} %param.13) | copy-start | bytes 772
  83.6 4.7 %collective-permute-start.10 = (f32[4,6,640]{2,1,0:T(8,128)}, f32[4,6,640]{2,1,0:T(8,128)S(1)}, u32[]{:S(2)}, u32[]{:S(2)}) collective-permute-start(f32[4,6,640]{2,1,0:T(8,128)} %bitcast.28), channel_id=1, source_target_pairs={{0,16},{16,0},{1,17},{17,1},{2,18},{18,2},{3,19},{19,3},{4,20},{20... | collective-permute-start | bytes 184328 | tf_op jit(solution)/shard_map/ppermute | solution.py:448
  89.2 3.2 %collective-permute-start.11 = (f32[4,1,640]{2,1,0:T(1,128)S(1)}, f32[4,1,640]{2,1,0:T(1,128)S(1)}, u32[]{:S(2)}, u32[]{:S(2)}) collective-permute-start(f32[4,1,640]{2,1,0:T(1,128)S(1)} %get-tuple-element.32), channel_id=1, source_target_pairs={{4,8},{8,4},{0,12},{12,0},{5,9},{9,5},{1,13},{13,1},{6,10},{10,6},... | collective-permute-start | bytes 30728 | tf_op jit(solution)/shard_map/ppermute | solution.py:448
  89.3 3.1 %collective-permute-start.12 = (f32[4,1,640]{2,1,0:T(1,128)S(1)}, f32[4,1,640]{2,1,0:T(1,128)S(1)}, u32[]{:S(2)}, u32[]{:S(2)}) collective-permute-start(f32[4,1,640]{2,1,0:T(1,128)S(1)} %get-tuple-element.33), channel_id=1, source_target_pairs={{0,4},{4,0},{8,12},{12,8},{1,5},{5,1},{9,13},{13,9},{2,6},{6,2},{1... | collective-permute-start | bytes 30728 | tf_op jit(solution)/shard_map/ppermute | solution.py:448
  92.5 12.0 %collective-permute-start.13 = (f32[4,4,32]{2,1,0:T(4,128)S(1)}, f32[4,4,32]{2,1,0:T(4,128)S(1)}, u32[]{:S(2)}, u32[]{:S(2)}) collective-permute-start(f32[4,4,32]{2,1,0:T(4,128)S(1)} %get-tuple-element.42), channel_id=1, source_target_pairs={{1,2},{2,1},{0,3},{3,0},{5,6},{6,5},{4,7},{7,4},{9,10},{10,9},{8,1... | collective-permute-start | bytes 6152 | tf_op jit(solution)/shard_map/ppermute | solution.py:448
  99.5 5.0 %collective-permute-start.14 = (f32[4,4,32]{2,1,0:T(4,128)S(1)}, f32[4,4,32]{2,1,0:T(4,128)S(1)}, u32[]{:S(2)}, u32[]{:S(2)}) collective-permute-start(f32[4,4,32]{2,1,0:T(4,128)S(1)} %get-tuple-element.43), channel_id=1, source_target_pairs={{0,1},{1,0},{2,3},{3,2},{4,5},{5,4},{6,7},{7,6},{8,9},{9,8},{10,11... | collective-permute-start | bytes 6152 | tf_op jit(solution)/shard_map/ppermute | solution.py:448
  100.4 12.4 %all-to-all-start.1 = ((f32[64,4,128]{2,1,0:T(4,128)}), f32[64,4,128]{2,1,0:T(4,128)S(1)}, u32[]{:S(2)}, u32[]{:S(2)}) async-start(f32[64,4,128]{2,1,0:T(4,128)} %get-tuple-element.24), calls=%async_computation.1 | async-start | bytes 262144 | tf_op jit(solution)/shard_map/all_to_all | solution.py:560
  112.7 0.6 copy-start.1
